TPU v7x, 16 devices: a whole 2x2x2 slice. The times are simulated.
16 devices in a mesh: dp: 2 (over z), tp: 8 (over y, x, core).
Axes of the slice: x: 2, y: 2, z: 2, core: 2. Of those that a mesh axis runs over, the one named last changes fastest.
Arguments:
- hidden: bfloat16 [2, 4096, 2048], P('dp', 'tp'), parts along dimension 0
- norm_attn: float32 [2, 2048], replicated
- w_q: bfloat16 [2, 2048, 16, 128], P(None, None, 'tp')
- w_kv: bfloat16 [2, 2048, 2, 2, 128], replicated
- w_o: bfloat16 [2, 16, 128, 2048], P(None, 'tp')
- norm_mlp: float32 [2, 2048], replicated
- w_gate: bfloat16 [2, 2048, 11008], P(None, None, 'tp')
- w_up: bfloat16 [2, 2048, 11008], P(None, None, 'tp')
- w_down: bfloat16 [2, 11008, 2048], P(None, 'tp')
Outputs:
- output: bfloat16 [2, 4096, 2048], P('dp', 'tp'), parts along dimension 0
There are 2 independent parts. A program takes and returns all parts, laid end to end along the dimension named above; an argument that names none is the same for every part.
All inputs are finite; a program needn't handle non-finite values.
Results may differ from a plain program's by a relative error of at most 0.011265.
Values are sent between devices in bfloat16 or wider.
A program may use at most 1 GiB of HBM per device.

v0:
```python
import math
import jax
import jax.numpy as jnp
from jax import lax
from jax.sharding import PartitionSpec as P

EPS = 1e-5
ROPE_BASE = 10000.0


def rms_norm(resid, gain):
    mean_sq = jnp.mean(resid * resid, axis=-1, keepdims=True)
    return (resid * lax.rsqrt(mean_sq + EPS) * gain).astype(jnp.bfloat16)


def rope_tables(positions, head_dim):
    half_dim = head_dim // 2
    inv_freq = jnp.power(ROPE_BASE, -2.0 * jnp.arange(half_dim, dtype=jnp.float32) / head_dim)
    angles = positions.astype(jnp.float32)[:, None] * inv_freq[None, :]
    return jnp.cos(angles), jnp.sin(angles)


def apply_rope(proj, cos_t, sin_t):
    half_dim = proj.shape[-1] // 2
    first_half = proj[..., :half_dim]
    second_half = proj[..., half_dim:]
    cos_b = cos_t[None, :, None, :]
    sin_b = sin_t[None, :, None, :]
    return jnp.concatenate([first_half * cos_b - second_half * sin_b, second_half * cos_b + first_half * sin_b], axis=-1)


def solution(mesh):
    n_tp = mesh.shape['tp']
    tok_spec = P('dp', 'tp', None)
    in_specs = (tok_spec, P(), P(None, None, 'tp', None), P(), P(None, 'tp', None, None), P(), P(None, None, 'tp'), P(None, None, 'tp'), P(None, 'tp', None))

    def gather_rows(normed):
        return lax.all_gather(normed, 'tp', axis=1, tiled=True)

    def reduce_rows(partial):
        batch_loc, seq_len, width = partial.shape
        blocks = partial.astype(jnp.bfloat16).reshape(batch_loc, n_tp, seq_len // n_tp, width)
        received = lax.all_to_all(blocks, 'tp', 1, 1)
        return jnp.sum(received, axis=1, dtype=jnp.float32)

    def body(hidden, norm_attn, w_q, w_kv, w_o, norm_mlp, w_gate, w_up, w_down):
        n_layers = w_q.shape[0]
        heads_loc = w_q.shape[2]
        head_dim = w_q.shape[3]
        n_kv = w_kv.shape[3]
        kv_loc = max(1, n_kv // n_tp)
        group_loc = heads_loc // kv_loc
        batch_loc, rows_loc, _ = hidden.shape
        seq_len = rows_loc * n_tp
        kv_start = (lax.axis_index('tp') * n_kv) // n_tp
        positions = jnp.arange(seq_len)
        cos_t, sin_t = rope_tables(positions, head_dim)
        causal_mask = positions[:, None] >= positions[None, :]
        inv_sqrt = 1.0 / math.sqrt(head_dim)
        resid = hidden.astype(jnp.float32)
        for layer_idx in range(n_layers):
            gathered = gather_rows(rms_norm(resid, norm_attn[layer_idx]))
            kv_weight = lax.dynamic_slice_in_dim(w_kv[layer_idx], kv_start, kv_loc, axis=2)
            q_proj = jnp.einsum('bsd,dhe->bshe', gathered, w_q[layer_idx], preferred_element_type=jnp.float32)
            kv_proj = jnp.einsum('bsd,dcke->bscke', gathered, kv_weight, preferred_element_type=jnp.float32)
            queries = apply_rope(q_proj, cos_t, sin_t).astype(jnp.bfloat16).reshape(batch_loc, seq_len, kv_loc, group_loc, head_dim)
            keys = apply_rope(kv_proj[:, :, 0], cos_t, sin_t).astype(jnp.bfloat16)
            values = kv_proj[:, :, 1].astype(jnp.bfloat16)
            scores = jnp.einsum('bqkgd,bskd->bkgqs', queries, keys, preferred_element_type=jnp.float32) * inv_sqrt
            scores = jnp.where(causal_mask, scores, -jnp.inf)
            attn_probs = jax.nn.softmax(scores, axis=-1).astype(jnp.bfloat16)
            context = jnp.einsum('bkgqs,bskd->bqkgd', attn_probs, values, preferred_element_type=jnp.float32).astype(jnp.bfloat16)
            context = context.reshape(batch_loc, seq_len, heads_loc, head_dim)
            partial = jnp.einsum('bqhd,hdf->bqf', context, w_o[layer_idx], preferred_element_type=jnp.float32)
            resid = resid + reduce_rows(partial)
            gathered = gather_rows(rms_norm(resid, norm_mlp[layer_idx]))
            gate_proj = jnp.einsum('bsd,df->bsf', gathered, w_gate[layer_idx], preferred_element_type=jnp.float32)
            up_proj = jnp.einsum('bsd,df->bsf', gathered, w_up[layer_idx], preferred_element_type=jnp.float32)
            activated = (jax.nn.silu(gate_proj) * up_proj).astype(jnp.bfloat16)
            partial = jnp.einsum('bsf,fd->bsd', activated, w_down[layer_idx], preferred_element_type=jnp.float32)
            resid = resid + reduce_rows(partial)
        return resid.astype(jnp.bfloat16)

    return jax.shard_map(body, mesh=mesh, in_specs=in_specs, out_specs=tok_spec, check_vma=False)
```

profile of v0, /device:TPU:0, one launch (start us, length us, event | category | flops | bytes accessed | tf_op | source)
XLA Modules:
  0.0 1706.3 jit_solution(3356374877015991525)
XLA Ops:
  34.3 11.0 iota_compare_fusion
  45.3 57.2 %all-gather.5.cloned.1.call-done = bf16[1,4096,2048]{2,1,0:T(8,128)(2,1)} async-done(((bf16[1,512,2048]{2,1,0:T(8,128)(2,1)}), bf16[1,4096,2048]{2,1,0:T(8,128)(2,1)}) %all-gather.5.cloned.1.call-update) | async-done | bytes 16777232 | tf_op jit(solution)/shard_map/all_gather | solution.py:38
  102.5 10.0 fusion.20
  122.5 52.6 %fusion.2 = (f32[2,4096]{1,0:T(2,128)S(1)}, f32[4096,4096,2]{1,0,2:T(8,128)}) fusion(pred[4096,4096]{0,1:T(8,128)(4,1)} %iota_compare_fusion, bf16[4096,2,64]{0,2,1:T(8,128)(2,1)S(1)} %get-tuple-element.10, bf16[4096,2,64]{0,2,1:T(8,128)(2,1)S(1)} %get-tuple-element.9, bf16[4096,64]{0,1:T(8,128)(2,1)S(1)} %get-tuple-element.16, ...), kind=kOutput, calls=%fused_computation.8 | convolution fusion | flops 8696881152 | bytes 154173440 | tf_op jit(solution)/shard_map/bqkgd,bskd->bkgqs/dot_general | solution.py:69
  175.2 46.2 %fusion = f32[2,4096]{1,0:T(2,128)S(1)} fusion(f32[4096,4096,2]{1,0,2:T(8,128)} %get-tuple-element.26, f32[2,4096]{1,0:T(2,128)S(1)} %get-tuple-element.25, pred[4096,4096]{0,1:T(8,128)(4,1)} %iota_compare_fusion), kind=kLoop, calls=%fused_computation.6 | loop fusion | flops 134209536 | bytes 151060480 | tf_op jit(solution)/shard_map/reduce_sum | solution.py:71
  221.4 54.3 %fusion.51.clone.5 = bf16[4096,2,128]{0,2,1:T(8,128)(2,1)S(1)} fusion(f32[2,4096]{1,0:T(2,128)S(1)} %fusion, f32[2,4096]{1,0:T(2,128)S(1)} %get-tuple-element.25, f32[4096,4096,2]{1,0,2:T(8,128)} %get-tuple-element.26, pred[4096,4096]{0,1:T(8,128)(4,1)} %iota_compare_fusion, f32[1,4096,2,1,128]{1,4,2,3,0:T(8,128)} %bitcast.320), kind=kOutput, calls=%fused_computation.57.clone.clone.clone.2 | convolution fusion | flops 8758755328 | bytes 154206208 | tf_op jit(solution)/shard_map/bkgqs,bskd->bqkgd/dot_general | solution.py:72
  275.7 9.4 bitcast_convert_fusion.1
  291.7 183.3 %all-to-all-done = bf16[1,8,512,2048]{3,2,0,1:T(8,128)(2,1)} async-done(((bf16[1,8,512,2048]{3,2,0,1:T(8,128)(2,1)}), bf16[1,8,512,2048]{3,2,0,1:T(8,128)(2,1)}, u32[]{:S(2)}, u32[]{:S(2)}) %all-to-all-start) | async-done | bytes 16777248 | tf_op jit(solution)/shard_map/all_to_all | solution.py:43
  486.4 85.1 %all-gather.7.cloned.1.call-done = bf16[1,4096,2048]{2,1,0:T(8,128)(2,1)} async-done(((bf16[1,512,2048]{2,1,0:T(8,128)(2,1)}), bf16[1,4096,2048]{2,1,0:T(8,128)(2,1)}) %all-gather.7.cloned.1.call-update) | async-done | bytes 16777232 | tf_op jit(solution)/shard_map/all_gather | solution.py:38
  571.4 30.6 %fusion.16 = f32[4096,1376]{0,1:T(8,128)} fusion(bf16[1,4096,2048]{2,1,0:T(8,128)(2,1)} %all-gather.7.cloned.1.call-done, bf16[2,2048,1376]{1,2,0:T(8,128)(2,1)} %param.15), kind=kOutput, calls=%fused_computation.31 | convolution fusion | flops 23085449216 | bytes 44957696 | tf_op jit(solution)/shard_map/bsd,df->bsf/dot_general | solution.py:77
  602.1 34.7 %multiply_convert_fusion.1.clone.5 = bf16[4096,1376]{0,1:T(8,128)(2,1)} fusion(f32[4096,1376]{0,1:T(8,128)} %fusion.16, bf16[1,4096,2048]{2,1,0:T(8,128)(2,1)} %all-gather.7.cloned.1.call-done, bf16[2,2048,1376]{1,2,0:T(8,128)(2,1)} %param.16), kind=kOutput, calls=%fused_computation.22.clone.clone.clone.2 | convolution fusion | flops 23119265792 | bytes 56229888 | tf_op jit(solution)/shard_map/bsd,df->bsf/dot_general | solution.py:78
  636.7 30.8 %convolution_convert_fusion.1 = bf16[4096,2048]{1,0:T(8,128)(2,1)S(1)} fusion(bf16[2,1376,2048]{2,1,0:T(8,128)(2,1)} %param.17, bf16[4096,1376]{0,1:T(8,128)(2,1)} %multiply_convert_fusion.1.clone.5), kind=kOutput, calls=%fused_computation.38 | convolution fusion | flops 23093837824 | bytes 33685504 | tf_op jit(solution)/shard_map/bsf,fd->bsd/dot_general | solution.py:80
  667.6 186.6 %all_to_all.20 = bf16[1,8,512,2048]{3,2,0,1:T(8,128)(2,1)S(1)} all-to-all(bf16[1,8,512,2048]{3,2,0,1:T(8,128)(2,1)S(1)} %bitcast.313), channel_id=1, replica_groups=mesh['dp'=2,'tp'=8] {'tp'}, dimensions={1} | all-to-all | bytes 33554432 | tf_op jit(solution)/shard_map/all_to_all | solution.py:43
  867.8 80.0 %all-gather.9.cloned.1.call-done = bf16[1,4096,2048]{2,1,0:T(8,128)(2,1)} async-done(((bf16[1,512,2048]{2,1,0:T(8,128)(2,1)}), bf16[1,4096,2048]{2,1,0:T(8,128)(2,1)}) %all-gather.9.cloned.1.call-update) | async-done | bytes 16777232 | tf_op jit(solution)/shard_map/all_gather | solution.py:38
  968.2 52.8 %fusion.3 = (f32[2,4096]{1,0:T(2,128)S(1)}, f32[4096,4096,2]{1,0,2:T(8,128)}) fusion(pred[4096,4096]{0,1:T(8,128)(4,1)} %iota_compare_fusion, bf16[4096,2,64]{0,2,1:T(8,128)(2,1)S(1)} %get-tuple-element.8, bf16[4096,2,64]{0,2,1:T(8,128)(2,1)S(1)} %get-tuple-element.7, bf16[4096,64]{0,1:T(8,128)(2,1)S(1)} %get-tuple-element.14, ...), kind=kOutput, calls=%fused_computation.9 | convolution fusion | flops 8696881152 | bytes 154173440 | tf_op jit(solution)/shard_map/bqkgd,bskd->bkgqs/dot_general | solution.py:69
  1021.0 46.2 %fusion.1 = f32[2,4096]{1,0:T(2,128)S(1)} fusion(f32[4096,4096,2]{1,0,2:T(8,128)} %get-tuple-element.28, f32[2,4096]{1,0:T(2,128)S(1)} %get-tuple-element.27, pred[4096,4096]{0,1:T(8,128)(4,1)} %iota_compare_fusion), kind=kLoop, calls=%fused_computation.7 | loop fusion | flops 134209536 | bytes 151060480 | tf_op jit(solution)/shard_map/reduce_sum | solution.py:71
  1067.2 53.9 %fusion.48.clone.5 = bf16[4096,2,128]{0,2,1:T(8,128)(2,1)S(1)} fusion(f32[2,4096]{1,0:T(2,128)S(1)} %fusion.1, f32[2,4096]{1,0:T(2,128)S(1)} %get-tuple-element.27, f32[4096,4096,2]{1,0,2:T(8,128)} %get-tuple-element.28, pred[4096,4096]{0,1:T(8,128)(4,1)} %iota_compare_fusion, f32[1,4096,2,1,128]{1,4,3,2,0:T(8,128)} %bitcast.322), kind=kOutput, calls=%fused_computation.56.clone.clone.clone.2 | convolution fusion | flops 8758755328 | bytes 154206208 | tf_op jit(solution)/shard_map/bkgqs,bskd->bqkgd/dot_general | solution.py:72
  1121.1 9.4 bitcast_convert_fusion
  1130.5 187.8 %all_to_all.21 = bf16[1,8,512,2048]{3,2,0,1:T(8,128)(2,1)S(1)} all-to-all(bf16[1,8,512,2048]{3,2,0,1:T(8,128)(2,1)} %bitcast.312), channel_id=1, replica_groups=mesh['dp'=2,'tp'=8] {'tp'}, dimensions={1} | all-to-all | bytes 33554432 | tf_op jit(solution)/shard_map/all_to_all | solution.py:43
  1325.8 85.1 %all-gather.11.cloned.1.call-done = bf16[1,4096,2048]{2,1,0:T(8,128)(2,1)} async-done(((bf16[1,512,2048]{2,1,0:T(8,128)(2,1)}), bf16[1,4096,2048]{2,1,0:T(8,128)(2,1)}) %all-gather.11.cloned.1.call-update) | async-done | bytes 16777232 | tf_op jit(solution)/shard_map/all_gather | solution.py:38
  1410.9 30.5 %fusion.9 = f32[4096,1376]{0,1:T(8,128)} fusion(bf16[1,4096,2048]{2,1,0:T(8,128)(2,1)} %all-gather.11.cloned.1.call-done, bf16[2,2048,1376]{1,2,0:T(8,128)(2,1)} %param.15), kind=kOutput, calls=%fused_computation.24 | convolution fusion | flops 23085449216 | bytes 44957696 | tf_op jit(solution)/shard_map/bsd,df->bsf/dot_general | solution.py:77
  1441.4 34.9 %multiply_convert_fusion.clone.5 = bf16[4096,1376]{0,1:T(8,128)(2,1)} fusion(f32[4096,1376]{0,1:T(8,128)} %fusion.9, bf16[1,4096,2048]{2,1,0:T(8,128)(2,1)} %all-gather.11.cloned.1.call-done, bf16[2,2048,1376]{1,2,0:T(8,128)(2,1)} %param.16), kind=kOutput, calls=%fused_computation.21.clone.clone.clone.2 | convolution fusion | flops 23119265792 | bytes 56229888 | tf_op jit(solution)/shard_map/bsd,df->bsf/dot_general | solution.py:78
  1476.3 30.6 %convolution_convert_fusion = bf16[4096,2048]{1,0:T(8,128)(2,1)S(1)} fusion(bf16[2,1376,2048]{2,1,0:T(8,128)(2,1)} %param.17, bf16[4096,1376]{0,1:T(8,128)(2,1)} %multiply_convert_fusion.clone.5), kind=kOutput, calls=%fused_computation.37 | convolution fusion | flops 23093837824 | bytes 33685504 | tf_op jit(solution)/shard_map/bsf,fd->bsd/dot_general | solution.py:80
  1506.9 186.6 %all_to_all.22 = bf16[1,8,512,2048]{3,2,0,1:T(8,128)(2,1)S(1)} all-to-all(bf16[1,8,512,2048]{3,2,0,1:T(8,128)(2,1)S(1)} %bitcast.314), channel_id=1, replica_groups=mesh['dp'=2,'tp'=8] {'tp'}, dimensions={1} | all-to-all | bytes 33554432 | tf_op jit(solution)/shard_map/all_to_all | solution.py:43
  (103 shorter events, 102.7 us)
Async XLA Ops:
  6.5 7.1 copy-start.15
  6.5 96.0 %all-gather.5.cloned.1.call-start = ((), (), s32[]{:S(2)}) async-start(), calls=%async_computation.4 | async-start | bytes 18874368 | tf_op jit(solution)/shard_map/all_gather | solution.py:38
  30.6 82.2 %copy-start.24 = (f32[64]{0:T(128)}, f32[64]{0:T(128)S(1)}, u32[]{:S(2)}) copy-start(f32[64]{0:T(128)S(1)} %multiply_power_fusion) | copy-start | bytes 772
  30.6 82.2 %copy-start.19 = (f32[4096]{0:T(1024)}, f32[4096]{0:T(1024)S(1)}, u32[]{:S(2)}) copy-start(f32[4096]{0:T(1024)S(1)} %iota_convert_fusion) | copy-start | bytes 49156
  34.3 87.5 %copy-start.9 = (f32[4096,64]{0,1:T(8,128)}, f32[4096,64]{0,1:T(8,128)S(1)}, u32[]{:S(2)}) copy-start(f32[4096,64]{0,1:T(8,128)S(1)} %get-tuple-element.19) | copy-start | bytes 3145732
  34.3 87.5 %copy-start.11 = (f32[4096,64]{0,1:T(8,128)}, f32[4096,64]{0,1:T(8,128)S(1)}, u32[]{:S(2)}) copy-start(f32[4096,64]{0,1:T(8,128)S(1)} %get-tuple-element.20) | copy-start | bytes 3145732
  102.5 14.7 copy-start.26
  112.6 4.6 copy-start.16
  112.6 4.7 copy-start.18
  285.1 5.9 copy-start.23
  285.1 189.8 %all-to-all-start = ((bf16[1,8,512,2048]{3,2,0,1:T(8,128)(2,1)}), bf16[1,8,512,2048]{3,2,0,1:T(8,128)(2,1)}, u32[]{:S(2)}, u32[]{:S(2)}) async-start(bf16[1,8,512,2048]{3,2,0,1:T(8,128)(2,1)} %bitcast.311), calls=%async_computation | async-start | bytes 33554432 | tf_op jit(solution)/shard_map/all_to_all | solution.py:43
  291.0 280.4 %all-gather.7.cloned.1.call-start = ((), (), s32[]{:S(2)}) async-start(), calls=%async_computation.5 | async-start | bytes 18874368 | tf_op jit(solution)/shard_map/all_gather | solution.py:38
  291.7 190.5 %copy-start.7 = (bf16[1,512,2048]{2,1,0:T(8,128)(2,1)S(1)}, bf16[1,512,2048]{2,1,0:T(8,128)(2,1)}, u32[]{:S(2)}) copy-start(bf16[1,512,2048]{2,1,0:T(8,128)(2,1)} %param.9) | copy-start | bytes 6291460
  486.3 461.4 %all-gather.9.cloned.1.call-start = ((), (), s32[]{:S(2)}) async-start(), calls=%async_computation.6 | async-start | bytes 18874368 | tf_op jit(solution)/shard_map/all_gather | solution.py:38
  858.7 3.9 copy-start.14
  858.7 6.4 copy-start.13
  862.6 548.3 %all-gather.11.cloned.1.call-start = ((), (), s32[]{:S(2)}) async-start(), calls=%async_computation.7 | async-start | bytes 18874368 | tf_op jit(solution)/shard_map/all_gather | solution.py:38
  947.8 8.6 copy-start.10
  947.8 8.6 copy-start.12
  947.8 11.5 copy-start.27
  959.2 4.7 copy-start.20
  959.2 4.7 copy-start.25
  963.8 4.4 copy-start.17
  1318.3 3.5 copy-start.1
  (9 other events, 25.3 us)
Sparse Core Ops, SparseCore 0:
  13.8 88.6 all-gather.4
  486.4 84.9 all-gather.6
  862.7 84.9 all-gather.8
  1325.9 84.9 all-gather.10
where the time goes:
time: 1720 us; the launch traced here: 1710 us
  blocking collectives  561 us (33%)
  waiting for transfers between devices  491 us (29%)
  matrix products  452 us (26%)
  other arithmetic  151 us (9%)
  local copies, waits for them, and re-layouts  31.5 us (2%)
    all_to_all x3, blocking collectives, reduce_rows(): received = lax.all_to_all(blocks, 'tp', 1, 1)  561 us
    all_gather x4, waiting for transfers between devices, gather_rows(): return lax.all_gather(normed, 'tp', axis=1, tiled=True)  307 us
    all_to_all x1, waiting for transfers between devices, reduce_rows(): received = lax.all_to_all(blocks, 'tp', 1, 1)  183 us
    dot_general x2, matrix products, body(): jnp.einsum('bkgqs,bskd->bqkgd', attn_probs, values, preferred_element_typ...  108 us
    dot_general x2, matrix products, body(): jnp.einsum('bqkgd,bskd->bkgqs', queries, keys, preferred_element_type=jnp...  105 us
    reduce_sum x2, other arithmetic, body(): attn_probs = jax.nn.softmax(scores, axis=-1).astype(jnp.bfloat16)  92.4 us
    dot_general x2, matrix products, body(): jnp.einsum('bsd,df->bsf', gathered, w_up[layer_idx], preferred_element_ty...  69.6 us
    dot_general x2, matrix products, body(): jnp.einsum('bsf,fd->bsd', activated, w_down[layer_idx], preferred_element...  61.4 us
  transfers between devices with their start and end apart: 5, of which 5 were waited for; matrix products, arithmetic and copies ran while one was open for 2% of the time, Pallas kernels for 0%

commit v1 on v0

v1 whole, which is shorter than its diff:
```python
import functools
import math
import jax
import jax.numpy as jnp
from jax import lax
from jax.experimental import pallas as pl
from jax.experimental.pallas import tpu as pltpu
from jax.sharding import PartitionSpec as P

EPS = 1e-5
ROPE_BASE = 10000.0
MESH = pl.DeviceIdType.MESH
VMEM_MAX = 67043328
F32 = jnp.float32
BF16 = jnp.bfloat16


def rms_norm(resid, gain):
    mean_sq = jnp.mean(resid * resid, axis=-1, keepdims=True)
    return (resid * lax.rsqrt(mean_sq + EPS) * gain).astype(BF16)


def rope_tables(positions, head_dim):
    half_dim = head_dim // 2
    inv_freq = jnp.power(ROPE_BASE, -2.0 * jnp.arange(half_dim, dtype=F32) / head_dim)
    angles = positions.astype(F32)[:, None] * inv_freq[None, :]
    return jnp.cos(angles), jnp.sin(angles)


def apply_rope(proj, cos_t, sin_t):
    half_dim = proj.shape[-1] // 2
    first_half = proj[..., :half_dim]
    second_half = proj[..., half_dim:]
    cos_b = cos_t[:, None, :]
    sin_b = sin_t[:, None, :]
    return jnp.concatenate([first_half * cos_b - second_half * sin_b, second_half * cos_b + first_half * sin_b], axis=-1)


def flash_kernel(bq, bk, head_dim, heads, q_ref, k_ref, v_ref, o_ref):
    i = pl.program_id(0)
    scale = math.log2(math.e) / math.sqrt(head_dim)
    rows = lax.broadcasted_iota(jnp.int32, (bq, bk), 0)
    cols = lax.broadcasted_iota(jnp.int32, (bq, bk), 1)
    qs = [q_ref[:, h * head_dim:(h + 1) * head_dim] for h in range(heads)]

    def step(j, carry, masked):
        at = pl.ds(pl.multiple_of(j * bk, bk), bk)
        k_blk = k_ref[at, :]
        v_blk = v_ref[at, :]
        out = []
        for h in range(heads):
            m, l, acc = carry[h]
            s = lax.dot_general(qs[h], k_blk, (((1,), (1,)), ((), ())), preferred_element_type=F32)
            if masked:
                s = jnp.where(i * bq + rows >= j * bk + cols, s, -jnp.inf)
            m_new = jnp.maximum(m, jnp.max(s, axis=-1, keepdims=True))
            p = jnp.exp2((s - m_new) * scale)
            alpha = jnp.exp2((m - m_new) * scale)
            l = l * alpha + jnp.sum(p, axis=-1, keepdims=True)
            acc = acc * alpha + jnp.dot(p.astype(BF16), v_blk, preferred_element_type=F32)
            out.append((m_new, l, acc))
        return tuple(out)

    init = tuple((jnp.full((bq, 1), -jnp.inf, F32), jnp.zeros((bq, 1), F32), jnp.zeros((bq, head_dim), F32)) for _ in range(heads))
    per = bq // bk
    carry = lax.fori_loop(0, i * per, functools.partial(step, masked=False), init)
    for d in range(per):
        carry = step(i * per + d, carry, True)
    for h in range(heads):
        m, l, acc = carry[h]
        o_ref[:, h * head_dim:(h + 1) * head_dim] = (acc / l).astype(BF16)


def flash(q, k, v, heads, head_dim, bq=512, bk=512):
    seq = q.shape[0]
    width = heads * head_dim
    return pl.pallas_call(
        functools.partial(flash_kernel, bq, bk, head_dim, heads),
        grid=(seq // bq,),
        in_specs=[
            pl.BlockSpec((bq, width), lambda i: (i, 0)),
            pl.BlockSpec((seq, head_dim), lambda i: (0, 0)),
            pl.BlockSpec((seq, head_dim), lambda i: (0, 0)),
        ],
        out_specs=pl.BlockSpec((bq, width), lambda i: (i, 0)),
        out_shape=jax.ShapeDtypeStruct((seq, width), BF16),
        compiler_params=pltpu.CompilerParams(dimension_semantics=("arbitrary",)),
        cost_estimate=pl.CostEstimate(flops=2 * seq * seq * width, bytes_accessed=8 * seq * width, transcendentals=seq * seq * heads // 2),
        name="flash",
    )(q, k, v)


def mlp_kernel(layer, r_hbm, gain_ref, wg_hbm, wu_hbm, wd_hbm, out_hbm,
               wg, wu, wd, xbuf, prec, recv, acc, stash, act,
               lsem, sx, sy, ag, fs, fr, ps, pr, rr, ss):
    t = lax.axis_index('tp')
    c = lax.rem(t, 2)
    xx = lax.rem(lax.div(t, 2), 2)
    yy = lax.div(t, 4)
    mate = t + 1 - 2 * c
    dev_x = t + 2 - 4 * xx
    dev_y = t + 4 - 8 * yy
    rows, width = acc.shape
    half = rows // 2
    hid = act.shape[1]
    h0 = pl.ds(0, half)
    h1 = pl.ds(half, half)
    hs = (h0, h1)

    def rcopy(src, dst, ssem, rsem, dev):
        return pltpu.make_async_remote_copy(src_ref=src, dst_ref=dst, send_sem=ssem, recv_sem=rsem,
                                            device_id={'tp': dev}, device_id_type=MESH)

    load_r = pltpu.make_async_copy(r_hbm, acc, lsem.at[0])
    load_g = pltpu.make_async_copy(wg_hbm.at[layer], wg, lsem.at[1])
    load_u = pltpu.make_async_copy(wu_hbm.at[layer], wu, lsem.at[2])
    load_d = pltpu.make_async_copy(wd_hbm.at[layer], wd, lsem.at[3])
    load_r.start()
    load_g.start()
    load_u.start()
    load_d.start()

    barrier = pltpu.get_barrier_semaphore()
    for dev in (mate, dev_x, dev_y):
        pl.semaphore_signal(barrier, inc=1, device_id={'tp': dev}, device_id_type=MESH)

    load_r.wait()
    nb = 64

    @pl.loop(0, rows // nb)
    def _(b):
        at = pl.ds(pl.multiple_of(b * nb, nb), nb)
        r = acc[at, :]
        mean_sq = jnp.mean(r * r, axis=-1, keepdims=True)
        xbuf[0, 0, at, :] = (r * lax.rsqrt(mean_sq + EPS) * gain_ref[...]).astype(BF16)

    pl.semaphore_wait(barrier, 3)

    own = xbuf.at[0, 0]
    send_x = (rcopy(own.at[h0], xbuf.at[1, 0, h0], sx.at[0], ag.at[1, 0], dev_x),
              rcopy(own.at[h1], xbuf.at[2, 0, h1], sx.at[1], ag.at[2, 1], dev_x),
              rcopy(xbuf.at[1, 0, h1], xbuf.at[3, 0, h1], sx.at[2], ag.at[3, 1], dev_x))
    send_y = (rcopy(own.at[h1], xbuf.at[1, 0, h1], sy.at[0], ag.at[1, 1], dev_y),
              rcopy(own.at[h0], xbuf.at[2, 0, h0], sy.at[1], ag.at[2, 0], dev_y),
              rcopy(xbuf.at[1, 0, h0], xbuf.at[3, 0, h0], sy.at[2], ag.at[3, 0], dev_y))
    for k in range(2):
        send_x[k].start()
        send_y[k].start()

    def forward(w):
        return rcopy(xbuf.at[w, 0], xbuf.at[w, 1], fs.at[w], fr.at[w], mate)

    def partial_send(w):
        return rcopy(xbuf.at[w, 1], prec.at[w], ps.at[w], pr.at[w], mate)

    stage = (rcopy(xbuf.at[1, 1, h0], recv.at[0], ss.at[0], rr.at[0], dev_x),
             rcopy(xbuf.at[1, 1, h1], recv.at[1], ss.at[1], rr.at[1], dev_y),
             rcopy(xbuf.at[3, 1, h0], recv.at[2], ss.at[2], rr.at[2], dev_x),
             rcopy(xbuf.at[3, 1, h1], recv.at[3], ss.at[3], rr.at[3], dev_y),
             rcopy(xbuf.at[2, 1, h0], recv.at[4], ss.at[4], rr.at[4], dev_y),
             rcopy(xbuf.at[2, 1, h1], recv.at[5], ss.at[5], rr.at[5], dev_x))

    forward(0).start()
    load_g.wait()
    load_u.wait()
    load_d.wait()

    nc = 256
    n_full = hid // nc
    tail = hid - n_full * nc

    def gate_up(x_at, at):
        g = jnp.dot(x_at[...], wg[:, at], preferred_element_type=F32)
        u = jnp.dot(x_at[...], wu[:, at], preferred_element_type=F32)
        act[:, at] = (g * jax.nn.sigmoid(g) * u).astype(BF16)

    @pl.loop(0, 8)
    def _(s):
        w = lax.div(s, 2)
        rc = 1 - lax.rem(s, 2)

        @pl.when(rc == 1)
        def _():
            @pl.when(w >= 1)
            def _():
                pltpu.make_async_copy(xbuf.at[0, 0, h0], xbuf.at[w, 0, h0], ag.at[w, 0]).wait()
                pltpu.make_async_copy(xbuf.at[0, 0, h1], xbuf.at[w, 0, h1], ag.at[w, 1]).wait()
                forward(w).start()

                @pl.when(w == 1)
                def _():
                    send_x[2].start()
                    send_y[2].start()
            forward(w).wait_recv()

        x_at = xbuf.at[w, rc]

        @pl.loop(0, n_full)
        def _(n):
            gate_up(x_at, pl.ds(pl.multiple_of(n * nc, nc), nc))
        if tail:
            gate_up(x_at, pl.ds(n_full * nc, tail))

        @pl.when(rc == 0)
        def _():
            partial_send(w).wait()

        @pl.loop(0, width // nc)
        def _(n):
            at = pl.ds(pl.multiple_of(n * nc, nc), nc)
            val = jnp.dot(act[...], wd[:, at], preferred_element_type=F32)

            @pl.when(rc == 1)
            def _():
                xbuf[w, 1, :, at] = val.astype(BF16)

            @pl.when(rc == 0)
            def _():
                total = val + prec[w, :, at].astype(F32)

                @pl.when(w == 0)
                def _():
                    acc[:, at] = acc[:, at] + total

                @pl.when(w == 2)
                def _():
                    stash[:, at] = total

                @pl.when(lax.rem(w, 2) == 1)
                def _():
                    xbuf[w, 1, :, at] = total.astype(BF16)

        @pl.when(rc == 1)
        def _():
            partial_send(w).start()

        @pl.when(s == 3)
        def _():
            stage[0].start()
            stage[1].start()

        @pl.when(s == 7)
        def _():
            stage[2].start()
            stage[3].start()

    def add_rows(dst, first, slot):
        @pl.loop(0, half // nb)
        def _(b):
            at = pl.ds(pl.multiple_of(b * nb, nb), nb)
            to = pl.ds(pl.multiple_of(first + b * nb, nb), nb)
            dst[to, :] = dst[to, :] + recv[slot, at, :].astype(F32)

    for k in range(2):
        stage[k].wait_recv()
        add_rows(acc, k * half, k)
    for k in range(2):
        stage[2 + k].wait_recv()

        @pl.loop(0, half // nb)
        def _(b):
            at = pl.ds(pl.multiple_of(b * nb, nb), nb)
            to = pl.ds(pl.multiple_of(k * half + b * nb, nb), nb)
            xbuf[2, 1, to, :] = (stash[to, :] + recv[2 + k, at, :].astype(F32)).astype(BF16)
        stage[4 + k].start()
    outs = []
    for k in range(2):
        stage[4 + k].wait_recv()
        add_rows(acc, k * half, 4 + k)
        outs.append(pltpu.make_async_copy(acc.at[hs[k]], out_hbm.at[hs[k]], lsem.at[k]))
        outs[k].start()
    for copy in send_x + send_y:
        copy.wait_send()
    for w in range(4):
        forward(w).wait_send()
    for copy in stage:
        copy.wait_send()
    for copy in outs:
        copy.wait()


def mlp(layer, resid, gain, w_gate, w_up, w_down):
    rows, width = resid.shape
    hid = w_gate.shape[2]
    half = rows // 2
    any_spec = pl.BlockSpec(memory_space=pl.ANY)
    dma = pltpu.SemaphoreType.DMA
    return pl.pallas_call(
        functools.partial(mlp_kernel, layer),
        out_shape=jax.ShapeDtypeStruct((rows, width), F32),
        in_specs=[any_spec, pl.BlockSpec(memory_space=pltpu.VMEM), any_spec, any_spec, any_spec],
        out_specs=any_spec,
        scratch_shapes=[
            pltpu.VMEM((width, hid), BF16),
            pltpu.VMEM((width, hid), BF16),
            pltpu.VMEM((hid, width), BF16),
            pltpu.VMEM((4, 2, rows, width), BF16),
            pltpu.VMEM((4, rows, width), BF16),
            pltpu.VMEM((6, half, width), BF16),
            pltpu.VMEM((rows, width), F32),
            pltpu.VMEM((rows, width), F32),
            pltpu.VMEM((rows, hid), BF16),
            dma((4,)), dma((3,)), dma((3,)), dma((4, 2)), dma((4,)), dma((4,)), dma((4,)), dma((4,)), dma((6,)), dma((6,)),
        ],
        compiler_params=pltpu.CompilerParams(collective_id=1 + layer, has_side_effects=True, vmem_limit_bytes=VMEM_MAX),
        cost_estimate=pl.CostEstimate(flops=6 * 8 * rows * width * hid, bytes_accessed=6 * width * hid, transcendentals=8 * rows * hid),
        name="mlp" + str(layer),
    )(resid, gain, w_gate, w_up, w_down)


def solution(mesh):
    n_tp = mesh.shape['tp']
    tok_spec = P('dp', 'tp', None)
    in_specs = (tok_spec, P(), P(None, None, 'tp', None), P(), P(None, 'tp', None, None), P(), P(None, None, 'tp'), P(None, None, 'tp'), P(None, 'tp', None))

    def body(hidden, norm_attn, w_q, w_kv, w_o, norm_mlp, w_gate, w_up, w_down):
        n_layers, width, heads, head_dim = w_q.shape
        n_kv = w_kv.shape[3]
        rows = hidden.shape[1]
        seq = rows * n_tp
        kv_head = (lax.axis_index('tp') * n_kv) // n_tp
        cos_t, sin_t = rope_tables(jnp.arange(seq), head_dim)
        resid = hidden[0].astype(F32)
        for layer in range(n_layers):
            o_full = lax.all_gather(w_o[layer], 'tp', axis=0, tiled=True)
            gathered = lax.all_gather(rms_norm(resid, norm_attn[layer]), 'tp', axis=0, tiled=True)
            kv_weight = lax.dynamic_index_in_dim(w_kv[layer], kv_head, axis=2, keepdims=False)
            q_proj = jnp.einsum('sd,dhe->she', gathered, w_q[layer], preferred_element_type=F32)
            kv_proj = jnp.einsum('sd,dce->sce', gathered, kv_weight, preferred_element_type=F32)
            queries = apply_rope(q_proj, cos_t, sin_t).astype(BF16).reshape(seq, heads * head_dim)
            keys = apply_rope(kv_proj[:, :1], cos_t, sin_t).astype(BF16)[:, 0]
            values = kv_proj[:, 1].astype(BF16)
            context = flash(queries, keys, values, heads, head_dim)
            blocks = lax.all_to_all(context.reshape(n_tp, rows, heads * head_dim), 'tp', 0, 0)
            blocks = jnp.transpose(blocks, (1, 0, 2)).reshape(rows, n_tp * heads * head_dim)
            resid = resid + jnp.dot(blocks, o_full.reshape(-1, width), preferred_element_type=F32)
            resid = mlp(layer, resid, norm_mlp[layer][None], w_gate, w_up, w_down)
        return resid.astype(BF16)[None]

    return jax.shard_map(body, mesh=mesh, in_specs=in_specs, out_specs=tok_spec, check_vma=False)
```

time: 1720 us -> 837 us (0.49)
  blocking collectives: 561 us -> 0 us
  Pallas kernels: 0 us -> 445 us
  matrix products: 452 us -> 54.1 us
  waiting for transfers between devices: 491 us -> 166 us
  other arithmetic: 151 us -> 43.9 us
  local copies, waits for them, and re-layouts: 31.5 us -> 95.2 us
    all_to_all x3 -> x0, blocking collectives: 561 us -> none  [reduce_rows(): received = lax.all_to_all(blocks, 'tp', 1, 1)]
    pallas_call x0 -> x4, Pallas kernels: none -> 445 us  [the longest x2 350 us: mlp(): pl.pallas_call(functools.partial(mlp_kernel, layer), out_shape=jax.ShapeD...]
    dot_general x12 -> x2, matrix products: 425 us -> 20.6 us  [body(): jnp.dot(blocks, o_full.reshape(-1, width), preferred_element_type=F32)]
    all_gather x4, waiting for transfers between devices: 307 us -> 139 us  [the longest x2 139 us: body(): lax.all_gather(rms_norm(resid, norm_attn[layer]), 'tp', axis=0, tiled=True)]
    all_to_all x1 -> x2, waiting for transfers between devices: 183 us -> 26.5 us  [body(): lax.all_to_all(context.reshape(n_tp, rows, heads * head_dim), 'tp', 0, 0)]
    reduce_sum x6 -> x0, other arithmetic: 110 us -> none  [the longest x2 92.4 us: body(): attn_probs = jax.nn.softmax(scores, axis=-1).astype(jnp.bfloat16)]
    unnamed x58 -> x41, local copies, waits for them, and re-layouts: 11.8 us -> 53.3 us
  transfers between devices with their start and end apart: 5 -> 6, of which waited for: 5 -> 3; matrix products, arithmetic and copies ran while one was open for 2% -> 19% of each run, Pallas kernels for 0% -> 11%
where the time goes in v1:
time: 837 us; the launch traced here: 826 us
  Pallas kernels  445 us (53%)
  waiting for transfers between devices  166 us (20%)
  local copies, waits for them, and re-layouts  95.2 us (11%)
  matrix products  54.1 us (6%)
  other arithmetic  43.9 us (5%)
  between operations  13.9 us (2%)
    pallas_call x2, Pallas kernels, mlp(): pl.pallas_call(functools.partial(mlp_kernel, layer), out_shape=jax.ShapeD...  350 us
    all_gather x2, waiting for transfers between devices, body(): lax.all_gather(rms_norm(resid, norm_attn[layer]), 'tp', axis=0, tiled=True)  139 us
    pallas_call x2, Pallas kernels, flash(): pl.pallas_call(functools.partial(flash_kernel, bq, bk, head_dim, heads),...  94.4 us
    unnamed x41, local copies, waits for them, and re-layouts  53.3 us
    unnamed x4, matrix products  33.5 us
    all_to_all x2, waiting for transfers between devices, body(): lax.all_to_all(context.reshape(n_tp, rows, heads * head_dim), 'tp', 0, 0)  26.5 us
    concatenate x6, other arithmetic, apply_rope(): jnp.concatenate([first_half * cos_b - second_half * sin_b, second_half *...  25.7 us
    dot_general x2, matrix products, body(): jnp.dot(blocks, o_full.reshape(-1, width), preferred_element_type=F32)  20.6 us
  transfers between devices with their start and end apart: 6, of which 3 were waited for; matrix products, arithmetic and copies ran while one was open for 19% of the time, Pallas kernels for 11%

profile of v1, /device:TPU:0, one launch (start us, length us, event | category | flops | bytes accessed | tf_op | source)
XLA Modules:
  0.0 826.1 jit_solution(5788693485410240092)
XLA Ops:
  20.8 4.7 fusion.24
  25.5 5.4 constant_dynamic-slice_fusion
  30.9 5.8 copy.46
  36.7 4.7 multiply_cosine_fusion.1
  41.5 59.4 %all-gather.7.cloned.1.call-done = bf16[4096,2048]{1,0:T(8,128)(2,1)} async-done(((bf16[512,2048]{1,0:T(8,128)(2,1)}), bf16[4096,2048]{1,0:T(8,128)(2,1)}) %all-gather.7.cloned.1.call-update) | async-done | bytes 16777232 | tf_op jit(solution)/shard_map/all_gather | solution.py:326
  100.9 8.5 %fusion.29 = f32[4096,256]{0,1:S(1)} fusion(bf16[4096,2048]{1,0:T(8,128)(2,1)} %all-gather.7.cloned.1.call-done, bf16[2048,256]{0,1:T(8,128)(2,1)} %bitcast.82), kind=kOutput, calls=%fused_computation.58 | convolution fusion | flops 4294967296 | bytes 22020096
  111.7 4.2 copy.64.q_ref
  115.9 8.2 fusion.30
  133.3 10.5 %fusion.22 = (bf16[4096,64]{1,0:T(8,128)(2,1)S(1)}, bf16[4096,64]{1,0:T(8,128)(2,1)S(1)}) fusion(f32[4096,1,64]{2,0,1:T(8,128)} %copy.71, f32[4096,1,64]{2,0,1:T(8,128)} %copy.70, f32[64]{0:T(128)S(1)} %multiply_power_fusion, f32[4096]{0:T(1024)S(1)} %iota_convert_fusion), kind=kLoop, calls=%fused_computation.39 | loop fusion | flops 2359296 | bytes 3162368 | tf_op jit(solution)/shard_map/concatenate | solution.py:36
  145.4 47.3 %flash.2 = bf16[4096,256]{1,0:T(8,128)(2,1)} custom-call(bf16[4096,256]{1,0:T(8,128)(2,1)} %copy.64.q_ref, bf16[4096,128]{1,0:T(8,128)(2,1)} %pad_maximum_fusion.2.k_ref, bf16[4096,128]{1,0:T(8,128)(2,1)} %bitcast.84), custom_call_target="tpu_custom_call" | custom-call | flops 8589934592 | bytes 8388608 | tf_op jit(solution)/shard_map/flash/pallas_call | solution.py:77
  192.7 3.9 copy.50
  196.6 4.3 all-to-all-start
  201.0 15.4 %copy.52.wg_hbm = bf16[2,2048,1376]{2,1,0:T(8,128)(2,1)} copy(bf16[2,2048,1376]{1,2,0:T(8,128)(2,1)} %param.15) | data formatting | bytes 22544384 | tf_op args[6]
  216.4 15.1 %copy.53.wu_hbm = bf16[2,2048,1376]{2,1,0:T(8,128)(2,1)} copy(bf16[2,2048,1376]{1,2,0:T(8,128)(2,1)} %param.16) | data formatting | bytes 22544384 | tf_op args[7]
  232.2 10.5 %convert_add_fusion.r_hbm = f32[512,2048]{1,0:T(8,128)} fusion(bf16[512,2048]{0,1:T(8,128)(2,1)} %bitcast.15, bf16[2048,2048]{1,0:T(8,128)(2,1)} %bitcast.69, bf16[1,512,2048]{2,1,0:T(8,128)(2,1)S(1)} %copy-done.1), kind=kOutput, calls=%fused_computation | convolution fusion | flops 4297064448 | bytes 16777216 | tf_op jit(solution)/shard_map/dot_general | solution.py:336
  242.7 176.1 %mlp0.1 = f32[512,2048]{1,0:T(8,128)} custom-call(f32[512,2048]{1,0:T(8,128)} %convert_add_fusion.r_hbm, f32[1,2048]{1,0:T(1,128)} %get-tuple-element.26.gain_ref, bf16[2,2048,1376]{2,1,0:T(8,128)(2,1)} %copy.52.wg_hbm, bf16[2,2048,1376]{2,1,0:T(8,128)(2,1)} %copy.53.wu_hbm, bf16[2,1376,2048]{2,1,0:T(8,128)(2,1)} %wd_hbm.3), custom_call_target="tpu_custom_call" | custom-call | flops 69256347648 | bytes 16908288 | tf_op jit(solution)/shard_map/mlp0/pallas_call | solution.py:288
  430.0 79.5 %all-gather.9.cloned.1.call-done = bf16[4096,2048]{1,0:T(8,128)(2,1)} async-done(((bf16[512,2048]{1,0:T(8,128)(2,1)}), bf16[4096,2048]{1,0:T(8,128)(2,1)}) %all-gather.9.cloned.1.call-update) | async-done | bytes 16777232 | tf_op jit(solution)/shard_map/all_gather | solution.py:326
  509.6 8.6 %fusion.31 = f32[4096,256]{0,1:S(1)} fusion(bf16[4096,2048]{1,0:T(8,128)(2,1)} %all-gather.9.cloned.1.call-done, bf16[2048,256]{0,1:T(8,128)(2,1)} %bitcast.85), kind=kOutput, calls=%fused_computation.60 | convolution fusion | flops 4294967296 | bytes 22020096
  521.5 8.1 fusion.32
  537.6 10.4 %fusion.20 = (bf16[4096,64]{1,0:T(8,128)(2,1)S(1)}, bf16[4096,64]{1,0:T(8,128)(2,1)S(1)}) fusion(f32[4096,1,64]{2,0,1:T(8,128)S(1)} %copy.74, f32[4096,1,64]{2,0,1:T(8,128)} %copy.73, f32[64]{0:T(128)S(1)} %copy-done.14, f32[4096]{0:T(1024)S(1)} %copy-done.10), kind=kLoop, calls=%fused_computation.37 | loop fusion | flops 2359296 | bytes 3162368 | tf_op jit(solution)/shard_map/concatenate | solution.py:36
  549.6 47.1 %flash.3 = bf16[4096,256]{1,0:T(8,128)(2,1)} custom-call(bf16[4096,256]{1,0:T(8,128)(2,1)} %copy.65.q_ref, bf16[4096,128]{1,0:T(8,128)(2,1)} %pad_maximum_fusion.3.k_ref, bf16[4096,128]{1,0:T(8,128)(2,1)} %bitcast.83), custom_call_target="tpu_custom_call" | custom-call | flops 8589934592 | bytes 8388608 | tf_op jit(solution)/shard_map/flash/pallas_call | solution.py:77
  604.5 26.5 %all-to-all-done.1 = bf16[8,512,256]{1,2,0:T(8,128)(2,1)S(1)} async-done(((bf16[8,512,256]{1,2,0:T(8,128)(2,1)}), bf16[8,512,256]{1,2,0:T(8,128)(2,1)S(1)}, u32[]{:S(2)}, u32[]{:S(2)}) %all-to-all-start.1) | async-done | bytes 2097184 | tf_op jit(solution)/shard_map/all_to_all | solution.py:334
  631.0 10.1 %convolution_add_fusion.r_hbm = f32[512,2048]{1,0:T(8,128)} fusion(f32[512,2048]{1,0:T(8,128)} %mlp0.1, bf16[512,2048]{0,1:T(8,128)(2,1)S(1)} %bitcast.68, bf16[2048,2048]{1,0:T(8,128)(2,1)} %bitcast.67), kind=kOutput, calls=%fused_computation.18 | convolution fusion | flops 4296015872 | bytes 18874368 | tf_op jit(solution)/shard_map/dot_general | solution.py:336
  641.1 174.2 %mlp1.1 = f32[512,2048]{1,0:T(8,128)} custom-call(f32[512,2048]{1,0:T(8,128)} %convolution_add_fusion.r_hbm, f32[1,2048]{1,0:T(1,128)} %get-tuple-element.25.gain_ref, bf16[2,2048,1376]{2,1,0:T(8,128)(2,1)} %copy.52.wg_hbm, bf16[2,2048,1376]{2,1,0:T(8,128)(2,1)} %copy.53.wu_hbm, bf16[2,1376,2048]{2,1,0:T(8,128)(2,1)} %wd_hbm.3), custom_call_target="tpu_custom_call" | custom-call | flops 69256347648 | bytes 16908288 | tf_op jit(solution)/shard_map/mlp1/pallas_call | solution.py:288
  (76 shorter events, 63.5 us)
Async XLA Ops:
  6.5 3.6 copy-start.1
  6.5 94.3 %all-gather.7.cloned.1.call-start = ((), (), s32[]{:S(2)}) async-start(), calls=%async_computation.2 | async-start | bytes 18874368 | tf_op jit(solution)/shard_map/all_gather | solution.py:326
  12.0 220.1 %all-gather.11.cloned.1.call-start = ((), (), s32[]{:S(2)}) async-start(), calls=%async_computation.4 | async-start | bytes 9437184 | tf_op jit(solution)/shard_map/all_gather | solution.py:325
  36.7 96.6 %copy-start.13 = (f32[64]{0:T(128)}, f32[64]{0:T(128)S(1)}, u32[]{:S(2)}) copy-start(f32[64]{0:T(128)S(1)} %multiply_power_fusion) | copy-start | bytes 772
  36.7 96.6 %copy-start.9 = (f32[4096]{0:T(1024)}, f32[4096]{0:T(1024)S(1)}, u32[]{:S(2)}) copy-start(f32[4096]{0:T(1024)S(1)} %iota_convert_fusion) | copy-start | bytes 49156
  41.5 68.0 %copy-start.2 = (f32[4096,64]{0,1:T(8,128)}, f32[4096,64]{0,1:T(8,128)S(1)}, u32[]{:S(2)}) copy-start(f32[4096,64]{0,1:T(8,128)S(1)} %get-tuple-element.23) | copy-start | bytes 3145732
  100.9 8.6 %copy-start.4 = (f32[4096,64]{0,1:T(8,128)S(1)}, f32[4096,64]{0,1:T(8,128)}, u32[]{:S(2)}) copy-start(f32[4096,64]{0,1:T(8,128)} %get-tuple-element.24) | copy-start | bytes 3145732
  111.7 4.2 copy-start.8
  196.6 35.6 %all-to-all-start = ((bf16[8,512,256]{1,2,0:T(8,128)(2,1)}), bf16[8,512,256]{1,2,0:T(8,128)(2,1)}, u32[]{:S(2)}, u32[]{:S(2)}) async-start(bf16[8,512,256]{1,2,0:T(8,128)(2,1)} %copy.50), calls=%async_computation | async-start | bytes 4194304 | tf_op jit(solution)/shard_map/all_to_all | solution.py:334
  201.0 308.6 %all-gather.9.cloned.1.call-start = ((), (), s32[]{:S(2)}) async-start(), calls=%async_computation.3 | async-start | bytes 18874368 | tf_op jit(solution)/shard_map/all_gather | solution.py:326
  216.4 15.1 %copy-start.12 = (f32[2,2048]{1,0:T(2,128)S(1)}, f32[2,2048]{1,0:T(2,128)}, u32[]{:S(2)}) copy-start(f32[2,2048]{1,0:T(2,128)} %param.14) | copy-start | bytes 49156
  418.8 3.5 copy-start
  418.8 3.4 copy-start.11
  424.0 1.2 copy-start.7
  424.0 3.4 copy-start.6
  424.0 180.5 %all-gather.13.cloned.1.call-start = ((), (), s32[]{:S(2)}) async-start(), calls=%async_computation.5 | async-start | bytes 9437184 | tf_op jit(solution)/shard_map/all_gather | solution.py:325
  509.6 8.6 %copy-start.3 = (f32[4096,64]{0,1:T(8,128)S(1)}, f32[4096,64]{0,1:T(8,128)}, u32[]{:S(2)}) copy-start(f32[4096,64]{0,1:T(8,128)} %copy-done.2) | copy-start | bytes 3145732
  509.6 8.6 %copy-start.5 = (f32[4096,64]{0,1:T(8,128)S(1)}, f32[4096,64]{0,1:T(8,128)}, u32[]{:S(2)}) copy-start(f32[4096,64]{0,1:T(8,128)} %get-tuple-element.24) | copy-start | bytes 3145732
  533.1 4.5 copy-start.10
  533.1 4.5 copy-start.14
  600.6 30.4 %all-to-all-start.1 = ((bf16[8,512,256]{1,2,0:T(8,128)(2,1)}), bf16[8,512,256]{1,2,0:T(8,128)(2,1)S(1)}, u32[]{:S(2)}, u32[]{:S(2)}) async-start(bf16[8,512,256]{1,2,0:T(8,128)(2,1)} %copy.60), calls=%async_computation.1 | async-start | bytes 4194304 | tf_op jit(solution)/shard_map/all_to_all | solution.py:334
Sparse Core Ops, SparseCore 0:
  12.1 88.6 all-gather.6
  102.7 50.1 all-gather.10
  424.1 85.4 all-gather.8
  511.3 50.1 all-gather.12

commit v2 on v1

v2 whole, which is shorter than its diff:
```python
import functools
import math
import jax
import jax.numpy as jnp
from jax import lax
from jax.experimental import pallas as pl
from jax.experimental.pallas import tpu as pltpu
from jax.sharding import PartitionSpec as P

EPS = 1e-5
ROPE_BASE = 10000.0
MESH = pl.DeviceIdType.MESH
VMEM_MAX = 67043328
F32 = jnp.float32
BF16 = jnp.bfloat16


def rope_tables(seq, head_dim):
    half_dim = head_dim // 2
    inv_freq = jnp.power(ROPE_BASE, -2.0 * jnp.arange(half_dim, dtype=F32) / head_dim)
    angles = jnp.arange(seq).astype(F32)[:, None] * inv_freq[None, :]
    cos_t, sin_t = jnp.cos(angles), jnp.sin(angles)
    return jnp.concatenate([cos_t, cos_t], axis=1), jnp.concatenate([-sin_t, sin_t], axis=1)


def coords():
    t = lax.axis_index('tp')
    c = lax.rem(t, 2)
    xx = lax.rem(lax.div(t, 2), 2)
    yy = lax.div(t, 4)
    return t, (yy, xx, c), (t + 1 - 2 * c, t + 2 - 4 * xx, t + 4 - 8 * yy)


def rcopy(src, dst, ssem, rsem, dev):
    return pltpu.make_async_remote_copy(src_ref=src, dst_ref=dst, send_sem=ssem, recv_sem=rsem,
                                        device_id={'tp': dev}, device_id_type=MESH)


def greet(devices):
    for dev in devices:
        pl.semaphore_signal(pltpu.get_barrier_semaphore(), inc=1, device_id={'tp': dev}, device_id_type=MESH)


class RowGather:
    def __init__(self, xbuf, sx, sy, ag, fs, fr, partners):
        mate, dev_x, dev_y = partners
        rows = xbuf.shape[2]
        half = rows // 2
        lead = half // 4
        h0, h1 = pl.ds(0, half), pl.ds(half, half)
        own = xbuf.at[0, 0]
        self.xbuf, self.ag, self.fs, self.fr, self.mate = xbuf, ag, fs, fr, mate
        self.halves = (h0, h1)

        def piece(k, sem, dev, first, size, window, slot):
            at = pl.ds(first, size)
            return rcopy(own.at[at], xbuf.at[window, 0, at], sem.at[k], ag.at[window, slot], dev)

        self.first = (piece(0, sx, dev_x, 0, half, 1, 0), piece(0, sy, dev_y, half, half, 1, 1))
        self.lead = (piece(1, sx, dev_x, half, lead, 3, 1), piece(1, sy, dev_y, 0, lead, 3, 0))
        self.rest = (piece(2, sx, dev_x, half + lead, half - lead, 3, 1), piece(2, sy, dev_y, lead, half - lead, 3, 0))
        self.relay = (rcopy(xbuf.at[1, 0, h1], xbuf.at[2, 0, h1], sx.at[3], ag.at[2, 1], dev_x),
                      rcopy(xbuf.at[1, 0, h0], xbuf.at[2, 0, h0], sy.at[3], ag.at[2, 0], dev_y))

    def forward(self, w):
        return rcopy(self.xbuf.at[w, 0], self.xbuf.at[w, 1], self.fs.at[w], self.fr.at[w], self.mate)

    def start(self, norm_half):
        norm_half(0)
        pl.semaphore_wait(pltpu.get_barrier_semaphore(), 3)
        self.first[0].start()
        norm_half(1)
        self.first[1].start()
        self.lead[0].start()
        self.lead[1].start()
        self.forward(0).start()

    def arrive(self, w):
        for k in range(2):
            at = self.halves[k]
            pltpu.make_async_copy(self.xbuf.at[0, 0, at], self.xbuf.at[w, 0, at], self.ag.at[w, k]).wait()

        @pl.when(w == 1)
        def _():
            for copy in self.relay + self.rest:
                copy.start()
        self.forward(w).start()

    def finish(self):
        for copy in self.first + self.lead + self.relay + self.rest:
            copy.wait_send()
        for w in range(4):
            self.forward(w).wait_send()


def gather_sems():
    dma = pltpu.SemaphoreType.DMA
    return [dma((4,)), dma((4,)), dma((4, 2)), dma((4,)), dma((4,))]


def norm_rows(src, gain_ref, dst, first, count):
    nb = 64

    @pl.loop(0, count // nb)
    def _(b):
        at = pl.ds(pl.multiple_of(first + b * nb, nb), nb)
        r = src[at, :].astype(F32)
        mean_sq = jnp.mean(r * r, axis=-1, keepdims=True)
        dst[at, :] = (r * lax.rsqrt(mean_sq + EPS) * gain_ref[...]).astype(BF16)


def qkv_kernel(heads, head_dim, r_ref, gain_ref, w_ref, cos_ref, sin_ref, out_ref, xbuf, sx, sy, ag, fs, fr):
    _, (yy, xx, c), partners = coords()
    rows = xbuf.shape[2]
    half = rows // 2
    greet(partners)
    gather = RowGather(xbuf, sx, sy, ag, fs, fr, partners)
    gather.start(lambda k: norm_rows(r_ref, gain_ref, xbuf.at[0, 0], k * half, half))

    @pl.loop(0, 8)
    def _(s):
        w = lax.div(s, 2)
        rc = lax.rem(s, 2)

        @pl.when((rc == 0) & (w >= 1))
        def _():
            gather.arrive(w)

        @pl.when(rc == 1)
        def _():
            gather.forward(w).wait_recv()
        proj = jnp.dot(xbuf[w, rc], w_ref[...], preferred_element_type=F32)
        core = c + rc - 2 * c * rc
        one = lax.rem(lax.div(w + 1, 2), 2)
        two = lax.div(w, 2)
        for k in range(2):
            flip_x, flip_y = (one, two) if k == 0 else (two, one)
            chip = 2 * (yy + flip_y - 2 * yy * flip_y) + xx + flip_x - 2 * xx * flip_x
            at = pl.ds(pl.multiple_of((chip * 2 + core) * rows + k * half, half), half)
            part = proj[k * half:(k + 1) * half]
            cos_b = cos_ref[at, :]
            sin_b = sin_ref[at, :]
            for h in range(heads + 1):
                cols = slice(h * head_dim, (h + 1) * head_dim)
                z = part[:, cols]
                out_ref[at, cols] = (z * cos_b + pltpu.roll(z, head_dim // 2, 1) * sin_b).astype(BF16)
            cols = slice((heads + 1) * head_dim, (heads + 2) * head_dim)
            out_ref[at, cols] = part[:, cols].astype(BF16)
    gather.finish()


def qkv(layer, resid, gain, w_qkv, cos_t, sin_t, heads, head_dim, n_tp):
    rows, width = resid.shape
    cols = w_qkv.shape[1]
    seq = rows * n_tp
    vmem = pl.BlockSpec(memory_space=pltpu.VMEM)
    return pl.pallas_call(
        functools.partial(qkv_kernel, heads, head_dim),
        out_shape=jax.ShapeDtypeStruct((seq, cols), BF16),
        in_specs=[vmem] * 5,
        out_specs=vmem,
        scratch_shapes=[pltpu.VMEM((4, 2, rows, width), BF16)] + gather_sems(),
        compiler_params=pltpu.CompilerParams(collective_id=1 + layer, has_side_effects=True, vmem_limit_bytes=VMEM_MAX),
        cost_estimate=pl.CostEstimate(flops=2 * seq * width * cols, bytes_accessed=4 * seq * cols, transcendentals=0),
        name="qkv" + str(layer),
    )(resid, gain, w_qkv, cos_t, sin_t)


def attend(qkv_ref, block, bq, bk, heads, head_dim):
    scale = math.log2(math.e) / math.sqrt(head_dim)
    rows = lax.broadcasted_iota(jnp.int32, (bq, bk), 0)
    cols = lax.broadcasted_iota(jnp.int32, (bq, bk), 1)
    q_at = pl.ds(pl.multiple_of(block * bq, bq), bq)
    qs = [qkv_ref[q_at, h * head_dim:(h + 1) * head_dim] for h in range(heads)]

    def step(j, carry, masked):
        at = pl.ds(pl.multiple_of(j * bk, bk), bk)
        k_blk = qkv_ref[at, heads * head_dim:(heads + 1) * head_dim]
        v_blk = qkv_ref[at, (heads + 1) * head_dim:(heads + 2) * head_dim]
        out = []
        for h in range(heads):
            m, l, acc = carry[h]
            s = lax.dot_general(qs[h], k_blk, (((1,), (1,)), ((), ())), preferred_element_type=F32)
            if masked:
                s = jnp.where(block * bq + rows >= j * bk + cols, s, -jnp.inf)
            m_new = jnp.maximum(m, jnp.max(s, axis=-1, keepdims=True))
            p = jnp.exp2((s - m_new) * scale)
            alpha = jnp.exp2((m - m_new) * scale)
            l = l * alpha + jnp.sum(p, axis=-1, keepdims=True)
            acc = acc * alpha + jnp.dot(p.astype(BF16), v_blk, preferred_element_type=F32)
            out.append((m_new, l, acc))
        return tuple(out)

    init = tuple((jnp.full((bq, 1), -jnp.inf, F32), jnp.zeros((bq, 1), F32), jnp.zeros((bq, head_dim), F32)) for _ in range(heads))
    last = lax.div(block * bq, bk)
    carry = lax.fori_loop(0, last, functools.partial(step, masked=False), init)
    carry = step(last, carry, True)
    return [(acc / l).astype(BF16) for _, l, acc in carry]


def attn_kernel(layer, n_tp, heads, head_dim, bk, qkv_ref, r_ref, wo_hbm, out_ref,
                wo, ctx, ctx_out, lsem, sx, sy, ag, fs, fr, cs, cr):
    t, (yy, xx, c), partners = coords()
    mate, dev_x, dev_y = partners
    rows = out_ref.shape[0]
    width = out_ref.shape[1]
    cols = heads * head_dim
    load_o = pltpu.make_async_copy(wo_hbm.at[layer], wo.at[pl.ds(pl.multiple_of(t * cols, cols), cols)], lsem.at[0])
    load_o.start()
    others = [lax.rem(t + k, n_tp) for k in range(1, n_tp)]
    greet(others)
    load_o.wait()
    pl.semaphore_wait(pltpu.get_barrier_semaphore(), n_tp - 1)

    def span(dev, k):
        return pl.ds(pl.multiple_of(dev * cols + k * head_dim, head_dim), head_dim)

    def same(at, ssem, rsem, dev):
        return rcopy(wo.at[at], wo.at[at], ssem, rsem, dev)

    send = (same(span(t, 0), sx.at[0], ag.at[0], dev_x), same(span(t, 1), sy.at[0], ag.at[1], dev_y),
            same(span(t, 1), sx.at[1], ag.at[2], dev_x), same(span(t, 0), sy.at[1], ag.at[3], dev_y))
    relay = (same(span(dev_y, 1), sx.at[2], ag.at[4], dev_x), same(span(dev_x, 0), sy.at[2], ag.at[5], dev_y))
    dev_d = dev_x + dev_y - t
    landed = (span(dev_x, 0), span(dev_y, 1), span(dev_x, 1), span(dev_y, 0), span(dev_d, 1), span(dev_d, 0))
    own = pl.ds(pl.multiple_of(t * cols, cols), cols)
    to_mate = tuple(same(landed[k], fs.at[k], fr.at[k], mate) for k in range(6)) + (same(own, fs.at[6], fr.at[6], mate),)

    def take(k):
        pltpu.make_async_copy(wo.at[landed[k]], wo.at[landed[k]], ag.at[k]).wait()

    for copy in send:
        copy.start()
    to_mate[6].start()

    mine = pl.ds(pl.multiple_of(t * cols, cols), cols)

    def ctx_send(i, dev):
        return rcopy(ctx_out.at[i], ctx.at[:, mine], cs.at[i], cr.at[t], dev)

    @pl.loop(0, n_tp)
    def _(i):
        block = lax.rem(t + 1 + i, n_tp)

        @pl.when(i == 3)
        def _():
            take(0)
            take(1)
            for copy in relay:
                copy.start()

        @pl.when(i == 6)
        def _():
            for k in range(2, 6):
                take(k)
            for k in range(6):
                to_mate[k].start()
        for h, val in enumerate(attend(qkv_ref, block, rows, bk, heads, head_dim)):
            ctx_out[i, :, h * head_dim:(h + 1) * head_dim] = val

        @pl.when(i < n_tp - 1)
        def _():
            ctx_send(i, block).start()

    ctx[:, mine] = ctx_out[n_tp - 1]
    for copy in to_mate:
        copy.wait_recv()
    for dev in others:
        at = pl.ds(pl.multiple_of(dev * cols, cols), cols)
        pltpu.make_async_copy(ctx_out.at[0], ctx.at[:, at], cr.at[dev]).wait()
    nc = 512

    @pl.loop(0, width // nc)
    def _(n):
        at = pl.ds(pl.multiple_of(n * nc, nc), nc)
        out_ref[:, at] = r_ref[:, at].astype(F32) + jnp.dot(ctx[...], wo[:, at], preferred_element_type=F32)
    for copy in send + relay + to_mate:
        copy.wait_send()
    for i in range(n_tp - 1):
        ctx_send(i, mate).wait_send()


def attention(layer, qkv_all, resid, w_o, heads, head_dim, n_tp, bk=1024):
    rows, width = resid.shape
    cols = heads * head_dim
    seq = rows * n_tp
    vmem = pl.BlockSpec(memory_space=pltpu.VMEM)
    dma = pltpu.SemaphoreType.DMA
    return pl.pallas_call(
        functools.partial(attn_kernel, layer, n_tp, heads, head_dim, bk),
        out_shape=jax.ShapeDtypeStruct((rows, width), F32),
        in_specs=[vmem, vmem, pl.BlockSpec(memory_space=pl.ANY)],
        out_specs=vmem,
        scratch_shapes=[
            pltpu.VMEM((n_tp * cols, width), BF16),
            pltpu.VMEM((rows, n_tp * cols), BF16),
            pltpu.VMEM((n_tp, rows, cols), BF16),
            dma((1,)), dma((3,)), dma((3,)), dma((6,)), dma((7,)), dma((7,)), dma((n_tp,)), dma((n_tp,)),
        ],
        compiler_params=pltpu.CompilerParams(collective_id=3 + layer, has_side_effects=True, vmem_limit_bytes=VMEM_MAX),
        cost_estimate=pl.CostEstimate(flops=2 * seq * seq * cols, bytes_accessed=4 * seq * cols, transcendentals=seq * seq),
        name="attention" + str(layer),
    )(qkv_all, resid, w_o)


def mlp_kernel(layer, r_hbm, gain_ref, wg_hbm, wu_hbm, wd_hbm, out_hbm,
               wg, wu, wd, xbuf, prec, recv, acc, stash, act,
               lsem, sx, sy, ag, fs, fr, ps, pr, rr, ss):
    _, _, partners = coords()
    mate, dev_x, dev_y = partners
    rows, width = acc.shape
    half = rows // 2
    hid = act.shape[1]
    h0, h1 = pl.ds(0, half), pl.ds(half, half)
    hs = (h0, h1)
    nb = 64

    load_r = pltpu.make_async_copy(r_hbm, acc, lsem.at[0])
    load_r.start()
    greet(partners)
    loads = [pltpu.make_async_copy(src.at[layer], dst, lsem.at[k + 1]) for k, (src, dst) in enumerate(((wg_hbm, wg), (wu_hbm, wu), (wd_hbm, wd)))]
    load_r.wait()
    for copy in loads:
        copy.start()
    gather = RowGather(xbuf, sx, sy, ag, fs, fr, partners)
    gather.start(lambda k: norm_rows(acc, gain_ref, xbuf.at[0, 0], k * half, half))

    def partial_send(w):
        return rcopy(xbuf.at[w, 1], prec.at[w], ps.at[w], pr.at[w], mate)

    stage = (rcopy(xbuf.at[1, 1, h0], recv.at[0], ss.at[0], rr.at[0], dev_x),
             rcopy(xbuf.at[1, 1, h1], recv.at[1], ss.at[1], rr.at[1], dev_y),
             rcopy(xbuf.at[2, 1, h0], recv.at[2], ss.at[2], rr.at[2], dev_x),
             rcopy(xbuf.at[2, 1, h1], recv.at[3], ss.at[3], rr.at[3], dev_y),
             rcopy(xbuf.at[3, 1, h0], recv.at[4], ss.at[4], rr.at[4], dev_y),
             rcopy(xbuf.at[3, 1, h1], recv.at[5], ss.at[5], rr.at[5], dev_x))

    for copy in loads:
        copy.wait()
    cut = 768
    nd = 1024

    def gate_up(x_at, at):
        g = lax.dot_general(x_at[...], wg[at, :], (((1,), (1,)), ((), ())), preferred_element_type=F32)
        u = lax.dot_general(x_at[...], wu[at, :], (((1,), (1,)), ((), ())), preferred_element_type=F32)
        act[:, at] = (g * jax.nn.sigmoid(g) * u).astype(BF16)

    @pl.loop(0, 8)
    def _(s):
        w = lax.div(s, 2)
        rc = 1 - lax.rem(s, 2)

        @pl.when(rc == 1)
        def _():
            gather.forward(w).wait_recv()
        x_at = xbuf.at[w, rc]
        gate_up(x_at, pl.ds(0, cut))
        gate_up(x_at, pl.ds(cut, hid - cut))

        @pl.when(rc == 0)
        def _():
            @pl.when(w < 3)
            def _():
                gather.arrive(w + 1)
            partial_send(w).wait()

        @pl.loop(0, width // nd)
        def _(n):
            at = pl.ds(pl.multiple_of(n * nd, nd), nd)
            val = jnp.dot(act[...], wd[:, at], preferred_element_type=F32)

            @pl.when(rc == 1)
            def _():
                xbuf[w, 1, :, at] = val.astype(BF16)

            @pl.when(rc == 0)
            def _():
                total = val + prec[w, :, at].astype(F32)

                @pl.when(w == 0)
                def _():
                    acc[:, at] = acc[:, at] + total

                @pl.when(w == 3)
                def _():
                    stash[:, at] = total

                @pl.when((w == 1) | (w == 2))
                def _():
                    xbuf[w, 1, :, at] = total.astype(BF16)

        @pl.when(rc == 1)
        def _():
            partial_send(w).start()

        @pl.when(s == 3)
        def _():
            stage[0].start()
            stage[1].start()

        @pl.when(s == 5)
        def _():
            stage[2].start()
            stage[3].start()

    def blocks_of(k):
        def each(fn):
            @pl.loop(0, half // nb)
            def _(b):
                fn(pl.ds(pl.multiple_of(b * nb, nb), nb), pl.ds(pl.multiple_of(k * half + b * nb, nb), nb))
        return each

    for k in range(2):
        stage[k].wait_recv()

        @blocks_of(k)
        def _(at, to):
            acc[to, :] = acc[to, :] + recv[k, at, :].astype(F32)
    for k in range(2):
        stage[2 + k].wait_recv()

        @blocks_of(k)
        def _(at, to):
            xbuf[3, 1, to, :] = (stash[to, :] + recv[2 + k, at, :].astype(F32)).astype(BF16)
        stage[4 + k].start()
    gather.finish()
    narrow = out_hbm.dtype == BF16
    final = xbuf.at[0, 0] if narrow else acc
    outs = []
    for k in range(2):
        stage[4 + k].wait_recv()

        @blocks_of(k)
        def _(at, to):
            final[to, :] = (acc[to, :] + recv[4 + k, at, :].astype(F32)).astype(final.dtype)
        outs.append(pltpu.make_async_copy(final.at[hs[k]], out_hbm.at[hs[k]], lsem.at[k]))
        outs[k].start()
    for copy in stage:
        copy.wait_send()
    for copy in outs:
        copy.wait()


def mlp(layer, resid, gain, w_gate, w_up, w_down, out_dtype):
    rows, width = resid.shape
    hid = w_gate.shape[1]
    half = rows // 2
    any_spec = pl.BlockSpec(memory_space=pl.ANY)
    dma = pltpu.SemaphoreType.DMA
    return pl.pallas_call(
        functools.partial(mlp_kernel, layer),
        out_shape=jax.ShapeDtypeStruct((rows, width), out_dtype),
        in_specs=[any_spec, pl.BlockSpec(memory_space=pltpu.VMEM), any_spec, any_spec, any_spec],
        out_specs=any_spec,
        scratch_shapes=[
            pltpu.VMEM((hid, width), BF16),
            pltpu.VMEM((hid, width), BF16),
            pltpu.VMEM((hid, width), BF16),
            pltpu.VMEM((4, 2, rows, width), BF16),
            pltpu.VMEM((4, rows, width), BF16),
            pltpu.VMEM((6, half, width), BF16),
            pltpu.VMEM((rows, width), F32),
            pltpu.VMEM((rows, width), F32),
            pltpu.VMEM((rows, hid), BF16),
            dma((4,)),
        ] + gather_sems() + [dma((4,)), dma((4,)), dma((6,)), dma((6,))],
        compiler_params=pltpu.CompilerParams(collective_id=5 + layer, has_side_effects=True, vmem_limit_bytes=VMEM_MAX),
        cost_estimate=pl.CostEstimate(flops=6 * 8 * rows * width * hid, bytes_accessed=6 * width * hid, transcendentals=8 * rows * hid),
        name="mlp" + str(layer),
    )(resid, gain, w_gate, w_up, w_down)


def solution(mesh):
    n_tp = mesh.shape['tp']
    tok_spec = P('dp', 'tp', None)
    in_specs = (tok_spec, P(), P(None, None, 'tp', None), P(), P(None, 'tp', None, None), P(), P(None, None, 'tp'), P(None, None, 'tp'), P(None, 'tp', None))

    def body(hidden, norm_attn, w_q, w_kv, w_o, norm_mlp, w_gate, w_up, w_down):
        n_layers, width, heads, head_dim = w_q.shape
        n_kv = w_kv.shape[3]
        rows = hidden.shape[1]
        kv_head = (lax.axis_index('tp') * n_kv) // n_tp
        cos_t, sin_t = rope_tables(rows * n_tp, head_dim)
        kv = lax.dynamic_index_in_dim(w_kv, kv_head, axis=3, keepdims=False)
        w_qkv = jnp.concatenate([w_q.reshape(n_layers, width, heads * head_dim), kv.reshape(n_layers, width, 2 * head_dim)], axis=2)
        w_o = w_o.reshape(n_layers, heads * head_dim, width)
        w_gate = jnp.swapaxes(w_gate, 1, 2)
        w_up = jnp.swapaxes(w_up, 1, 2)
        resid = hidden[0]
        for layer in range(n_layers):
            qkv_all = qkv(layer, resid, norm_attn[layer][None], w_qkv[layer], cos_t, sin_t, heads, head_dim, n_tp)
            resid = attention(layer, qkv_all, resid, w_o, heads, head_dim, n_tp)
            resid = mlp(layer, resid, norm_mlp[layer][None], w_gate, w_up, w_down, BF16 if layer == n_layers - 1 else F32)
        return resid[None]

    return jax.shard_map(body, mesh=mesh, in_specs=in_specs, out_specs=tok_spec, check_vma=False)
```

time: 837 us -> 648 us (0.77); the launches traced: 826 us -> 647 us
  waiting for transfers between devices: 166 us -> 0 us
  Pallas kernels: 445 us -> 603 us
  local copies, waits for them, and re-layouts: 95.2 us -> 29.6 us
  matrix products: 54.1 us -> 0 us
  other arithmetic: 43.9 us -> 14 us
  between operations: 13.9 us -> 0.08 us
    pallas_call x2 -> x4, Pallas kernels: 94.4 us -> 306 us  [the longest x2 163 us: qkv(): pl.pallas_call(functools.partial(qkv_kernel, heads, head_dim), out_shape=...]
    all_gather x4 -> x0, waiting for transfers between devices: 139 us -> none  [the longest x2 139 us: body(): lax.all_gather(rms_norm(resid, norm_attn[layer]), 'tp', axis=0, tiled=True)]
    pallas_call x2, Pallas kernels: 350 us -> 297 us  [mlp(): pl.pallas_call(functools.partial(mlp_kernel, layer), out_shape=jax.ShapeD...]
    unnamed x41 -> x6, local copies, waits for them, and re-layouts: 53.3 us -> 12.2 us
    unnamed x4 -> x0, matrix products: 33.5 us -> none
    all_to_all x2 -> x0, waiting for transfers between devices: 26.5 us -> none  [body(): lax.all_to_all(context.reshape(n_tp, rows, heads * head_dim), 'tp', 0, 0)]
    concatenate x6 -> x1, other arithmetic: 25.7 us -> 3.12 us  [rope_tables(): jnp.concatenate([cos_t, cos_t], axis=1)]
    dot_general x2 -> x0, matrix products: 20.6 us -> none  [body(): jnp.dot(blocks, o_full.reshape(-1, width), preferred_element_type=F32)]
  transfers between devices with their start and end apart: 6 -> 0, of which waited for: 3 -> 0; matrix products, arithmetic and copies ran while one was open for 19% -> 0% of each run, Pallas kernels for 11% -> 0%
where the time goes in v2:
time: 648 us; the launch traced here: 647 us
  Pallas kernels  603 us (93%)
  local copies, waits for them, and re-layouts  29.6 us (5%)
  other arithmetic  14 us (2%)
    pallas_call x2, Pallas kernels, mlp(): pl.pallas_call(functools.partial(mlp_kernel, layer), out_shape=jax.ShapeD...  297 us
    pallas_call x2, Pallas kernels, qkv(): pl.pallas_call(functools.partial(qkv_kernel, heads, head_dim), out_shape=...  163 us
    pallas_call x2, Pallas kernels, attention(): pl.pallas_call(functools.partial(attn_kernel, layer, n_tp, heads, head_di...  143 us

profile of v2, /device:TPU:0, one launch (start us, length us, event | category | flops | bytes accessed | tf_op | source)
XLA Modules:
  0.0 646.9 jit_solution(11383418393122819220)
XLA Ops:
  0.0 8.4 %constant_dynamic-slice_fusion = bf16[2,2048,2,1,128]{4,3,2,1,0:T(2,128)(2,1)} fusion(bf16[2,2048,2,2,128]{4,3,2,1,0:T(2,128)(2,1)} %param.12, s32[]{:T(128)S(6)} %select_n.10), kind=kLoop, calls=%fused_computation.13 | loop fusion | bytes 4194308 | tf_op jit(solution)/shard_map/jit(dynamic_index_in_dim)/dynamic_slice | solution.py:484
  8.4 9.0 %copy.12 = bf16[2,2048,2,1,128]{1,4,2,0,3:T(8,128)(2,1)S(1)} copy(bf16[2,2048,2,1,128]{4,3,2,1,0:T(2,128)(2,1)} %constant_dynamic-slice_fusion) | data formatting | bytes 4194304
  17.4 2.5 copy.11
  19.9 0.0 copy-start
  19.9 4.5 reshape.19
  24.5 0.0 copy-done
  24.5 3.4 fusion.2
  27.9 7.5 %fusion.3 = (f32[4096,64]{1,0:T(8,128)S(1)}, f32[4096,64]{1,0:T(8,128)S(1)}, f32[4096,64]{1,0:T(8,128)S(1)}) fusion(f32[64]{0:T(128)S(1)} %multiply_power_fusion, f32[4096]{0:T(1024)S(1)} %iota_convert_fusion), kind=kLoop, calls=%fused_computation.10 | loop fusion | flops 524288 | bytes 3162368 | tf_op jit(solution)/shard_map/neg | solution.py:23
  35.4 0.0 copy-start.1
  35.4 3.1 pad_maximum_fusion.1
  38.5 0.0 copy-done.1
  38.5 0.6 fusion.5
  39.1 82.9 %qkv0.1.qkv_ref = bf16[4096,512]{1,0:T(8,128)(2,1)} custom-call(bf16[512,2048]{1,0:T(8,128)(2,1)} %bitcast.16, f32[1,2048]{1,0:T(1,128)} %get-tuple-element.13.gain_ref, bf16[2048,512]{1,0:T(8,128)(2,1)} %get-tuple-element.6.w_ref, f32[4096,128]{1,0:T(8,128)} %get-tuple-element.14.cos_ref, f32[4096,128]{1,0:T(8,128)} %get-tuple-element.15.sin_ref), custom_call_target="tpu_custom_call" | custom-call | flops 8589934592 | bytes 8388608 | tf_op jit(solution)/shard_map/qkv0/pallas_call | solution.py:157
  122.0 70.6 %attention0.1.r_hbm = f32[512,2048]{1,0:T(8,128)} custom-call(bf16[4096,512]{1,0:T(8,128)(2,1)} %qkv0.1.qkv_ref, bf16[512,2048]{1,0:T(8,128)(2,1)} %bitcast.17, bf16[2,256,2048]{2,1,0:T(8,128)(2,1)} %bitcast.18), custom_call_target="tpu_custom_call" | custom-call | flops 8589934592 | bytes 4194304 | tf_op jit(solution)/shard_map/attention0/pallas_call | solution.py:289
  192.6 1.4 fusion.4
  194.0 149.6 %mlp0.1.r_ref = f32[512,2048]{1,0:T(8,128)} custom-call(f32[512,2048]{1,0:T(8,128)} %attention0.1.r_hbm, f32[1,2048]{1,0:T(1,128)} %get-tuple-element.11.gain_ref, bf16[2,1376,2048]{2,1,0:T(8,128)(2,1)} %bitcast.12, bf16[2,1376,2048]{2,1,0:T(8,128)(2,1)} %bitcast.14, bf16[2,1376,2048]{2,1,0:T(8,128)(2,1)} %wd_hbm.3), custom_call_target="tpu_custom_call" | custom-call | flops 69256347648 | bytes 16908288 | tf_op jit(solution)/shard_map/mlp0/pallas_call | solution.py:450
  343.7 80.2 %qkv1.1.qkv_ref = bf16[4096,512]{1,0:T(8,128)(2,1)} custom-call(f32[512,2048]{1,0:T(8,128)} %mlp0.1.r_ref, f32[1,2048]{1,0:T(1,128)} %get-tuple-element.12.gain_ref, bf16[2048,512]{1,0:T(8,128)(2,1)} %get-tuple-element.5.w_ref, f32[4096,128]{1,0:T(8,128)} %get-tuple-element.14.cos_ref, f32[4096,128]{1,0:T(8,128)} %get-tuple-element.15.sin_ref), custom_call_target="tpu_custom_call" | custom-call | flops 8589934592 | bytes 8388608 | tf_op jit(solution)/shard_map/qkv1/pallas_call | solution.py:157
  423.9 72.1 %attention1.1.r_hbm = f32[512,2048]{1,0:T(8,128)} custom-call(bf16[4096,512]{1,0:T(8,128)(2,1)} %qkv1.1.qkv_ref, f32[512,2048]{1,0:T(8,128)} %mlp0.1.r_ref, bf16[2,256,2048]{2,1,0:T(8,128)(2,1)} %bitcast.19), custom_call_target="tpu_custom_call" | custom-call | flops 8589934592 | bytes 4194304 | tf_op jit(solution)/shard_map/attention1/pallas_call | solution.py:289
  496.0 147.7 %mlp1.1 = bf16[512,2048]{1,0:T(8,128)(2,1)} custom-call(f32[512,2048]{1,0:T(8,128)} %attention1.1.r_hbm, f32[1,2048]{1,0:T(1,128)} %get-tuple-element.10.gain_ref, bf16[2,1376,2048]{2,1,0:T(8,128)(2,1)} %bitcast.13, bf16[2,1376,2048]{2,1,0:T(8,128)(2,1)} %bitcast.15, bf16[2,1376,2048]{2,1,0:T(8,128)(2,1)} %wd_hbm.3), custom_call_target="tpu_custom_call" | custom-call | flops 69256347648 | bytes 16908288 | tf_op jit(solution)/shard_map/mlp1/pallas_call | solution.py:450
  643.7 3.2 copy.14
  (2 shorter events, 0.0 us)
Async XLA Ops:
  19.9 4.5 copy-start
  35.4 3.1 copy-start.1

commit v3 on v2

--- a/solution.py
+++ b/solution.py
@@ -2,6 +2,7 @@
 import math
 import jax
 import jax.numpy as jnp
+import numpy as np
 from jax import lax
 from jax.experimental import pallas as pl
 from jax.experimental.pallas import tpu as pltpu
@@ -15,12 +16,16 @@
 BF16 = jnp.bfloat16
 
 
-def rope_tables(seq, head_dim):
+def rope_tables(seq, step, head_dim):
     half_dim = head_dim // 2
-    inv_freq = jnp.power(ROPE_BASE, -2.0 * jnp.arange(half_dim, dtype=F32) / head_dim)
-    angles = jnp.arange(seq).astype(F32)[:, None] * inv_freq[None, :]
-    cos_t, sin_t = jnp.cos(angles), jnp.sin(angles)
-    return jnp.concatenate([cos_t, cos_t], axis=1), jnp.concatenate([-sin_t, sin_t], axis=1)
+    inv_freq = ROPE_BASE ** (-2.0 * np.arange(half_dim, dtype=np.float64) / head_dim)
+
+    def table(positions):
+        angles = positions.astype(np.float64)[:, None] * inv_freq[None, :]
+        cos_t, sin_t = np.cos(angles), np.sin(angles)
+        return np.stack([np.concatenate([cos_t, cos_t], axis=1), np.concatenate([-sin_t, sin_t], axis=1)]).astype(np.float32)
+
+    return table(np.arange(0, seq, step)), table(np.arange(step))
 
 
 def coords():
@@ -42,7 +47,7 @@
 
 
 class RowGather:
-    def __init__(self, xbuf, sx, sy, ag, fs, fr, partners):
+    def __init__(self, xbuf, sx, sy, ag, fs, fr, partners, greeted=3):
         mate, dev_x, dev_y = partners
         rows = xbuf.shape[2]
         half = rows // 2
@@ -51,6 +56,7 @@
         own = xbuf.at[0, 0]
         self.xbuf, self.ag, self.fs, self.fr, self.mate = xbuf, ag, fs, fr, mate
         self.halves = (h0, h1)
+        self.greeted = greeted
 
         def piece(k, sem, dev, first, size, window, slot):
             at = pl.ds(first, size)
@@ -67,7 +73,7 @@
 
     def start(self, norm_half):
         norm_half(0)
-        pl.semaphore_wait(pltpu.get_barrier_semaphore(), 3)
+        pl.semaphore_wait(pltpu.get_barrier_semaphore(), self.greeted)
         self.first[0].start()
         norm_half(1)
         self.first[1].start()
@@ -109,72 +115,14 @@
         dst[at, :] = (r * lax.rsqrt(mean_sq + EPS) * gain_ref[...]).astype(BF16)
 
 
-def qkv_kernel(heads, head_dim, r_ref, gain_ref, w_ref, cos_ref, sin_ref, out_ref, xbuf, sx, sy, ag, fs, fr):
-    _, (yy, xx, c), partners = coords()
-    rows = xbuf.shape[2]
-    half = rows // 2
-    greet(partners)
-    gather = RowGather(xbuf, sx, sy, ag, fs, fr, partners)
-    gather.start(lambda k: norm_rows(r_ref, gain_ref, xbuf.at[0, 0], k * half, half))
-
-    @pl.loop(0, 8)
-    def _(s):
-        w = lax.div(s, 2)
-        rc = lax.rem(s, 2)
-
-        @pl.when((rc == 0) & (w >= 1))
-        def _():
-            gather.arrive(w)
-
-        @pl.when(rc == 1)
-        def _():
-            gather.forward(w).wait_recv()
-        proj = jnp.dot(xbuf[w, rc], w_ref[...], preferred_element_type=F32)
-        core = c + rc - 2 * c * rc
-        one = lax.rem(lax.div(w + 1, 2), 2)
-        two = lax.div(w, 2)
-        for k in range(2):
-            flip_x, flip_y = (one, two) if k == 0 else (two, one)
-            chip = 2 * (yy + flip_y - 2 * yy * flip_y) + xx + flip_x - 2 * xx * flip_x
-            at = pl.ds(pl.multiple_of((chip * 2 + core) * rows + k * half, half), half)
-            part = proj[k * half:(k + 1) * half]
-            cos_b = cos_ref[at, :]
-            sin_b = sin_ref[at, :]
-            for h in range(heads + 1):
-                cols = slice(h * head_dim, (h + 1) * head_dim)
-                z = part[:, cols]
-                out_ref[at, cols] = (z * cos_b + pltpu.roll(z, head_dim // 2, 1) * sin_b).astype(BF16)
-            cols = slice((heads + 1) * head_dim, (heads + 2) * head_dim)
-            out_ref[at, cols] = part[:, cols].astype(BF16)
-    gather.finish()
-
-
-def qkv(layer, resid, gain, w_qkv, cos_t, sin_t, heads, head_dim, n_tp):
-    rows, width = resid.shape
-    cols = w_qkv.shape[1]
-    seq = rows * n_tp
-    vmem = pl.BlockSpec(memory_space=pltpu.VMEM)
-    return pl.pallas_call(
-        functools.partial(qkv_kernel, heads, head_dim),
-        out_shape=jax.ShapeDtypeStruct((seq, cols), BF16),
-        in_specs=[vmem] * 5,
-        out_specs=vmem,
-        scratch_shapes=[pltpu.VMEM((4, 2, rows, width), BF16)] + gather_sems(),
-        compiler_params=pltpu.CompilerParams(collective_id=1 + layer, has_side_effects=True, vmem_limit_bytes=VMEM_MAX),
-        cost_estimate=pl.CostEstimate(flops=2 * seq * width * cols, bytes_accessed=4 * seq * cols, transcendentals=0),
-        name="qkv" + str(layer),
-    )(resid, gain, w_qkv, cos_t, sin_t)
-
-
 def attend(qkv_ref, block, bq, bk, heads, head_dim):
     scale = math.log2(math.e) / math.sqrt(head_dim)
-    rows = lax.broadcasted_iota(jnp.int32, (bq, bk), 0)
-    cols = lax.broadcasted_iota(jnp.int32, (bq, bk), 1)
+    mask = lax.broadcasted_iota(jnp.int32, (bq, bq), 0) >= lax.broadcasted_iota(jnp.int32, (bq, bq), 1)
     q_at = pl.ds(pl.multiple_of(block * bq, bq), bq)
     qs = [qkv_ref[q_at, h * head_dim:(h + 1) * head_dim] for h in range(heads)]
 
-    def step(j, carry, masked):
-        at = pl.ds(pl.multiple_of(j * bk, bk), bk)
+    def step(first, count, carry, masked):
+        at = pl.ds(pl.multiple_of(first, bq), count)
         k_blk = qkv_ref[at, heads * head_dim:(heads + 1) * head_dim]
         v_blk = qkv_ref[at, (heads + 1) * head_dim:(heads + 2) * head_dim]
         out = []
@@ -182,7 +130,7 @@
             m, l, acc = carry[h]
             s = lax.dot_general(qs[h], k_blk, (((1,), (1,)), ((), ())), preferred_element_type=F32)
             if masked:
-                s = jnp.where(block * bq + rows >= j * bk + cols, s, -jnp.inf)
+                s = jnp.where(mask, s, -jnp.inf)
             m_new = jnp.maximum(m, jnp.max(s, axis=-1, keepdims=True))
             p = jnp.exp2((s - m_new) * scale)
             alpha = jnp.exp2((m - m_new) * scale)
@@ -191,52 +139,119 @@
             out.append((m_new, l, acc))
         return tuple(out)
 
-    init = tuple((jnp.full((bq, 1), -jnp.inf, F32), jnp.zeros((bq, 1), F32), jnp.zeros((bq, head_dim), F32)) for _ in range(heads))
-    last = lax.div(block * bq, bk)
-    carry = lax.fori_loop(0, last, functools.partial(step, masked=False), init)
-    carry = step(last, carry, True)
+    carry = tuple((jnp.full((bq, 1), -jnp.inf, F32), jnp.zeros((bq, 1), F32), jnp.zeros((bq, head_dim), F32)) for _ in range(heads))
+    carry = step(block * bq, bq, carry, True)
+    full = lax.div(block * bq, bk)
+    carry = lax.fori_loop(0, full, lambda j, cur: step(j * bk, bk, cur, False), carry)
+    carry = lax.fori_loop(full * (bk // bq), block, lambda j, cur: step(j * bq, bq, cur, False), carry)
     return [(acc / l).astype(BF16) for _, l, acc in carry]
 
 
-def attn_kernel(layer, n_tp, heads, head_dim, bk, qkv_ref, r_ref, wo_hbm, out_ref,
-                wo, ctx, ctx_out, lsem, sx, sy, ag, fs, fr, cs, cr):
+def attn_kernel(layer, n_tp, n_kv, heads, head_dim, bk, r_hbm, gain_ref, far_ref, near_ref, wq_hbm, wkv_hbm, wo_hbm, out_hbm,
+                xbuf, rin, wq, wkv, wide, w_all, qkv_ref, wo, ctx, ctx_out, res,
+                lsem, sx, sy, ag, fs, fr, ox, oy, oz, oa, ob, om, on, cs, cr, es):
     t, (yy, xx, c), partners = coords()
+    z = lax.axis_index('dp')
     mate, dev_x, dev_y = partners
-    rows = out_ref.shape[0]
-    width = out_ref.shape[1]
+    dev_d = dev_x + dev_y - t
+    rows, width = res.shape
+    half = rows // 2
     cols = heads * head_dim
-    load_o = pltpu.make_async_copy(wo_hbm.at[layer], wo.at[pl.ds(pl.multiple_of(t * cols, cols), cols)], lsem.at[0])
-    load_o.start()
+
+    load_r = pltpu.make_async_copy(r_hbm, rin, lsem.at[0])
+    load_r.start()
     others = [lax.rem(t + k, n_tp) for k in range(1, n_tp)]
     greet(others)
-    load_o.wait()
-    pl.semaphore_wait(pltpu.get_barrier_semaphore(), n_tp - 1)
-
-    def span(dev, k):
-        return pl.ds(pl.multiple_of(dev * cols + k * head_dim, head_dim), head_dim)
+    pl.semaphore_signal(pltpu.get_barrier_semaphore(), inc=1, device_id={'dp': 1 - z, 'tp': t}, device_id_type=MESH)
+    own_o = pl.ds(pl.multiple_of(t * cols, cols), cols)
+    loads = (pltpu.make_async_copy(wq_hbm.at[layer], wq, lsem.at[1]),
+             pltpu.make_async_copy(wkv_hbm.at[layer], wkv, lsem.at[2]),
+             pltpu.make_async_copy(wo_hbm.at[layer], wo.at[own_o], lsem.at[3]))
+    load_r.wait()
+    for copy in loads:
+        copy.start()
+    gather = RowGather(xbuf, sx, sy, ag, fs, fr, partners, n_tp)
+    gather.start(lambda k: norm_rows(rin, gain_ref, xbuf.at[0, 0], k * half, half))
+    for copy in loads:
+        copy.wait()
+
+    kv_head = lax.div(t * n_kv, n_tp)
+    nd = 256
+
+    @pl.loop(0, width // nd)
+    def _(b):
+        to = pl.ds(pl.multiple_of(b * nd, nd), nd)
+        wide[pl.ds(0, heads * nd), :] = wq[pl.ds(pl.multiple_of(b * heads * nd, nd), heads * nd), :].astype(F32)
+        for h in range(heads):
+            w_all[to, h * head_dim:(h + 1) * head_dim] = wide[pl.ds(h, nd, stride=heads), :].astype(BF16)
+        wide[pl.ds(0, 2 * n_kv * nd), :] = wkv[pl.ds(pl.multiple_of(b * 2 * n_kv * nd, nd), 2 * n_kv * nd), :].astype(F32)
+        for h in range(2):
+            w_all[to, (heads + h) * head_dim:(heads + h + 1) * head_dim] = wide[pl.ds(h * n_kv + kv_head, nd, stride=2 * n_kv), :].astype(BF16)
+
+    @pl.loop(0, 8)
+    def _(s):
+        w = lax.div(s, 2)
+        rc = lax.rem(s, 2)
+
+        @pl.when((rc == 0) & (w >= 1))
+        def _():
+            gather.arrive(w)
+
+        @pl.when(rc == 1)
+        def _():
+            gather.forward(w).wait_recv()
+        proj = jnp.dot(xbuf[w, rc], w_all[...], preferred_element_type=F32)
+        core = c + rc - 2 * c * rc
+        one = lax.rem(lax.div(w + 1, 2), 2)
+        two = lax.div(w, 2)
+        for k in range(2):
+            flip_x, flip_y = (one, two) if k == 0 else (two, one)
+            chip = 2 * (yy + flip_y - 2 * yy * flip_y) + xx + flip_x - 2 * xx * flip_x
+            piece = (chip * 2 + core) * 2 + k
+            at = pl.ds(pl.multiple_of(piece * half, half), half)
+            part = proj[k * half:(k + 1) * half]
+            cos_f, sin_f = far_ref[0, pl.ds(piece, 1), :], far_ref[1, pl.ds(piece, 1), :]
+            cos_n, sin_n = near_ref[0], near_ref[1]
+            cos_b = cos_f * cos_n - sin_f * sin_n
+            sin_b = sin_f * cos_n + cos_f * sin_n
+            for h in range(heads + 1):
+                at_h = slice(h * head_dim, (h + 1) * head_dim)
+                v = part[:, at_h]
+                qkv_ref[at, at_h] = (v * cos_b + pltpu.roll(v, head_dim // 2, 1) * sin_b).astype(BF16)
+            at_h = slice((heads + 1) * head_dim, (heads + 2) * head_dim)
+            qkv_ref[at, at_h] = part[:, at_h].astype(BF16)
+
+    part_rows = head_dim // 2
+
+    def span(dev, k, p):
+        return pl.ds(pl.multiple_of(dev * cols + k * head_dim + p * part_rows, part_rows), part_rows)
 
     def same(at, ssem, rsem, dev):
         return rcopy(wo.at[at], wo.at[at], ssem, rsem, dev)
 
-    send = (same(span(t, 0), sx.at[0], ag.at[0], dev_x), same(span(t, 1), sy.at[0], ag.at[1], dev_y),
-            same(span(t, 1), sx.at[1], ag.at[2], dev_x), same(span(t, 0), sy.at[1], ag.at[3], dev_y))
-    relay = (same(span(dev_y, 1), sx.at[2], ag.at[4], dev_x), same(span(dev_x, 0), sy.at[2], ag.at[5], dev_y))
-    dev_d = dev_x + dev_y - t
-    landed = (span(dev_x, 0), span(dev_y, 1), span(dev_x, 1), span(dev_y, 0), span(dev_d, 1), span(dev_d, 0))
-    own = pl.ds(pl.multiple_of(t * cols, cols), cols)
-    to_mate = tuple(same(landed[k], fs.at[k], fr.at[k], mate) for k in range(6)) + (same(own, fs.at[6], fr.at[6], mate),)
-
-    def take(k):
-        pltpu.make_async_copy(wo.at[landed[k]], wo.at[landed[k]], ag.at[k]).wait()
+    def across(at, ssem, rsem):
+        return pltpu.make_async_remote_copy(src_ref=wo.at[at], dst_ref=wo.at[at], send_sem=ssem, recv_sem=rsem,
+                                            device_id={'dp': 1 - z, 'tp': t}, device_id_type=MESH)
+
+    send = (same(span(t, 0, z), ox.at[0], oa.at[0], dev_x), same(span(t, 1, z), oy.at[0], oa.at[1], dev_y),
+            same(span(t, 1, z), ox.at[1], oa.at[2], dev_x), same(span(t, 0, z), oy.at[1], oa.at[3], dev_y))
+    relay = (same(span(dev_y, 1, z), ox.at[2], oa.at[4], dev_x), same(span(dev_x, 0, z), oy.at[2], oa.at[5], dev_y))
+    from_dev = ((dev_x, 0), (dev_y, 1), (dev_x, 1), (dev_y, 0), (dev_d, 1), (dev_d, 0))
+    via_z = [across(span(dev, k, z), oz.at[i], ob.at[i]) for i, (dev, k) in enumerate(from_dev)]
+    to_mate = [same(span(dev, k, z), om.at[i], on.at[i], mate) for i, (dev, k) in enumerate(from_dev)]
+    to_mate += [same(span(dev, k, 1 - z), om.at[6 + i], on.at[6 + i], mate) for i, (dev, k) in enumerate(from_dev)]
+    to_mate.append(same(own_o, om.at[12], on.at[12], mate))
+
+    def take(i, sem, p):
+        at = span(from_dev[i][0], from_dev[i][1], p)
+        pltpu.make_async_copy(wo.at[at], wo.at[at], sem.at[i]).wait()
 
     for copy in send:
         copy.start()
-    to_mate[6].start()
-
-    mine = pl.ds(pl.multiple_of(t * cols, cols), cols)
+    to_mate[12].start()
 
     def ctx_send(i, dev):
-        return rcopy(ctx_out.at[i], ctx.at[:, mine], cs.at[i], cr.at[t], dev)
+        return rcopy(ctx_out.at[i], ctx.at[:, own_o], cs.at[i], cr.at[t], dev)
 
     @pl.loop(0, n_tp)
     def _(i):
@@ -244,17 +259,28 @@
 
         @pl.when(i == 3)
         def _():
-            take(0)
-            take(1)
+            take(0, oa, z)
+            take(1, oa, z)
             for copy in relay:
                 copy.start()
-
-        @pl.when(i == 6)
-        def _():
-            for k in range(2, 6):
-                take(k)
+            take(2, oa, z)
+            take(3, oa, z)
+            for k in range(4):
+                via_z[k].start()
+                to_mate[k].start()
+
+        @pl.when(i == 5)
+        def _():
+            for k in range(4, 6):
+                take(k, oa, z)
+                via_z[k].start()
+                to_mate[k].start()
+
+        @pl.when(i == 7)
+        def _():
             for k in range(6):
-                to_mate[k].start()
+                take(k, ob, 1 - z)
+                to_mate[6 + k].start()
         for h, val in enumerate(attend(qkv_ref, block, rows, bk, heads, head_dim)):
             ctx_out[i, :, h * head_dim:(h + 1) * head_dim] = val
 
@@ -262,45 +288,60 @@
         def _():
             ctx_send(i, block).start()
 
-    ctx[:, mine] = ctx_out[n_tp - 1]
+    ctx[:, own_o] = ctx_out[n_tp - 1]
     for copy in to_mate:
         copy.wait_recv()
     for dev in others:
         at = pl.ds(pl.multiple_of(dev * cols, cols), cols)
         pltpu.make_async_copy(ctx_out.at[0], ctx.at[:, at], cr.at[dev]).wait()
     nc = 512
-
-    @pl.loop(0, width // nc)
-    def _(n):
-        at = pl.ds(pl.multiple_of(n * nc, nc), nc)
-        out_ref[:, at] = r_ref[:, at].astype(F32) + jnp.dot(ctx[...], wo[:, at], preferred_element_type=F32)
-    for copy in send + relay + to_mate:
+    outs = []
+    for n in range(width // nc):
+        at = pl.ds(n * nc, nc)
+        res[:, at] = rin[:, at].astype(F32) + jnp.dot(ctx[...], wo[:, at], preferred_element_type=F32)
+        outs.append(pltpu.make_async_copy(res.at[:, at], out_hbm.at[:, at], es.at[n]))
+        outs[n].start()
+    gather.finish()
+    for copy in list(send + relay) + via_z + to_mate:
         copy.wait_send()
     for i in range(n_tp - 1):
         ctx_send(i, mate).wait_send()
-
-
-def attention(layer, qkv_all, resid, w_o, heads, head_dim, n_tp, bk=1024):
+    for copy in outs:
+        copy.wait()
+
+
+def attention(layer, resid, gain, far, near, w_q, w_kv, w_o, n_tp, bk=1024):
     rows, width = resid.shape
-    cols = heads * head_dim
+    cols, head_dim = w_o.shape[1], w_q.shape[2]
+    heads = cols // head_dim
+    n_kv = w_kv.shape[1] // (2 * width)
     seq = rows * n_tp
     vmem = pl.BlockSpec(memory_space=pltpu.VMEM)
+    anywhere = pl.BlockSpec(memory_space=pl.ANY)
     dma = pltpu.SemaphoreType.DMA
     return pl.pallas_call(
-        functools.partial(attn_kernel, layer, n_tp, heads, head_dim, bk),
+        functools.partial(attn_kernel, layer, n_tp, n_kv, heads, head_dim, bk),
         out_shape=jax.ShapeDtypeStruct((rows, width), F32),
-        in_specs=[vmem, vmem, pl.BlockSpec(memory_space=pl.ANY)],
-        out_specs=vmem,
+        in_specs=[anywhere, vmem, vmem, vmem, anywhere, anywhere, anywhere],
+        out_specs=anywhere,
         scratch_shapes=[
+            pltpu.VMEM((4, 2, rows, width), BF16),
+            pltpu.VMEM((rows, width), resid.dtype),
+            pltpu.VMEM(w_q.shape[1:], BF16),
+            pltpu.VMEM(w_kv.shape[1:], BF16),
+            pltpu.VMEM((256 * max(heads, 2 * n_kv), head_dim), F32),
+            pltpu.VMEM((width, cols + 2 * head_dim), BF16),
+            pltpu.VMEM((seq, cols + 2 * head_dim), BF16),
             pltpu.VMEM((n_tp * cols, width), BF16),
             pltpu.VMEM((rows, n_tp * cols), BF16),
             pltpu.VMEM((n_tp, rows, cols), BF16),
-            dma((1,)), dma((3,)), dma((3,)), dma((6,)), dma((7,)), dma((7,)), dma((n_tp,)), dma((n_tp,)),
-        ],
-        compiler_params=pltpu.CompilerParams(collective_id=3 + layer, has_side_effects=True, vmem_limit_bytes=VMEM_MAX),
+            pltpu.VMEM((rows, width), F32),
+            dma((4,)),
+        ] + gather_sems() + [dma((3,)), dma((3,)), dma((6,)), dma((6,)), dma((6,)), dma((13,)), dma((13,)), dma((n_tp,)), dma((n_tp,)), dma((4,))],
+        compiler_params=pltpu.CompilerParams(collective_id=1 + layer, has_side_effects=True, vmem_limit_bytes=VMEM_MAX),
         cost_estimate=pl.CostEstimate(flops=2 * seq * seq * cols, bytes_accessed=4 * seq * cols, transcendentals=seq * seq),
         name="attention" + str(layer),
-    )(qkv_all, resid, w_o)
+    )(resid, gain, far, near, w_q, w_kv, w_o)
 
 
 def mlp_kernel(layer, r_hbm, gain_ref, wg_hbm, wu_hbm, wd_hbm, out_hbm,
@@ -479,17 +520,15 @@
         n_layers, width, heads, head_dim = w_q.shape
         n_kv = w_kv.shape[3]
         rows = hidden.shape[1]
-        kv_head = (lax.axis_index('tp') * n_kv) // n_tp
-        cos_t, sin_t = rope_tables(rows * n_tp, head_dim)
-        kv = lax.dynamic_index_in_dim(w_kv, kv_head, axis=3, keepdims=False)
-        w_qkv = jnp.concatenate([w_q.reshape(n_layers, width, heads * head_dim), kv.reshape(n_layers, width, 2 * head_dim)], axis=2)
+        far, near = rope_tables(rows * n_tp, rows // 2, head_dim)
+        w_q = w_q.reshape(n_layers, width * heads, head_dim)
+        w_kv = w_kv.reshape(n_layers, width * 2 * n_kv, head_dim)
         w_o = w_o.reshape(n_layers, heads * head_dim, width)
         w_gate = jnp.swapaxes(w_gate, 1, 2)
         w_up = jnp.swapaxes(w_up, 1, 2)
         resid = hidden[0]
         for layer in range(n_layers):
-            qkv_all = qkv(layer, resid, norm_attn[layer][None], w_qkv[layer], cos_t, sin_t, heads, head_dim, n_tp)
-            resid = attention(layer, qkv_all, resid, w_o, heads, head_dim, n_tp)
+            resid = attention(layer, resid, norm_attn[layer][None], far, near, w_q, w_kv, w_o, n_tp)
             resid = mlp(layer, resid, norm_mlp[layer][None], w_gate, w_up, w_down, BF16 if layer == n_layers - 1 else F32)
         return resid[None]
 

time: 648 us -> 581 us (0.90)
  Pallas kernels: 603 us -> 574 us
  local copies, waits for them, and re-layouts: 29.6 us -> 5.97 us
  other arithmetic: 14 us -> 0 us
    pallas_call x4 -> x2, Pallas kernels: 306 us -> 273 us  [attention(): pl.pallas_call(functools.partial(attn_kernel, layer, n_tp, n_kv, heads, h...]
    unnamed x6 -> x1, local copies, waits for them, and re-layouts: 12.2 us -> 3.16 us
    dynamic_slice x1 -> x0, local copies, waits for them, and re-layouts: 8.43 us -> none  [body(): kv = lax.dynamic_index_in_dim(w_kv, kv_head, axis=3, keepdims=False)]
    neg x1 -> x0, other arithmetic: 7.48 us -> none  [rope_tables(): -sin_t]
    reshape x2 -> x0, local copies, waits for them, and re-layouts: 7.02 us -> none  [the longest x1 4.53 us: body(): w_q.reshape(n_layers, width, heads * head_dim)]
where the time goes in v3:
time: 581 us; the launch traced here: 580 us
  Pallas kernels  574 us (99%)
  local copies, waits for them, and re-layouts  5.97 us (1%)
    pallas_call x2, Pallas kernels, mlp(): pl.pallas_call(functools.partial(mlp_kernel, layer), out_shape=jax.ShapeD...  301 us
    pallas_call x2, Pallas kernels, attention(): pl.pallas_call(functools.partial(attn_kernel, layer, n_tp, n_kv, heads, h...  273 us

profile of v3, /device:TPU:0, one launch (start us, length us, event | category | flops | bytes accessed | tf_op | source)
XLA Modules:
  0.0 580.2 jit_solution(9734339344374200953)
XLA Ops:
  0.0 1.4 fusion.1
  1.4 1.4 fusion
  2.8 137.7 %attention0.1.r_hbm = f32[512,2048]{1,0:T(8,128)} custom-call(bf16[512,2048]{1,0:T(8,128)(2,1)} %bitcast.14, f32[1,2048]{1,0:T(1,128)} %get-tuple-element.8.gain_ref, f32[2,16,128]{2,1,0:T(8,128)} %constant.4.clone.far_ref, f32[2,256,128]{2,1,0:T(8,128)} %constant.5.clone.near_ref, bf16[2,4096,128]{2,1,0:T(8,128)(2,1)} %bitcast.15, ...), custom_call_target="tpu_custom_call" | custom-call | flops 8589934592 | bytes 4194304 | tf_op jit(solution)/shard_map/attention0/pallas_call | solution.py:322
  140.5 151.9 %mlp0.1.r_hbm = f32[512,2048]{1,0:T(8,128)} custom-call(f32[512,2048]{1,0:T(8,128)} %attention0.1.r_hbm, f32[1,2048]{1,0:T(1,128)} %get-tuple-element.6.gain_ref, bf16[2,1376,2048]{2,1,0:T(8,128)(2,1)} %bitcast.8, bf16[2,1376,2048]{2,1,0:T(8,128)(2,1)} %bitcast.10, bf16[2,1376,2048]{2,1,0:T(8,128)(2,1)} %wd_hbm.3), custom_call_target="tpu_custom_call" | custom-call | flops 69256347648 | bytes 16908288 | tf_op jit(solution)/shard_map/mlp0/pallas_call | solution.py:491
  292.4 135.8 %attention1.1.r_hbm = f32[512,2048]{1,0:T(8,128)} custom-call(f32[512,2048]{1,0:T(8,128)} %mlp0.1.r_hbm, f32[1,2048]{1,0:T(1,128)} %get-tuple-element.7.gain_ref, f32[2,16,128]{2,1,0:T(8,128)} %constant.4.clone.far_ref, f32[2,256,128]{2,1,0:T(8,128)} %constant.5.clone.near_ref, bf16[2,4096,128]{2,1,0:T(8,128)(2,1)} %bitcast.16, ...), custom_call_target="tpu_custom_call" | custom-call | flops 8589934592 | bytes 4194304 | tf_op jit(solution)/shard_map/attention1/pallas_call | solution.py:322
  428.2 148.9 %mlp1.1 = bf16[512,2048]{1,0:T(8,128)(2,1)} custom-call(f32[512,2048]{1,0:T(8,128)} %attention1.1.r_hbm, f32[1,2048]{1,0:T(1,128)} %get-tuple-element.5.gain_ref, bf16[2,1376,2048]{2,1,0:T(8,128)(2,1)} %bitcast.9, bf16[2,1376,2048]{2,1,0:T(8,128)(2,1)} %bitcast.11, bf16[2,1376,2048]{2,1,0:T(8,128)(2,1)} %wd_hbm.3), custom_call_target="tpu_custom_call" | custom-call | flops 69256347648 | bytes 16908288 | tf_op jit(solution)/shard_map/mlp1/pallas_call | solution.py:491
  577.1 3.2 copy.13

commit v4 on v3

--- a/solution.py
+++ b/solution.py
@@ -47,7 +47,7 @@
 
 
 class RowGather:
-    def __init__(self, xbuf, sx, sy, ag, fs, fr, partners, greeted=3):
+    def __init__(self, xbuf, sx, sy, ag, fs, fr, partners):
         mate, dev_x, dev_y = partners
         rows = xbuf.shape[2]
         half = rows // 2
@@ -56,7 +56,6 @@
         own = xbuf.at[0, 0]
         self.xbuf, self.ag, self.fs, self.fr, self.mate = xbuf, ag, fs, fr, mate
         self.halves = (h0, h1)
-        self.greeted = greeted
 
         def piece(k, sem, dev, first, size, window, slot):
             at = pl.ds(first, size)
@@ -73,7 +72,7 @@
 
     def start(self, norm_half):
         norm_half(0)
-        pl.semaphore_wait(pltpu.get_barrier_semaphore(), self.greeted)
+        pl.semaphore_wait(pltpu.get_barrier_semaphore(), 3)
         self.first[0].start()
         norm_half(1)
         self.first[1].start()
@@ -115,45 +114,54 @@
         dst[at, :] = (r * lax.rsqrt(mean_sq + EPS) * gain_ref[...]).astype(BF16)
 
 
-def attend(qkv_ref, block, bq, bk, heads, head_dim):
-    scale = math.log2(math.e) / math.sqrt(head_dim)
-    mask = lax.broadcasted_iota(jnp.int32, (bq, bq), 0) >= lax.broadcasted_iota(jnp.int32, (bq, bq), 1)
-    q_at = pl.ds(pl.multiple_of(block * bq, bq), bq)
-    qs = [qkv_ref[q_at, h * head_dim:(h + 1) * head_dim] for h in range(heads)]
-
-    def step(first, count, carry, masked):
-        at = pl.ds(pl.multiple_of(first, bq), count)
-        k_blk = qkv_ref[at, heads * head_dim:(heads + 1) * head_dim]
-        v_blk = qkv_ref[at, (heads + 1) * head_dim:(heads + 2) * head_dim]
-        out = []
-        for h in range(heads):
-            m, l, acc = carry[h]
-            s = lax.dot_general(qs[h], k_blk, (((1,), (1,)), ((), ())), preferred_element_type=F32)
-            if masked:
-                s = jnp.where(mask, s, -jnp.inf)
-            m_new = jnp.maximum(m, jnp.max(s, axis=-1, keepdims=True))
-            p = jnp.exp2((s - m_new) * scale)
-            alpha = jnp.exp2((m - m_new) * scale)
-            l = l * alpha + jnp.sum(p, axis=-1, keepdims=True)
-            acc = acc * alpha + jnp.dot(p.astype(BF16), v_blk, preferred_element_type=F32)
-            out.append((m_new, l, acc))
-        return tuple(out)
-
-    carry = tuple((jnp.full((bq, 1), -jnp.inf, F32), jnp.zeros((bq, 1), F32), jnp.zeros((bq, head_dim), F32)) for _ in range(heads))
-    carry = step(block * bq, bq, carry, True)
-    full = lax.div(block * bq, bk)
-    carry = lax.fori_loop(0, full, lambda j, cur: step(j * bk, bk, cur, False), carry)
-    carry = lax.fori_loop(full * (bk // bq), block, lambda j, cur: step(j * bq, bq, cur, False), carry)
-    return [(acc / l).astype(BF16) for _, l, acc in carry]
-
-
-def attn_kernel(layer, n_tp, n_kv, heads, head_dim, bk, r_hbm, gain_ref, far_ref, near_ref, wq_hbm, wkv_hbm, wo_hbm, out_hbm,
-                xbuf, rin, wq, wkv, wide, w_all, qkv_ref, wo, ctx, ctx_out, res,
-                lsem, sx, sy, ag, fs, fr, ox, oy, oz, oa, ob, om, on, cs, cr, es):
-    t, (yy, xx, c), partners = coords()
+class BlockGather:
+    def __init__(self, xbuf, sf, ag, fs, fr, mate, dev_f, dev_s):
+        rows = xbuf.shape[2]
+        half = rows // 2
+        self.halves = (pl.ds(0, half), pl.ds(half, half))
+        self.xbuf, self.ag, self.fs, self.fr, self.mate = xbuf, ag, fs, fr, mate
+
+        def copies(source, target, sem, dev):
+            return [rcopy(xbuf.at[source, 0, at], xbuf.at[target, 0, at], sf.at[sem + k], ag.at[target, k], dev)
+                    for k, at in enumerate(self.halves)]
+
+        self.first = copies(0, 1, 0, dev_f)
+        self.relay = copies(1, 2, 2, dev_s)
+        self.second = copies(0, 3, 4, dev_s)
+
+    def forward(self, w):
+        return rcopy(self.xbuf.at[w, 0], self.xbuf.at[w, 1], self.fs.at[w], self.fr.at[w], self.mate)
+
+    def arrive(self, w, between):
+        for k, at in enumerate(self.halves):
+            pltpu.make_async_copy(self.xbuf.at[0, 0, at], self.xbuf.at[w, 0, at], self.ag.at[w, k]).wait()
+
+            @pl.when(w == 1)
+            def _():
+                self.relay[k].start()
+        self.forward(w).start()
+
+        @pl.when(w == 1)
+        def _():
+            between()
+            for copy in self.second:
+                copy.start()
+
+    def finish(self):
+        for copy in self.first + self.relay + self.second:
+            copy.wait_send()
+        for w in range(4):
+            self.forward(w).wait_send()
+
+
+def attn_kernel(layer, n_tp, n_kv, heads, head_dim, r_hbm, gain_ref, far_ref, near_ref, wq_hbm, wkv_hbm, wo_hbm, out_hbm,
+                xbuf, rin, wq, wkv, wide, w_all, qkv_ref, wo, ctx, ctx_out, res, stat, total,
+                lsem, sf, ag, fs, fr, of, oz, oa, ob, om, on, cs, cr, es):
+    t, (yy, xx, c), (mate, dev_x, dev_y) = coords()
     z = lax.axis_index('dp')
-    mate, dev_x, dev_y = partners
     dev_d = dev_x + dev_y - t
+    dev_f = dev_x + c * (dev_y - dev_x)
+    dev_s = dev_y + c * (dev_x - dev_y)
     rows, width = res.shape
     half = rows // 2
     cols = heads * head_dim
@@ -164,16 +172,59 @@
     greet(others)
     pl.semaphore_signal(pltpu.get_barrier_semaphore(), inc=1, device_id={'dp': 1 - z, 'tp': t}, device_id_type=MESH)
     own_o = pl.ds(pl.multiple_of(t * cols, cols), cols)
-    loads = (pltpu.make_async_copy(wq_hbm.at[layer], wq, lsem.at[1]),
-             pltpu.make_async_copy(wkv_hbm.at[layer], wkv, lsem.at[2]),
-             pltpu.make_async_copy(wo_hbm.at[layer], wo.at[own_o], lsem.at[3]))
+    loads = (pltpu.make_async_copy(wo_hbm.at[layer], wo.at[own_o], lsem.at[3]),
+             pltpu.make_async_copy(wq_hbm.at[layer], wq, lsem.at[1]),
+             pltpu.make_async_copy(wkv_hbm.at[layer], wkv, lsem.at[2]))
     load_r.wait()
     for copy in loads:
         copy.start()
-    gather = RowGather(xbuf, sx, sy, ag, fs, fr, partners, n_tp)
-    gather.start(lambda k: norm_rows(rin, gain_ref, xbuf.at[0, 0], k * half, half))
+    gather = BlockGather(xbuf, sf, ag, fs, fr, mate, dev_f, dev_s)
+    norm_rows(rin, gain_ref, xbuf.at[0, 0], 0, half)
+    pl.semaphore_wait(pltpu.get_barrier_semaphore(), n_tp)
+    gather.first[0].start()
+    norm_rows(rin, gain_ref, xbuf.at[0, 0], half, half)
+    gather.first[1].start()
+    gather.forward(0).start()
+
+    part_rows = head_dim // 2
+
+    def span(dev, k, p):
+        return pl.ds(pl.multiple_of(dev * cols + k * head_dim + p * part_rows, part_rows), part_rows)
+
+    def same(at, ssem, rsem, dev):
+        return rcopy(wo.at[at], wo.at[at], ssem, rsem, dev)
+
+    def across(at, ssem, rsem):
+        return pltpu.make_async_remote_copy(src_ref=wo.at[at], dst_ref=wo.at[at], send_sem=ssem, recv_sem=rsem,
+                                            device_id={'dp': 1 - z, 'tp': t}, device_id_type=MESH)
+
+    from_dev = ((dev_f, 0), (dev_s, 1), (dev_f, 1), (dev_s, 0), (dev_d, 1), (dev_d, 0))
+    send = (same(span(t, 0, z), of.at[0], oa.at[0], dev_f), same(span(t, 1, z), of.at[1], oa.at[1], dev_s),
+            same(span(t, 1, z), of.at[2], oa.at[2], dev_f), same(span(t, 0, z), of.at[3], oa.at[3], dev_s))
+    relay = (same(span(dev_s, 1, z), of.at[4], oa.at[4], dev_f), same(span(dev_f, 0, z), of.at[5], oa.at[5], dev_s))
+    via_z = [across(span(dev, k, z), oz.at[i], ob.at[i]) for i, (dev, k) in enumerate(from_dev)]
+    to_mate = [same(span(dev, k, z), om.at[i], on.at[i], mate) for i, (dev, k) in enumerate(from_dev)]
+    to_mate += [same(span(dev, k, 1 - z), om.at[6 + i], on.at[6 + i], mate) for i, (dev, k) in enumerate(from_dev)]
+    to_mate.append(same(own_o, om.at[12], on.at[12], mate))
+
+    def take(i, sem, p):
+        at = span(from_dev[i][0], from_dev[i][1], p)
+        pltpu.make_async_copy(wo.at[at], wo.at[at], sem.at[i]).wait()
+
+    def pass_on(i):
+        take(i, oa, z)
+        via_z[i].start()
+        to_mate[i].start()
+
+    def from_z(i):
+        take(i, ob, 1 - z)
+        to_mate[6 + i].start()
+
     for copy in loads:
         copy.wait()
+    send[0].start()
+    send[2].start()
+    to_mate[12].start()
 
     kv_head = lax.div(t * n_kv, n_tp)
     nd = 256
@@ -188,30 +239,25 @@
         for h in range(2):
             w_all[to, (heads + h) * head_dim:(heads + h + 1) * head_dim] = wide[pl.ds(h * n_kv + kv_head, nd, stride=2 * n_kv), :].astype(BF16)
 
-    @pl.loop(0, 8)
-    def _(s):
-        w = lax.div(s, 2)
-        rc = lax.rem(s, 2)
-
-        @pl.when((rc == 0) & (w >= 1))
-        def _():
-            gather.arrive(w)
-
-        @pl.when(rc == 1)
-        def _():
-            gather.forward(w).wait_recv()
-        proj = jnp.dot(xbuf[w, rc], w_all[...], preferred_element_type=F32)
-        core = c + rc - 2 * c * rc
+    def block_of(i):
+        w = lax.div(i, 2)
+        j = lax.rem(i, 2)
+        core = c + j - 2 * c * j
         one = lax.rem(lax.div(w + 1, 2), 2)
         two = lax.div(w, 2)
+        flip_x = one + core * (two - one)
+        flip_y = two + core * (one - two)
+        return (2 * (yy + flip_y - 2 * yy * flip_y) + xx + flip_x - 2 * xx * flip_x) * 2 + core
+
+    def project(i):
+        block = block_of(i)
+        proj = jnp.dot(xbuf[lax.div(i, 2), lax.rem(i, 2)], w_all[...], preferred_element_type=F32)
+        cos_n, sin_n = near_ref[0], near_ref[1]
         for k in range(2):
-            flip_x, flip_y = (one, two) if k == 0 else (two, one)
-            chip = 2 * (yy + flip_y - 2 * yy * flip_y) + xx + flip_x - 2 * xx * flip_x
-            piece = (chip * 2 + core) * 2 + k
+            piece = block * 2 + k
             at = pl.ds(pl.multiple_of(piece * half, half), half)
             part = proj[k * half:(k + 1) * half]
             cos_f, sin_f = far_ref[0, pl.ds(piece, 1), :], far_ref[1, pl.ds(piece, 1), :]
-            cos_n, sin_n = near_ref[0], near_ref[1]
             cos_b = cos_f * cos_n - sin_f * sin_n
             sin_b = sin_f * cos_n + cos_f * sin_n
             for h in range(heads + 1):
@@ -220,75 +266,108 @@
                 qkv_ref[at, at_h] = (v * cos_b + pltpu.roll(v, head_dim // 2, 1) * sin_b).astype(BF16)
             at_h = slice((heads + 1) * head_dim, (heads + 2) * head_dim)
             qkv_ref[at, at_h] = part[:, at_h].astype(BF16)
-
-    part_rows = head_dim // 2
-
-    def span(dev, k, p):
-        return pl.ds(pl.multiple_of(dev * cols + k * head_dim + p * part_rows, part_rows), part_rows)
-
-    def same(at, ssem, rsem, dev):
-        return rcopy(wo.at[at], wo.at[at], ssem, rsem, dev)
-
-    def across(at, ssem, rsem):
-        return pltpu.make_async_remote_copy(src_ref=wo.at[at], dst_ref=wo.at[at], send_sem=ssem, recv_sem=rsem,
-                                            device_id={'dp': 1 - z, 'tp': t}, device_id_type=MESH)
-
-    send = (same(span(t, 0, z), ox.at[0], oa.at[0], dev_x), same(span(t, 1, z), oy.at[0], oa.at[1], dev_y),
-            same(span(t, 1, z), ox.at[1], oa.at[2], dev_x), same(span(t, 0, z), oy.at[1], oa.at[3], dev_y))
-    relay = (same(span(dev_y, 1, z), ox.at[2], oa.at[4], dev_x), same(span(dev_x, 0, z), oy.at[2], oa.at[5], dev_y))
-    from_dev = ((dev_x, 0), (dev_y, 1), (dev_x, 1), (dev_y, 0), (dev_d, 1), (dev_d, 0))
-    via_z = [across(span(dev, k, z), oz.at[i], ob.at[i]) for i, (dev, k) in enumerate(from_dev)]
-    to_mate = [same(span(dev, k, z), om.at[i], on.at[i], mate) for i, (dev, k) in enumerate(from_dev)]
-    to_mate += [same(span(dev, k, 1 - z), om.at[6 + i], on.at[6 + i], mate) for i, (dev, k) in enumerate(from_dev)]
-    to_mate.append(same(own_o, om.at[12], on.at[12], mate))
-
-    def take(i, sem, p):
-        at = span(from_dev[i][0], from_dev[i][1], p)
-        pltpu.make_async_copy(wo.at[at], wo.at[at], sem.at[i]).wait()
-
-    for copy in send:
-        copy.start()
-    to_mate[12].start()
+        stat[i] = jnp.where(lax.rem(lax.broadcasted_iota(jnp.int32, (rows, head_dim), 1), 2) == 0, -jnp.inf, 0.0)
+        total[i] = jnp.zeros((heads, rows, head_dim), F32)
+
+    scale = math.log2(math.e) / math.sqrt(head_dim)
+
+    def tile(i, q_block, k_block, masked):
+        q_at = pl.ds(pl.multiple_of(q_block * rows, rows), rows)
+        k_at = pl.ds(pl.multiple_of(k_block * rows, rows), rows)
+        k_blk = qkv_ref[k_at, heads * head_dim:(heads + 1) * head_dim]
+        v_blk = qkv_ref[k_at, (heads + 1) * head_dim:(heads + 2) * head_dim]
+        for h in range(heads):
+            s = lax.dot_general(qkv_ref[q_at, h * head_dim:(h + 1) * head_dim], k_blk, (((1,), (1,)), ((), ())), preferred_element_type=F32)
+            if masked:
+                s = jnp.where(lax.broadcasted_iota(jnp.int32, (rows, rows), 0) >= lax.broadcasted_iota(jnp.int32, (rows, rows), 1), s, -jnp.inf)
+            m = stat[i, :, 2 * h:2 * h + 1]
+            m_new = jnp.maximum(m, jnp.max(s, axis=-1, keepdims=True))
+            p = jnp.exp2((s - m_new) * scale)
+            alpha = jnp.exp2((m - m_new) * scale)
+            stat[i, :, 2 * h:2 * h + 1] = m_new
+            stat[i, :, 2 * h + 1:2 * h + 2] = stat[i, :, 2 * h + 1:2 * h + 2] * alpha + jnp.sum(p, axis=-1, keepdims=True)
+            total[i, h] = total[i, h] * alpha + jnp.dot(p.astype(BF16), v_blk, preferred_element_type=F32)
 
     def ctx_send(i, dev):
         return rcopy(ctx_out.at[i], ctx.at[:, own_o], cs.at[i], cr.at[t], dev)
 
-    @pl.loop(0, n_tp)
-    def _(i):
-        block = lax.rem(t + 1 + i, n_tp)
-
-        @pl.when(i == 3)
+    def second_sends():
+        send[1].start()
+        send[3].start()
+
+    @pl.loop(0, 4)
+    def _(w):
+        @pl.when(w >= 1)
+        def _():
+            gather.arrive(w, second_sends)
+
+        @pl.when(w == 2)
         def _():
             take(0, oa, z)
+            relay[1].start()
+            via_z[0].start()
+            to_mate[0].start()
+            pass_on(2)
+
+        @pl.when(w == 3)
+        def _():
             take(1, oa, z)
-            for copy in relay:
-                copy.start()
-            take(2, oa, z)
-            take(3, oa, z)
-            for k in range(4):
-                via_z[k].start()
-                to_mate[k].start()
-
-        @pl.when(i == 5)
-        def _():
-            for k in range(4, 6):
-                take(k, oa, z)
-                via_z[k].start()
-                to_mate[k].start()
-
-        @pl.when(i == 7)
-        def _():
-            for k in range(6):
-                take(k, ob, 1 - z)
-                to_mate[6 + k].start()
-        for h, val in enumerate(attend(qkv_ref, block, rows, bk, heads, head_dim)):
-            ctx_out[i, :, h * head_dim:(h + 1) * head_dim] = val
-
-        @pl.when(i < n_tp - 1)
-        def _():
-            ctx_send(i, block).start()
-
-    ctx[:, own_o] = ctx_out[n_tp - 1]
+            relay[0].start()
+            via_z[1].start()
+            to_mate[1].start()
+            pass_on(3)
+            from_z(0)
+            from_z(2)
+
+        @pl.loop(0, 2)
+        def _(j):
+            @pl.when(j == 1)
+            def _():
+                gather.forward(w).wait_recv()
+            project(2 * w + j)
+        count = 2 * w + 2
+
+        @pl.loop(0, count)
+        def _(n):
+            i = lax.rem(n + 1, count)
+            q_block = block_of(i)
+
+            @pl.when((w == 3) & (n == 3))
+            def _():
+                pass_on(4)
+                pass_on(5)
+
+            @pl.when((w == 3) & (n == 5))
+            def _():
+                from_z(1)
+                from_z(3)
+
+            def one_tile(k, _):
+                k_block = block_of(k)
+
+                @pl.when(k_block < q_block)
+                def _():
+                    tile(i, q_block, k_block, False)
+
+                @pl.when(k_block == q_block)
+                def _():
+                    tile(i, q_block, k_block, True)
+                return 0
+
+            lax.fori_loop(jnp.where(i >= 2 * w, 0, 2 * w), count, one_tile, 0)
+
+            @pl.when(w == 3)
+            def _():
+                for h in range(heads):
+                    ctx_out[i, :, h * head_dim:(h + 1) * head_dim] = (total[i, h] / stat[i, :, 2 * h + 1:2 * h + 2]).astype(BF16)
+
+                @pl.when(i >= 1)
+                def _():
+                    ctx_send(i, q_block).start()
+
+    from_z(4)
+    from_z(5)
+    ctx[:, own_o] = ctx_out[0]
     for copy in to_mate:
         copy.wait_recv()
     for dev in others:
@@ -304,13 +383,13 @@
     gather.finish()
     for copy in list(send + relay) + via_z + to_mate:
         copy.wait_send()
-    for i in range(n_tp - 1):
+    for i in range(1, n_tp):
         ctx_send(i, mate).wait_send()
     for copy in outs:
         copy.wait()
 
 
-def attention(layer, resid, gain, far, near, w_q, w_kv, w_o, n_tp, bk=1024):
+def attention(layer, resid, gain, far, near, w_q, w_kv, w_o, n_tp):
     rows, width = resid.shape
     cols, head_dim = w_o.shape[1], w_q.shape[2]
     heads = cols // head_dim
@@ -320,7 +399,7 @@
     anywhere = pl.BlockSpec(memory_space=pl.ANY)
     dma = pltpu.SemaphoreType.DMA
     return pl.pallas_call(
-        functools.partial(attn_kernel, layer, n_tp, n_kv, heads, head_dim, bk),
+        functools.partial(attn_kernel, layer, n_tp, n_kv, heads, head_dim),
         out_shape=jax.ShapeDtypeStruct((rows, width), F32),
         in_specs=[anywhere, vmem, vmem, vmem, anywhere, anywhere, anywhere],
         out_specs=anywhere,
@@ -336,8 +415,10 @@
             pltpu.VMEM((rows, n_tp * cols), BF16),
             pltpu.VMEM((n_tp, rows, cols), BF16),
             pltpu.VMEM((rows, width), F32),
-            dma((4,)),
-        ] + gather_sems() + [dma((3,)), dma((3,)), dma((6,)), dma((6,)), dma((6,)), dma((13,)), dma((13,)), dma((n_tp,)), dma((n_tp,)), dma((4,))],
+            pltpu.VMEM((n_tp, rows, head_dim), F32),
+            pltpu.VMEM((n_tp, heads, rows, head_dim), F32),
+            dma((4,)), dma((6,)), dma((4, 2)), dma((4,)), dma((4,)), dma((6,)), dma((6,)), dma((6,)), dma((6,)), dma((13,)), dma((13,)), dma((n_tp,)), dma((n_tp,)), dma((4,)),
+        ],
         compiler_params=pltpu.CompilerParams(collective_id=1 + layer, has_side_effects=True, vmem_limit_bytes=VMEM_MAX),
         cost_estimate=pl.CostEstimate(flops=2 * seq * seq * cols, bytes_accessed=4 * seq * cols, transcendentals=seq * seq),
         name="attention" + str(layer),

time: 581 us -> 600 us (1.033)
  Pallas kernels: 574 us -> 593 us
    pallas_call x2, Pallas kernels: 273 us -> 306 us  [attention(): pl.pallas_call(functools.partial(attn_kernel, layer, n_tp, n_kv, heads, h...]
    pallas_call x2, Pallas kernels: 301 us -> 286 us  [mlp(): pl.pallas_call(functools.partial(mlp_kernel, layer), out_shape=jax.ShapeD...]
where the time goes in v4:
time: 600 us; the launch traced here: 599 us
  Pallas kernels  593 us (99%)
    pallas_call x2, Pallas kernels, attention(): pl.pallas_call(functools.partial(attn_kernel, layer, n_tp, n_kv, heads, h...  306 us
    pallas_call x2, Pallas kernels, mlp(): pl.pallas_call(functools.partial(mlp_kernel, layer), out_shape=jax.ShapeD...  286 us

profile of v4, /device:TPU:0, one launch (start us, length us, event | category | flops | bytes accessed | tf_op | source)
XLA Modules:
  0.0 598.9 jit_solution(4898218635141277105)
XLA Ops:
  0.0 1.4 fusion.1
  1.4 1.4 fusion
  2.8 154.0 %attention0.1.r_hbm = f32[512,2048]{1,0:T(8,128)} custom-call(bf16[512,2048]{1,0:T(8,128)(2,1)} %bitcast.14, f32[1,2048]{1,0:T(1,128)} %get-tuple-element.8.gain_ref, f32[2,16,128]{2,1,0:T(8,128)} %constant.4.clone.far_ref, f32[2,256,128]{2,1,0:T(8,128)} %constant.5.clone.near_ref, bf16[2,4096,128]{2,1,0:T(8,128)(2,1)} %bitcast.15, ...), custom_call_target="tpu_custom_call" | custom-call | flops 8589934592 | bytes 4194304 | tf_op jit(solution)/shard_map/attention0/pallas_call | solution.py:401
  156.8 143.1 %mlp0.1.r_hbm = f32[512,2048]{1,0:T(8,128)} custom-call(f32[512,2048]{1,0:T(8,128)} %attention0.1.r_hbm, f32[1,2048]{1,0:T(1,128)} %get-tuple-element.6.gain_ref, bf16[2,1376,2048]{2,1,0:T(8,128)(2,1)} %bitcast.8, bf16[2,1376,2048]{2,1,0:T(8,128)(2,1)} %bitcast.10, bf16[2,1376,2048]{2,1,0:T(8,128)(2,1)} %wd_hbm.3), custom_call_target="tpu_custom_call" | custom-call | flops 69256347648 | bytes 16908288 | tf_op jit(solution)/shard_map/mlp0/pallas_call | solution.py:572
  300.0 152.4 %attention1.1.r_hbm = f32[512,2048]{1,0:T(8,128)} custom-call(f32[512,2048]{1,0:T(8,128)} %mlp0.1.r_hbm, f32[1,2048]{1,0:T(1,128)} %get-tuple-element.7.gain_ref, f32[2,16,128]{2,1,0:T(8,128)} %constant.4.clone.far_ref, f32[2,256,128]{2,1,0:T(8,128)} %constant.5.clone.near_ref, bf16[2,4096,128]{2,1,0:T(8,128)(2,1)} %bitcast.16, ...), custom_call_target="tpu_custom_call" | custom-call | flops 8589934592 | bytes 4194304 | tf_op jit(solution)/shard_map/attention1/pallas_call | solution.py:401
  452.4 143.3 %mlp1.1 = bf16[512,2048]{1,0:T(8,128)(2,1)} custom-call(f32[512,2048]{1,0:T(8,128)} %attention1.1.r_hbm, f32[1,2048]{1,0:T(1,128)} %get-tuple-element.5.gain_ref, bf16[2,1376,2048]{2,1,0:T(8,128)(2,1)} %bitcast.9, bf16[2,1376,2048]{2,1,0:T(8,128)(2,1)} %bitcast.11, bf16[2,1376,2048]{2,1,0:T(8,128)(2,1)} %wd_hbm.3), custom_call_target="tpu_custom_call" | custom-call | flops 69256347648 | bytes 16908288 | tf_op jit(solution)/shard_map/mlp1/pallas_call | solution.py:572
  595.7 3.2 copy.13

commit v5 on v4

--- a/solution.py
+++ b/solution.py
@@ -266,8 +266,8 @@
                 qkv_ref[at, at_h] = (v * cos_b + pltpu.roll(v, head_dim // 2, 1) * sin_b).astype(BF16)
             at_h = slice((heads + 1) * head_dim, (heads + 2) * head_dim)
             qkv_ref[at, at_h] = part[:, at_h].astype(BF16)
-        stat[i] = jnp.where(lax.rem(lax.broadcasted_iota(jnp.int32, (rows, head_dim), 1), 2) == 0, -jnp.inf, 0.0)
-        total[i] = jnp.zeros((heads, rows, head_dim), F32)
+        stat[i] = jnp.where(lax.rem(lax.broadcasted_iota(jnp.int32, (2 * heads, rows), 0), 2) == 0, -jnp.inf, 0.0)
+        total[i] = jnp.zeros((heads, head_dim, rows), F32)
 
     scale = math.log2(math.e) / math.sqrt(head_dim)
 
@@ -276,17 +276,22 @@
         k_at = pl.ds(pl.multiple_of(k_block * rows, rows), rows)
         k_blk = qkv_ref[k_at, heads * head_dim:(heads + 1) * head_dim]
         v_blk = qkv_ref[k_at, (heads + 1) * head_dim:(heads + 2) * head_dim]
+        qs = [qkv_ref[q_at, h * head_dim:(h + 1) * head_dim] for h in range(heads)]
+        old = [(stat[i, 2 * h:2 * h + 1, :], stat[i, 2 * h + 1:2 * h + 2, :], total[i, h]) for h in range(heads)]
+        out = []
         for h in range(heads):
-            s = lax.dot_general(qkv_ref[q_at, h * head_dim:(h + 1) * head_dim], k_blk, (((1,), (1,)), ((), ())), preferred_element_type=F32)
+            m, l, acc = old[h]
+            s = lax.dot_general(k_blk, qs[h], (((1,), (1,)), ((), ())), preferred_element_type=F32)
             if masked:
-                s = jnp.where(lax.broadcasted_iota(jnp.int32, (rows, rows), 0) >= lax.broadcasted_iota(jnp.int32, (rows, rows), 1), s, -jnp.inf)
-            m = stat[i, :, 2 * h:2 * h + 1]
-            m_new = jnp.maximum(m, jnp.max(s, axis=-1, keepdims=True))
+                s = jnp.where(lax.broadcasted_iota(jnp.int32, (rows, rows), 0) <= lax.broadcasted_iota(jnp.int32, (rows, rows), 1), s, -jnp.inf)
+            m_new = jnp.maximum(m, jnp.max(s, axis=0, keepdims=True))
             p = jnp.exp2((s - m_new) * scale)
             alpha = jnp.exp2((m - m_new) * scale)
-            stat[i, :, 2 * h:2 * h + 1] = m_new
-            stat[i, :, 2 * h + 1:2 * h + 2] = stat[i, :, 2 * h + 1:2 * h + 2] * alpha + jnp.sum(p, axis=-1, keepdims=True)
-            total[i, h] = total[i, h] * alpha + jnp.dot(p.astype(BF16), v_blk, preferred_element_type=F32)
+            l = l * alpha + jnp.sum(p, axis=0, keepdims=True)
+            acc = acc * alpha + lax.dot_general(v_blk, p.astype(BF16), (((0,), (0,)), ((), ())), preferred_element_type=F32)
+            out.append((m_new, l, acc))
+        for h in range(heads):
+            stat[i, 2 * h:2 * h + 1, :], stat[i, 2 * h + 1:2 * h + 2, :], total[i, h] = out[h]
 
     def ctx_send(i, dev):
         return rcopy(ctx_out.at[i], ctx.at[:, own_o], cs.at[i], cr.at[t], dev)
@@ -359,7 +364,7 @@
             @pl.when(w == 3)
             def _():
                 for h in range(heads):
-                    ctx_out[i, :, h * head_dim:(h + 1) * head_dim] = (total[i, h] / stat[i, :, 2 * h + 1:2 * h + 2]).astype(BF16)
+                    ctx_out[i, :, h * head_dim:(h + 1) * head_dim] = (total[i, h] / stat[i, 2 * h + 1:2 * h + 2, :]).T.astype(BF16)
 
                 @pl.when(i >= 1)
                 def _():
@@ -415,8 +420,8 @@
             pltpu.VMEM((rows, n_tp * cols), BF16),
             pltpu.VMEM((n_tp, rows, cols), BF16),
             pltpu.VMEM((rows, width), F32),
-            pltpu.VMEM((n_tp, rows, head_dim), F32),
-            pltpu.VMEM((n_tp, heads, rows, head_dim), F32),
+            pltpu.VMEM((n_tp, 2 * heads, rows), F32),
+            pltpu.VMEM((n_tp, heads, head_dim, rows), F32),
             dma((4,)), dma((6,)), dma((4, 2)), dma((4,)), dma((4,)), dma((6,)), dma((6,)), dma((6,)), dma((6,)), dma((13,)), dma((13,)), dma((n_tp,)), dma((n_tp,)), dma((4,)),
         ],
         compiler_params=pltpu.CompilerParams(collective_id=1 + layer, has_side_effects=True, vmem_limit_bytes=VMEM_MAX),

time: 600 us -> 545 us (0.908)
  Pallas kernels: 593 us -> 538 us
    pallas_call x2, Pallas kernels: 306 us -> 251 us  [attention(): pl.pallas_call(functools.partial(attn_kernel, layer, n_tp, n_kv, heads, h...]
where the time goes in v5:
time: 545 us; the launch traced here: 544 us
  Pallas kernels  538 us (99%)
  local copies, waits for them, and re-layouts  5.97 us (1%)
    pallas_call x2, Pallas kernels, mlp(): pl.pallas_call(functools.partial(mlp_kernel, layer), out_shape=jax.ShapeD...  287 us
    pallas_call x2, Pallas kernels, attention(): pl.pallas_call(functools.partial(attn_kernel, layer, n_tp, n_kv, heads, h...  251 us

profile of v5, /device:TPU:0, one launch (start us, length us, event | category | flops | bytes accessed | tf_op | source)
XLA Modules:
  0.0 544.4 jit_solution(13188586325463391439)
XLA Ops:
  0.0 1.4 fusion.1
  1.4 1.4 fusion
  2.8 127.0 %attention0.1.r_hbm = f32[512,2048]{1,0:T(8,128)} custom-call(bf16[512,2048]{1,0:T(8,128)(2,1)} %bitcast.14, f32[1,2048]{1,0:T(1,128)} %get-tuple-element.8.gain_ref, f32[2,16,128]{2,1,0:T(8,128)} %constant.4.clone.far_ref, f32[2,256,128]{2,1,0:T(8,128)} %constant.5.clone.near_ref, bf16[2,4096,128]{2,1,0:T(8,128)(2,1)} %bitcast.15, ...), custom_call_target="tpu_custom_call" | custom-call | flops 8589934592 | bytes 4194304 | tf_op jit(solution)/shard_map/attention0/pallas_call | solution.py:406
  129.8 143.7 %mlp0.1.r_hbm = f32[512,2048]{1,0:T(8,128)} custom-call(f32[512,2048]{1,0:T(8,128)} %attention0.1.r_hbm, f32[1,2048]{1,0:T(1,128)} %get-tuple-element.6.gain_ref, bf16[2,1376,2048]{2,1,0:T(8,128)(2,1)} %bitcast.8, bf16[2,1376,2048]{2,1,0:T(8,128)(2,1)} %bitcast.10, bf16[2,1376,2048]{2,1,0:T(8,128)(2,1)} %wd_hbm.3), custom_call_target="tpu_custom_call" | custom-call | flops 69256347648 | bytes 16908288 | tf_op jit(solution)/shard_map/mlp0/pallas_call | solution.py:577
  273.6 124.5 %attention1.1.r_hbm = f32[512,2048]{1,0:T(8,128)} custom-call(f32[512,2048]{1,0:T(8,128)} %mlp0.1.r_hbm, f32[1,2048]{1,0:T(1,128)} %get-tuple-element.7.gain_ref, f32[2,16,128]{2,1,0:T(8,128)} %constant.4.clone.far_ref, f32[2,256,128]{2,1,0:T(8,128)} %constant.5.clone.near_ref, bf16[2,4096,128]{2,1,0:T(8,128)(2,1)} %bitcast.16, ...), custom_call_target="tpu_custom_call" | custom-call | flops 8589934592 | bytes 4194304 | tf_op jit(solution)/shard_map/attention1/pallas_call | solution.py:406
  398.1 143.2 %mlp1.1 = bf16[512,2048]{1,0:T(8,128)(2,1)} custom-call(f32[512,2048]{1,0:T(8,128)} %attention1.1.r_hbm, f32[1,2048]{1,0:T(1,128)} %get-tuple-element.5.gain_ref, bf16[2,1376,2048]{2,1,0:T(8,128)(2,1)} %bitcast.9, bf16[2,1376,2048]{2,1,0:T(8,128)(2,1)} %bitcast.11, bf16[2,1376,2048]{2,1,0:T(8,128)(2,1)} %wd_hbm.3), custom_call_target="tpu_custom_call" | custom-call | flops 69256347648 | bytes 16908288 | tf_op jit(solution)/shard_map/mlp1/pallas_call | solution.py:577
  541.3 3.2 copy.13

commit v6 on v3

--- a/solution.py
+++ b/solution.py
@@ -47,7 +47,7 @@
 
 
 class RowGather:
-    def __init__(self, xbuf, sx, sy, ag, fs, fr, partners, greeted=3):
+    def __init__(self, xbuf, sx, sy, ag, fs, fr, partners):
         mate, dev_x, dev_y = partners
         rows = xbuf.shape[2]
         half = rows // 2
@@ -56,7 +56,6 @@
         own = xbuf.at[0, 0]
         self.xbuf, self.ag, self.fs, self.fr, self.mate = xbuf, ag, fs, fr, mate
         self.halves = (h0, h1)
-        self.greeted = greeted
 
         def piece(k, sem, dev, first, size, window, slot):
             at = pl.ds(first, size)
@@ -73,7 +72,7 @@
 
     def start(self, norm_half):
         norm_half(0)
-        pl.semaphore_wait(pltpu.get_barrier_semaphore(), self.greeted)
+        pl.semaphore_wait(pltpu.get_barrier_semaphore(), 3)
         self.first[0].start()
         norm_half(1)
         self.first[1].start()
@@ -104,7 +103,7 @@
     return [dma((4,)), dma((4,)), dma((4, 2)), dma((4,)), dma((4,))]
 
 
-def norm_rows(src, gain_ref, dst, first, count):
+def norm_rows(src, gain, dst, first, count):
     nb = 64
 
     @pl.loop(0, count // nb)
@@ -112,7 +111,70 @@
         at = pl.ds(pl.multiple_of(first + b * nb, nb), nb)
         r = src[at, :].astype(F32)
         mean_sq = jnp.mean(r * r, axis=-1, keepdims=True)
-        dst[at, :] = (r * lax.rsqrt(mean_sq + EPS) * gain_ref[...]).astype(BF16)
+        dst[at, :] = (r * lax.rsqrt(mean_sq + EPS) * gain).astype(BF16)
+
+
+class WeightGather:
+    def __init__(self, buf, unit, sems, t, z, mate, dev_f, dev_s, dev_d):
+        so, sz, oa, ob, om, on = sems
+        part = unit // 4
+        self.buf, self.oa, self.ob, self.z = buf, oa, ob, z
+        self.from_dev = ((dev_f, 0), (dev_s, 1), (dev_f, 1), (dev_s, 0), (dev_d, 1), (dev_d, 0))
+
+        def span(dev, k, p):
+            return pl.ds(pl.multiple_of(dev * unit + (2 * k + p) * part, part), part)
+
+        def same(at, ssem, rsem, dev):
+            return rcopy(buf.at[at], buf.at[at], ssem, rsem, dev)
+
+        def across(at, ssem, rsem):
+            return pltpu.make_async_remote_copy(src_ref=buf.at[at], dst_ref=buf.at[at], send_sem=ssem, recv_sem=rsem,
+                                                device_id={'dp': 1 - z, 'tp': t}, device_id_type=MESH)
+
+        self.span = span
+        self.send = (same(span(t, 0, z), so.at[0], oa.at[0], dev_f), same(span(t, 1, z), so.at[1], oa.at[1], dev_s),
+                     same(span(t, 1, z), so.at[2], oa.at[2], dev_f), same(span(t, 0, z), so.at[3], oa.at[3], dev_s))
+        self.relay = (same(span(dev_s, 1, z), so.at[4], oa.at[4], dev_f), same(span(dev_f, 0, z), so.at[5], oa.at[5], dev_s))
+        self.via_z = [across(span(dev, k, z), sz.at[i], ob.at[i]) for i, (dev, k) in enumerate(self.from_dev)]
+        self.to_mate = [same(span(dev, k, z), om.at[i], on.at[i], mate) for i, (dev, k) in enumerate(self.from_dev)]
+        self.to_mate += [same(span(dev, k, 1 - z), om.at[6 + i], on.at[6 + i], mate) for i, (dev, k) in enumerate(self.from_dev)]
+        own = pl.ds(pl.multiple_of(t * unit, unit), unit)
+        self.to_mate.append(same(own, om.at[12], on.at[12], mate))
+
+    def take(self, i, sem, p):
+        at = self.span(self.from_dev[i][0], self.from_dev[i][1], p)
+        pltpu.make_async_copy(self.buf.at[at], self.buf.at[at], sem.at[i]).wait()
+
+    def start(self):
+        for copy in self.send:
+            copy.start()
+        self.to_mate[12].start()
+
+    def received(self, pieces):
+        for i in pieces:
+            self.take(i, self.oa, self.z)
+            if i < 2:
+                self.relay[1 - i].start()
+            self.via_z[i].start()
+            self.to_mate[i].start()
+
+    def from_z(self, pieces):
+        for i in pieces:
+            self.take(i, self.ob, 1 - self.z)
+            self.to_mate[6 + i].start()
+
+    def from_mate(self, pieces):
+        for i in pieces:
+            self.to_mate[i].wait_recv()
+
+    def finish(self):
+        for copy in list(self.send + self.relay) + self.via_z + self.to_mate:
+            copy.wait_send()
+
+
+def weight_sems():
+    dma = pltpu.SemaphoreType.DMA
+    return [dma((6,)), dma((6,)), dma((6,)), dma((6,)), dma((13,)), dma((13,))]
 
 
 def attend(qkv_ref, block, bq, bk, heads, head_dim):
@@ -148,163 +210,200 @@
 
 
 def attn_kernel(layer, n_tp, n_kv, heads, head_dim, bk, r_hbm, gain_ref, far_ref, near_ref, wq_hbm, wkv_hbm, wo_hbm, out_hbm,
-                xbuf, rin, wq, wkv, wide, w_all, qkv_ref, wo, ctx, ctx_out, res,
-                lsem, sx, sy, ag, fs, fr, ox, oy, oz, oa, ob, om, on, cs, cr, es):
-    t, (yy, xx, c), partners = coords()
+                x, rin, wq, wkv, wide, w_kv, w_q, rope, kv_out, q_out, qkv_ref, wo, ctx, ctx_out, res,
+                lsem, ks, kr, km, kn, qs, qr, cs, cr, es, *gather_sem):
+    t, (yy, xx, c), (mate, dev_x, dev_y) = coords()
     z = lax.axis_index('dp')
-    mate, dev_x, dev_y = partners
     dev_d = dev_x + dev_y - t
+    dev_f = dev_x + c * (dev_y - dev_x)
+    dev_s = dev_y + c * (dev_x - dev_y)
     rows, width = res.shape
     half = rows // 2
     cols = heads * head_dim
 
     load_r = pltpu.make_async_copy(r_hbm, rin, lsem.at[0])
+    load_q = pltpu.make_async_copy(wq_hbm.at[layer], wq, lsem.at[1])
     load_r.start()
+    load_q.start()
     others = [lax.rem(t + k, n_tp) for k in range(1, n_tp)]
     greet(others)
     pl.semaphore_signal(pltpu.get_barrier_semaphore(), inc=1, device_id={'dp': 1 - z, 'tp': t}, device_id_type=MESH)
     own_o = pl.ds(pl.multiple_of(t * cols, cols), cols)
-    loads = (pltpu.make_async_copy(wq_hbm.at[layer], wq, lsem.at[1]),
-             pltpu.make_async_copy(wkv_hbm.at[layer], wkv, lsem.at[2]),
-             pltpu.make_async_copy(wo_hbm.at[layer], wo.at[own_o], lsem.at[3]))
+    load_kv = pltpu.make_async_copy(wkv_hbm.at[layer], wkv, lsem.at[2])
+    load_o = pltpu.make_async_copy(wo_hbm.at[layer], wo.at[own_o], lsem.at[3])
+    load_kv.start()
+    load_o.start()
+    place = (t, z, mate, dev_f, dev_s, dev_d)
+    get_q = WeightGather(w_q, width, gather_sem[:6], *place)
+    get_o = WeightGather(wo, cols, gather_sem[6:], *place)
+    nd = 256
+
+    def deinterleave(raw, count, dst, first):
+        @pl.loop(0, width // nd)
+        def _(b):
+            wide[pl.ds(0, count * nd), :] = raw[pl.ds(pl.multiple_of(b * count * nd, nd), count * nd), :].astype(F32)
+            for h in range(count):
+                dst[pl.ds(pl.multiple_of(first + b * nd, nd), nd), h * head_dim:(h + 1) * head_dim] = wide[pl.ds(h, nd, stride=count), :].astype(BF16)
+
+    load_q.wait()
+    deinterleave(wq, heads, w_q, t * width)
+    pl.semaphore_wait(pltpu.get_barrier_semaphore(), n_tp)
+    get_q.start()
+
     load_r.wait()
-    for copy in loads:
+    norm_rows(rin, gain_ref[layer:layer + 1], x, 0, rows)
+    for k in range(2):
+        at = slice(k * half, (k + 1) * half)
+        cos_f, sin_f = far_ref[0, pl.ds(t * 2 + k, 1), :], far_ref[1, pl.ds(t * 2 + k, 1), :]
+        rope[0, at] = cos_f * near_ref[0] - sin_f * near_ref[1]
+        rope[1, at] = sin_f * near_ref[0] + cos_f * near_ref[1]
+
+    def rotate(v):
+        return (v * rope[0] + pltpu.roll(v, head_dim // 2, 1) * rope[1]).astype(BF16)
+
+    own = pl.ds(pl.multiple_of(t * rows, rows), rows)
+    kv_cols = pl.ds(cols, 2 * head_dim)
+    q_cols = pl.ds(0, cols)
+    load_kv.wait()
+    deinterleave(wkv, 2 * n_kv, w_kv, 0)
+    for g in range(n_kv):
+        proj = jnp.dot(x[...], w_kv[:, g * head_dim:(g + 1) * head_dim], preferred_element_type=F32)
+        kv_out[g, :, 0:head_dim] = rotate(proj)
+        proj = jnp.dot(x[...], w_kv[:, (n_kv + g) * head_dim:(n_kv + g + 1) * head_dim], preferred_element_type=F32)
+        kv_out[g, :, head_dim:2 * head_dim] = proj.astype(BF16)
+
+    def kv_send(k, dev):
+        return rcopy(kv_out.at[lax.div(dev * n_kv, n_tp)], qkv_ref.at[own, kv_cols], ks.at[k], kr.at[k], dev)
+
+    def kv_mate(k, dev):
+        at = pl.ds(pl.multiple_of(dev * rows, rows), rows)
+        return rcopy(qkv_ref.at[at, kv_cols], qkv_ref.at[at, kv_cols], km.at[k], kn.at[k], mate)
+
+    near = (dev_x, dev_y, dev_d)
+    sends = [kv_send(k, dev) for k, dev in enumerate(near)]
+    for copy in sends:
         copy.start()
-    gather = RowGather(xbuf, sx, sy, ag, fs, fr, partners, n_tp)
-    gather.start(lambda k: norm_rows(rin, gain_ref, xbuf.at[0, 0], k * half, half))
-    for copy in loads:
-        copy.wait()
-
-    kv_head = lax.div(t * n_kv, n_tp)
-    nd = 256
-
-    @pl.loop(0, width // nd)
-    def _(b):
-        to = pl.ds(pl.multiple_of(b * nd, nd), nd)
-        wide[pl.ds(0, heads * nd), :] = wq[pl.ds(pl.multiple_of(b * heads * nd, nd), heads * nd), :].astype(F32)
-        for h in range(heads):
-            w_all[to, h * head_dim:(h + 1) * head_dim] = wide[pl.ds(h, nd, stride=heads), :].astype(BF16)
-        wide[pl.ds(0, 2 * n_kv * nd), :] = wkv[pl.ds(pl.multiple_of(b * 2 * n_kv * nd, nd), 2 * n_kv * nd), :].astype(F32)
-        for h in range(2):
-            w_all[to, (heads + h) * head_dim:(heads + h + 1) * head_dim] = wide[pl.ds(h * n_kv + kv_head, nd, stride=2 * n_kv), :].astype(BF16)
-
-    @pl.loop(0, 8)
-    def _(s):
-        w = lax.div(s, 2)
-        rc = lax.rem(s, 2)
-
-        @pl.when((rc == 0) & (w >= 1))
-        def _():
-            gather.arrive(w)
-
-        @pl.when(rc == 1)
-        def _():
-            gather.forward(w).wait_recv()
-        proj = jnp.dot(xbuf[w, rc], w_all[...], preferred_element_type=F32)
-        core = c + rc - 2 * c * rc
+    qkv_ref[own, kv_cols] = kv_out[lax.div(t * n_kv, n_tp)]
+    hand_on = [kv_mate(k, dev) for k, dev in enumerate(near)] + [
+        rcopy(kv_out.at[lax.div(t * n_kv, n_tp)], qkv_ref.at[own, kv_cols], km.at[3], kn.at[3], mate)]
+    hand_on[3].start()
+
+    def block_of(i):
+        w = lax.div(i, 2)
+        j = lax.rem(i, 2)
+        core = c + j - 2 * c * j
         one = lax.rem(lax.div(w + 1, 2), 2)
         two = lax.div(w, 2)
-        for k in range(2):
-            flip_x, flip_y = (one, two) if k == 0 else (two, one)
-            chip = 2 * (yy + flip_y - 2 * yy * flip_y) + xx + flip_x - 2 * xx * flip_x
-            piece = (chip * 2 + core) * 2 + k
-            at = pl.ds(pl.multiple_of(piece * half, half), half)
-            part = proj[k * half:(k + 1) * half]
-            cos_f, sin_f = far_ref[0, pl.ds(piece, 1), :], far_ref[1, pl.ds(piece, 1), :]
-            cos_n, sin_n = near_ref[0], near_ref[1]
-            cos_b = cos_f * cos_n - sin_f * sin_n
-            sin_b = sin_f * cos_n + cos_f * sin_n
-            for h in range(heads + 1):
-                at_h = slice(h * head_dim, (h + 1) * head_dim)
-                v = part[:, at_h]
-                qkv_ref[at, at_h] = (v * cos_b + pltpu.roll(v, head_dim // 2, 1) * sin_b).astype(BF16)
-            at_h = slice((heads + 1) * head_dim, (heads + 2) * head_dim)
-            qkv_ref[at, at_h] = part[:, at_h].astype(BF16)
-
-    part_rows = head_dim // 2
-
-    def span(dev, k, p):
-        return pl.ds(pl.multiple_of(dev * cols + k * head_dim + p * part_rows, part_rows), part_rows)
-
-    def same(at, ssem, rsem, dev):
-        return rcopy(wo.at[at], wo.at[at], ssem, rsem, dev)
-
-    def across(at, ssem, rsem):
-        return pltpu.make_async_remote_copy(src_ref=wo.at[at], dst_ref=wo.at[at], send_sem=ssem, recv_sem=rsem,
-                                            device_id={'dp': 1 - z, 'tp': t}, device_id_type=MESH)
-
-    send = (same(span(t, 0, z), ox.at[0], oa.at[0], dev_x), same(span(t, 1, z), oy.at[0], oa.at[1], dev_y),
-            same(span(t, 1, z), ox.at[1], oa.at[2], dev_x), same(span(t, 0, z), oy.at[1], oa.at[3], dev_y))
-    relay = (same(span(dev_y, 1, z), ox.at[2], oa.at[4], dev_x), same(span(dev_x, 0, z), oy.at[2], oa.at[5], dev_y))
-    from_dev = ((dev_x, 0), (dev_y, 1), (dev_x, 1), (dev_y, 0), (dev_d, 1), (dev_d, 0))
-    via_z = [across(span(dev, k, z), oz.at[i], ob.at[i]) for i, (dev, k) in enumerate(from_dev)]
-    to_mate = [same(span(dev, k, z), om.at[i], on.at[i], mate) for i, (dev, k) in enumerate(from_dev)]
-    to_mate += [same(span(dev, k, 1 - z), om.at[6 + i], on.at[6 + i], mate) for i, (dev, k) in enumerate(from_dev)]
-    to_mate.append(same(own_o, om.at[12], on.at[12], mate))
-
-    def take(i, sem, p):
-        at = span(from_dev[i][0], from_dev[i][1], p)
-        pltpu.make_async_copy(wo.at[at], wo.at[at], sem.at[i]).wait()
-
-    for copy in send:
-        copy.start()
-    to_mate[12].start()
+        flip_x = one + core * (two - one)
+        flip_y = two + core * (one - two)
+        return (2 * (yy + flip_y - 2 * yy * flip_y) + xx + flip_x - 2 * xx * flip_x) * 2 + core
+
+    def project(i):
+        dev = block_of(i)
+        proj = jnp.dot(x[...], w_q[pl.ds(pl.multiple_of(dev * width, width), width), :], preferred_element_type=F32)
+        for h in range(heads):
+            at_h = slice(h * head_dim, (h + 1) * head_dim)
+            q_out[i, :, at_h] = rotate(proj[:, at_h])
+
+    def q_send(i):
+        return rcopy(q_out.at[i], qkv_ref.at[own, q_cols], qs.at[i], qr.at[t], block_of(i))
+
+    def project_all(first, last):
+        @pl.loop(first, last)
+        def _(i):
+            project(i)
+
+            @pl.when(i >= 1)
+            def _():
+                q_send(i).start()
+
+    get_q.from_mate([12])
+    project_all(0, 2)
+    qkv_ref[own, q_cols] = q_out[0]
+    get_q.received(range(4))
+    for k in range(3):
+        pltpu.make_async_copy(kv_out.at[0], qkv_ref.at[pl.ds(pl.multiple_of(near[k] * rows, rows), rows), kv_cols], kr.at[k]).wait()
+        hand_on[k].start()
+    for copy in hand_on:
+        copy.wait_recv()
 
     def ctx_send(i, dev):
-        return rcopy(ctx_out.at[i], ctx.at[:, own_o], cs.at[i], cr.at[t], dev)
+        return rcopy(ctx_out.at[i], ctx.at[t], cs.at[i], cr.at[t], dev)
+
+    load_o.wait()
 
     @pl.loop(0, n_tp)
-    def _(i):
-        block = lax.rem(t + 1 + i, n_tp)
-
-        @pl.when(i == 3)
-        def _():
-            take(0, oa, z)
-            take(1, oa, z)
-            for copy in relay:
-                copy.start()
-            take(2, oa, z)
-            take(3, oa, z)
-            for k in range(4):
-                via_z[k].start()
-                to_mate[k].start()
-
-        @pl.when(i == 5)
-        def _():
-            for k in range(4, 6):
-                take(k, oa, z)
-                via_z[k].start()
-                to_mate[k].start()
-
-        @pl.when(i == 7)
-        def _():
-            for k in range(6):
-                take(k, ob, 1 - z)
-                to_mate[6 + k].start()
+    def _(n):
+        i = n + jnp.where(n < 4, 0, jnp.where(n < 6, 2, -2))
+        block = block_of(i)
+
+        @pl.when(n == 0)
+        def _():
+            get_o.start()
+
+        @pl.when(n == 1)
+        def _():
+            get_q.received((4, 5))
+
+        @pl.when(n == 2)
+        def _():
+            get_q.from_z(range(4))
+            get_q.from_mate((0, 1, 2, 3, 6, 7, 8, 9))
+            project_all(2, 4)
+            project_all(6, 8)
+            get_o.received(range(4))
+
+        @pl.when(n == 4)
+        def _():
+            get_q.from_z((4, 5))
+            get_q.from_mate((4, 5, 10, 11))
+            project_all(4, 6)
+            get_o.received((4, 5))
+
+        @pl.when(n == 7)
+        def _():
+            get_o.from_z(range(4))
+
+        @pl.when(n >= 1)
+        def _():
+            pltpu.make_async_copy(q_out.at[0], qkv_ref.at[pl.ds(pl.multiple_of(block * rows, rows), rows), q_cols], qr.at[block]).wait()
         for h, val in enumerate(attend(qkv_ref, block, rows, bk, heads, head_dim)):
             ctx_out[i, :, h * head_dim:(h + 1) * head_dim] = val
 
-        @pl.when(i < n_tp - 1)
+        @pl.when(n >= 1)
         def _():
             ctx_send(i, block).start()
 
-    ctx[:, own_o] = ctx_out[n_tp - 1]
-    for copy in to_mate:
-        copy.wait_recv()
-    for dev in others:
-        at = pl.ds(pl.multiple_of(dev * cols, cols), cols)
-        pltpu.make_async_copy(ctx_out.at[0], ctx.at[:, at], cr.at[dev]).wait()
+    get_o.from_z((4, 5))
+    get_o.from_mate(range(13))
     nc = 512
+    chunks = [pl.ds(n * nc, nc) for n in range(width // nc)]
+    for at in chunks:
+        res[:, at] = rin[:, at].astype(F32) + jnp.dot(ctx_out[0], wo[own_o, at], preferred_element_type=F32)
+
+    def from_sender(n):
+        dev = block_of(n + jnp.where(n < 4, 0, jnp.where(n < 6, 2, -2)))
+        pltpu.make_async_copy(ctx_out.at[0], ctx.at[dev], cr.at[dev]).wait()
+        return dev, pl.ds(pl.multiple_of(dev * cols, cols), cols)
+
+    @pl.loop(1, n_tp - 1)
+    def _(n):
+        dev, rows_o = from_sender(n)
+        for at in chunks:
+            res[:, at] = res[:, at] + jnp.dot(ctx[dev], wo[rows_o, at], preferred_element_type=F32)
+
+    dev, rows_o = from_sender(jnp.int32(n_tp - 1))
     outs = []
-    for n in range(width // nc):
-        at = pl.ds(n * nc, nc)
-        res[:, at] = rin[:, at].astype(F32) + jnp.dot(ctx[...], wo[:, at], preferred_element_type=F32)
+    for n, at in enumerate(chunks):
+        res[:, at] = res[:, at] + jnp.dot(ctx[dev], wo[rows_o, at], preferred_element_type=F32)
         outs.append(pltpu.make_async_copy(res.at[:, at], out_hbm.at[:, at], es.at[n]))
         outs[n].start()
-    gather.finish()
-    for copy in list(send + relay) + via_z + to_mate:
+    get_q.finish()
+    get_o.finish()
+    for copy in sends + hand_on:
         copy.wait_send()
-    for i in range(n_tp - 1):
+    for i in range(1, n_tp):
+        q_send(jnp.int32(i)).wait_send()
         ctx_send(i, mate).wait_send()
     for copy in outs:
         copy.wait()
@@ -325,19 +424,23 @@
         in_specs=[anywhere, vmem, vmem, vmem, anywhere, anywhere, anywhere],
         out_specs=anywhere,
         scratch_shapes=[
-            pltpu.VMEM((4, 2, rows, width), BF16),
+            pltpu.VMEM((rows, width), BF16),
             pltpu.VMEM((rows, width), resid.dtype),
             pltpu.VMEM(w_q.shape[1:], BF16),
             pltpu.VMEM(w_kv.shape[1:], BF16),
             pltpu.VMEM((256 * max(heads, 2 * n_kv), head_dim), F32),
-            pltpu.VMEM((width, cols + 2 * head_dim), BF16),
+            pltpu.VMEM((width, 2 * n_kv * head_dim), BF16),
+            pltpu.VMEM((n_tp * width, cols), BF16),
+            pltpu.VMEM((2, rows, head_dim), F32),
+            pltpu.VMEM((n_kv, rows, 2 * head_dim), BF16),
+            pltpu.VMEM((n_tp, rows, cols), BF16),
             pltpu.VMEM((seq, cols + 2 * head_dim), BF16),
             pltpu.VMEM((n_tp * cols, width), BF16),
-            pltpu.VMEM((rows, n_tp * cols), BF16),
+            pltpu.VMEM((n_tp, rows, cols), BF16),
             pltpu.VMEM((n_tp, rows, cols), BF16),
             pltpu.VMEM((rows, width), F32),
-            dma((4,)),
-        ] + gather_sems() + [dma((3,)), dma((3,)), dma((6,)), dma((6,)), dma((6,)), dma((13,)), dma((13,)), dma((n_tp,)), dma((n_tp,)), dma((4,))],
+            dma((4,)), dma((3,)), dma((3,)), dma((4,)), dma((4,)), dma((n_tp,)), dma((n_tp,)), dma((n_tp,)), dma((n_tp,)), dma((4,)),
+        ] + weight_sems() + weight_sems(),
         compiler_params=pltpu.CompilerParams(collective_id=1 + layer, has_side_effects=True, vmem_limit_bytes=VMEM_MAX),
         cost_estimate=pl.CostEstimate(flops=2 * seq * seq * cols, bytes_accessed=4 * seq * cols, transcendentals=seq * seq),
         name="attention" + str(layer),
@@ -364,7 +467,7 @@
     for copy in loads:
         copy.start()
     gather = RowGather(xbuf, sx, sy, ag, fs, fr, partners)
-    gather.start(lambda k: norm_rows(acc, gain_ref, xbuf.at[0, 0], k * half, half))
+    gather.start(lambda k: norm_rows(acc, gain_ref[layer:layer + 1], xbuf.at[0, 0], k * half, half))
 
     def partial_send(w):
         return rcopy(xbuf.at[w, 1], prec.at[w], ps.at[w], pr.at[w], mate)
@@ -528,8 +631,8 @@
         w_up = jnp.swapaxes(w_up, 1, 2)
         resid = hidden[0]
         for layer in range(n_layers):
-            resid = attention(layer, resid, norm_attn[layer][None], far, near, w_q, w_kv, w_o, n_tp)
-            resid = mlp(layer, resid, norm_mlp[layer][None], w_gate, w_up, w_down, BF16 if layer == n_layers - 1 else F32)
+            resid = attention(layer, resid, norm_attn, far, near, w_q, w_kv, w_o, n_tp)
+            resid = mlp(layer, resid, norm_mlp, w_gate, w_up, w_down, BF16 if layer == n_layers - 1 else F32)
         return resid[None]
 
     return jax.shard_map(body, mesh=mesh, in_specs=in_specs, out_specs=tok_spec, check_vma=False)

time: 581 us -> 517 us (0.89); the launches traced: 580 us -> 508 us
  Pallas kernels: 574 us -> 505 us
    pallas_call x2, Pallas kernels: 273 us -> 213 us  [attention(): pl.pallas_call(functools.partial(attn_kernel, layer, n_tp, n_kv, heads, h...]
    pallas_call x2, Pallas kernels: 301 us -> 292 us  [mlp(): pl.pallas_call(functools.partial(mlp_kernel, layer), out_shape=jax.ShapeD...]
where the time goes in v6:
time: 517 us; the launch traced here: 508 us
  Pallas kernels  505 us (98%)
    pallas_call x2, Pallas kernels, mlp(): pl.pallas_call(functools.partial(mlp_kernel, layer), out_shape=jax.ShapeD...  292 us
    pallas_call x2, Pallas kernels, attention(): pl.pallas_call(functools.partial(attn_kernel, layer, n_tp, n_kv, heads, h...  213 us

profile of v6, /device:TPU:0, one launch (start us, length us, event | category | flops | bytes accessed | tf_op | source)
XLA Modules:
  0.0 508.3 jit_solution(1145189248108824999)
XLA Ops:
  0.0 107.0 %attention0.1.r_hbm = f32[512,2048]{1,0:T(8,128)} custom-call(bf16[512,2048]{1,0:T(8,128)(2,1)} %bitcast.14, f32[2,2048]{1,0:T(2,128)} %gain_ref.6, f32[2,16,128]{2,1,0:T(8,128)} %constant.4.clone.far_ref, f32[2,256,128]{2,1,0:T(8,128)} %constant.5.clone.near_ref, bf16[2,4096,128]{2,1,0:T(8,128)(2,1)} %bitcast.15, bf16[2,8192,128]{2,1,0:T(8,128)(2,1)} %bitcast.12, ...), custom_call_target="tpu_custom_call" | custom-call | flops 8589934592 | bytes 4194304 | tf_op jit(solution)/shard_map/attention0/pallas_call | solution.py:421
  107.0 145.8 %mlp0.1.r_hbm = f32[512,2048]{1,0:T(8,128)} custom-call(f32[512,2048]{1,0:T(8,128)} %attention0.1.r_hbm, f32[2,2048]{1,0:T(2,128)} %gain_ref.7, bf16[2,1376,2048]{2,1,0:T(8,128)(2,1)} %bitcast.8, bf16[2,1376,2048]{2,1,0:T(8,128)(2,1)} %bitcast.10, bf16[2,1376,2048]{2,1,0:T(8,128)(2,1)} %wd_hbm.3), custom_call_target="tpu_custom_call" | custom-call | flops 69256347648 | bytes 16908288 | tf_op jit(solution)/shard_map/mlp0/pallas_call | solution.py:594
  252.8 105.8 %attention1.1.r_hbm = f32[512,2048]{1,0:T(8,128)} custom-call(f32[512,2048]{1,0:T(8,128)} %mlp0.1.r_hbm, f32[2,2048]{1,0:T(2,128)} %gain_ref.6, f32[2,16,128]{2,1,0:T(8,128)} %constant.4.clone.far_ref, f32[2,256,128]{2,1,0:T(8,128)} %constant.5.clone.near_ref, bf16[2,4096,128]{2,1,0:T(8,128)(2,1)} %bitcast.16, bf16[2,8192,128]{2,1,0:T(8,128)(2,1)} %bitcast.13, ...), custom_call_target="tpu_custom_call" | custom-call | flops 8589934592 | bytes 4194304 | tf_op jit(solution)/shard_map/attention1/pallas_call | solution.py:421
  358.6 146.1 %mlp1.1 = bf16[512,2048]{1,0:T(8,128)(2,1)} custom-call(f32[512,2048]{1,0:T(8,128)} %attention1.1.r_hbm, f32[2,2048]{1,0:T(2,128)} %gain_ref.7, bf16[2,1376,2048]{2,1,0:T(8,128)(2,1)} %bitcast.9, bf16[2,1376,2048]{2,1,0:T(8,128)(2,1)} %bitcast.11, bf16[2,1376,2048]{2,1,0:T(8,128)(2,1)} %wd_hbm.3), custom_call_target="tpu_custom_call" | custom-call | flops 69256347648 | bytes 16908288 | tf_op jit(solution)/shard_map/mlp1/pallas_call | solution.py:594
  504.7 3.2 copy.13

commit v7 on v6

--- a/solution.py
+++ b/solution.py
@@ -238,15 +238,15 @@
     get_o = WeightGather(wo, cols, gather_sem[6:], *place)
     nd = 256
 
-    def deinterleave(raw, count, dst, first):
+    def deinterleave(raw, count, dst, first, order):
         @pl.loop(0, width // nd)
         def _(b):
             wide[pl.ds(0, count * nd), :] = raw[pl.ds(pl.multiple_of(b * count * nd, nd), count * nd), :].astype(F32)
             for h in range(count):
-                dst[pl.ds(pl.multiple_of(first + b * nd, nd), nd), h * head_dim:(h + 1) * head_dim] = wide[pl.ds(h, nd, stride=count), :].astype(BF16)
+                dst[pl.ds(pl.multiple_of(first + b * nd, nd), nd), h * head_dim:(h + 1) * head_dim] = wide[pl.ds(order[h], nd, stride=count), :].astype(BF16)
 
     load_q.wait()
-    deinterleave(wq, heads, w_q, t * width)
+    deinterleave(wq, heads, w_q, t * width, range(heads))
     pl.semaphore_wait(pltpu.get_barrier_semaphore(), n_tp)
     get_q.start()
 
@@ -265,12 +265,14 @@
     kv_cols = pl.ds(cols, 2 * head_dim)
     q_cols = pl.ds(0, cols)
     load_kv.wait()
-    deinterleave(wkv, 2 * n_kv, w_kv, 0)
-    for g in range(n_kv):
-        proj = jnp.dot(x[...], w_kv[:, g * head_dim:(g + 1) * head_dim], preferred_element_type=F32)
-        kv_out[g, :, 0:head_dim] = rotate(proj)
-        proj = jnp.dot(x[...], w_kv[:, (n_kv + g) * head_dim:(n_kv + g + 1) * head_dim], preferred_element_type=F32)
-        kv_out[g, :, head_dim:2 * head_dim] = proj.astype(BF16)
+    deinterleave(wkv, 2 * n_kv, w_kv, 0, [g + n_kv * k for g in range(n_kv) for k in range(2)])
+
+    @pl.loop(0, n_kv)
+    def _(g):
+        at = pl.ds(pl.multiple_of(g * 2 * head_dim, 2 * head_dim), 2 * head_dim)
+        proj = jnp.dot(x[...], w_kv[:, at], preferred_element_type=F32)
+        kv_out[g, :, 0:head_dim] = rotate(proj[:, 0:head_dim])
+        kv_out[g, :, head_dim:2 * head_dim] = proj[:, head_dim:2 * head_dim].astype(BF16)
 
     def kv_send(k, dev):
         return rcopy(kv_out.at[lax.div(dev * n_kv, n_tp)], qkv_ref.at[own, kv_cols], ks.at[k], kr.at[k], dev)
@@ -308,24 +310,13 @@
     def q_send(i):
         return rcopy(q_out.at[i], qkv_ref.at[own, q_cols], qs.at[i], qr.at[t], block_of(i))
 
-    def project_all(first, last):
-        @pl.loop(first, last)
-        def _(i):
-            project(i)
-
-            @pl.when(i >= 1)
-            def _():
-                q_send(i).start()
-
-    get_q.from_mate([12])
-    project_all(0, 2)
-    qkv_ref[own, q_cols] = q_out[0]
-    get_q.received(range(4))
-    for k in range(3):
-        pltpu.make_async_copy(kv_out.at[0], qkv_ref.at[pl.ds(pl.multiple_of(near[k] * rows, rows), rows), kv_cols], kr.at[k]).wait()
-        hand_on[k].start()
-    for copy in hand_on:
-        copy.wait_recv()
+    def take_kv():
+        for k in range(3):
+            at = pl.ds(pl.multiple_of(near[k] * rows, rows), rows)
+            pltpu.make_async_copy(kv_out.at[0], qkv_ref.at[at, kv_cols], kr.at[k]).wait()
+            hand_on[k].start()
+        for copy in hand_on:
+            copy.wait_recv()
 
     def ctx_send(i, dev):
         return rcopy(ctx_out.at[i], ctx.at[t], cs.at[i], cr.at[t], dev)
@@ -339,7 +330,7 @@
 
         @pl.when(n == 0)
         def _():
-            get_o.start()
+            get_q.from_mate([12])
 
         @pl.when(n == 1)
         def _():
@@ -349,15 +340,36 @@
         def _():
             get_q.from_z(range(4))
             get_q.from_mate((0, 1, 2, 3, 6, 7, 8, 9))
-            project_all(2, 4)
-            project_all(6, 8)
-            get_o.received(range(4))
 
         @pl.when(n == 4)
         def _():
             get_q.from_z((4, 5))
             get_q.from_mate((4, 5, 10, 11))
-            project_all(4, 6)
+
+        @pl.when((n == 0) | (n == 2) | (n == 4))
+        def _():
+            @pl.loop(0, jnp.where(n == 2, 4, 2))
+            def _(m):
+                which = n + m + jnp.where(m < 2, 0, 2)
+                project(which)
+
+                @pl.when(which >= 1)
+                def _():
+                    q_send(which).start()
+
+        @pl.when(n == 0)
+        def _():
+            qkv_ref[own, q_cols] = q_out[0]
+            get_q.received(range(4))
+            take_kv()
+            get_o.start()
+
+        @pl.when(n == 2)
+        def _():
+            get_o.received(range(4))
+
+        @pl.when(n == 4)
+        def _():
             get_o.received((4, 5))
 
         @pl.when(n == 7)
@@ -374,30 +386,30 @@
         def _():
             ctx_send(i, block).start()
 
+    ctx[t] = ctx_out[0]
+    res[...] = rin[...].astype(F32)
     get_o.from_z((4, 5))
     get_o.from_mate(range(13))
     nc = 512
-    chunks = [pl.ds(n * nc, nc) for n in range(width // nc)]
-    for at in chunks:
-        res[:, at] = rin[:, at].astype(F32) + jnp.dot(ctx_out[0], wo[own_o, at], preferred_element_type=F32)
-
-    def from_sender(n):
+
+    @pl.loop(0, n_tp)
+    def _(n):
         dev = block_of(n + jnp.where(n < 4, 0, jnp.where(n < 6, 2, -2)))
-        pltpu.make_async_copy(ctx_out.at[0], ctx.at[dev], cr.at[dev]).wait()
-        return dev, pl.ds(pl.multiple_of(dev * cols, cols), cols)
-
-    @pl.loop(1, n_tp - 1)
-    def _(n):
-        dev, rows_o = from_sender(n)
-        for at in chunks:
+
+        @pl.when(n >= 1)
+        def _():
+            pltpu.make_async_copy(ctx_out.at[0], ctx.at[dev], cr.at[dev]).wait()
+        rows_o = pl.ds(pl.multiple_of(dev * cols, cols), cols)
+
+        @pl.loop(0, width // nc)
+        def _(k):
+            at = pl.ds(pl.multiple_of(k * nc, nc), nc)
             res[:, at] = res[:, at] + jnp.dot(ctx[dev], wo[rows_o, at], preferred_element_type=F32)
 
-    dev, rows_o = from_sender(jnp.int32(n_tp - 1))
-    outs = []
-    for n, at in enumerate(chunks):
-        res[:, at] = res[:, at] + jnp.dot(ctx[dev], wo[rows_o, at], preferred_element_type=F32)
-        outs.append(pltpu.make_async_copy(res.at[:, at], out_hbm.at[:, at], es.at[n]))
-        outs[n].start()
+            @pl.when(n == n_tp - 1)
+            def _():
+                pltpu.make_async_copy(res.at[:, at], out_hbm.at[:, at], es.at[k]).start()
+
     get_q.finish()
     get_o.finish()
     for copy in sends + hand_on:
@@ -405,8 +417,9 @@
     for i in range(1, n_tp):
         q_send(jnp.int32(i)).wait_send()
         ctx_send(i, mate).wait_send()
-    for copy in outs:
-        copy.wait()
+    for k in range(width // nc):
+        at = pl.ds(k * nc, nc)
+        pltpu.make_async_copy(res.at[:, at], out_hbm.at[:, at], es.at[k]).wait()
 
 
 def attention(layer, resid, gain, far, near, w_q, w_kv, w_o, n_tp, bk=1024):
@@ -456,7 +469,6 @@
     half = rows // 2
     hid = act.shape[1]
     h0, h1 = pl.ds(0, half), pl.ds(half, half)
-    hs = (h0, h1)
     nb = 64
 
     load_r = pltpu.make_async_copy(r_hbm, acc, lsem.at[0])
@@ -473,11 +485,12 @@
         return rcopy(xbuf.at[w, 1], prec.at[w], ps.at[w], pr.at[w], mate)
 
     stage = (rcopy(xbuf.at[1, 1, h0], recv.at[0], ss.at[0], rr.at[0], dev_x),
-             rcopy(xbuf.at[1, 1, h1], recv.at[1], ss.at[1], rr.at[1], dev_y),
-             rcopy(xbuf.at[2, 1, h0], recv.at[2], ss.at[2], rr.at[2], dev_x),
-             rcopy(xbuf.at[2, 1, h1], recv.at[3], ss.at[3], rr.at[3], dev_y),
-             rcopy(xbuf.at[3, 1, h0], recv.at[4], ss.at[4], rr.at[4], dev_y),
-             rcopy(xbuf.at[3, 1, h1], recv.at[5], ss.at[5], rr.at[5], dev_x))
+             rcopy(xbuf.at[1, 1, h1], recv.at[1], ss.at[1], rr.at[1], dev_y))
+    quarter = half // 2
+    cuts = [(k, m, pl.ds(m * quarter, quarter), pl.ds(k * half + m * quarter, quarter)) for m in range(2) for k in range(2)]
+    to_first, to_second = (dev_x, dev_y), (dev_y, dev_x)
+    stage_two = [rcopy(xbuf.at[2, 1, to], recv.at[2 + k, at], ss.at[2 + k + 2 * m], rr.at[2 + k + 2 * m], to_first[k]) for k, m, at, to in cuts]
+    stage_three = [rcopy(xbuf.at[3, 1, to], recv.at[4 + k, at], ss.at[6 + k + 2 * m], rr.at[6 + k + 2 * m], to_second[k]) for k, m, at, to in cuts]
 
     for copy in loads:
         copy.wait()
@@ -544,42 +557,42 @@
 
         @pl.when(s == 5)
         def _():
-            stage[2].start()
-            stage[3].start()
-
-    def blocks_of(k):
+            for copy in stage_two:
+                copy.start()
+
+    def rows_from(first, count):
         def each(fn):
-            @pl.loop(0, half // nb)
+            @pl.loop(0, count // nb)
             def _(b):
-                fn(pl.ds(pl.multiple_of(b * nb, nb), nb), pl.ds(pl.multiple_of(k * half + b * nb, nb), nb))
+                fn(pl.multiple_of(b * nb, nb), pl.ds(pl.multiple_of(first + b * nb, nb), nb))
         return each
 
     for k in range(2):
         stage[k].wait_recv()
 
-        @blocks_of(k)
+        @rows_from(k * half, half)
         def _(at, to):
-            acc[to, :] = acc[to, :] + recv[k, at, :].astype(F32)
-    for k in range(2):
-        stage[2 + k].wait_recv()
-
-        @blocks_of(k)
+            acc[to, :] = acc[to, :] + recv[k, pl.ds(at, nb), :].astype(F32)
+    for copy, send, (k, m, _, _) in zip(stage_two, stage_three, cuts):
+        copy.wait_recv()
+
+        @rows_from(k * half + m * quarter, quarter)
         def _(at, to):
-            xbuf[3, 1, to, :] = (stash[to, :] + recv[2 + k, at, :].astype(F32)).astype(BF16)
-        stage[4 + k].start()
+            xbuf[3, 1, to, :] = (stash[to, :] + recv[2 + k, pl.ds(m * quarter + at, nb), :].astype(F32)).astype(BF16)
+        send.start()
     gather.finish()
     narrow = out_hbm.dtype == BF16
     final = xbuf.at[0, 0] if narrow else acc
     outs = []
-    for k in range(2):
-        stage[4 + k].wait_recv()
-
-        @blocks_of(k)
+    for copy, (k, m, _, out_at) in zip(stage_three, cuts):
+        copy.wait_recv()
+
+        @rows_from(k * half + m * quarter, quarter)
         def _(at, to):
-            final[to, :] = (acc[to, :] + recv[4 + k, at, :].astype(F32)).astype(final.dtype)
-        outs.append(pltpu.make_async_copy(final.at[hs[k]], out_hbm.at[hs[k]], lsem.at[k]))
-        outs[k].start()
-    for copy in stage:
+            final[to, :] = (acc[to, :] + recv[4 + k, pl.ds(m * quarter + at, nb), :].astype(F32)).astype(final.dtype)
+        outs.append(pltpu.make_async_copy(final.at[out_at], out_hbm.at[out_at], lsem.at[k + 2 * m]))
+        outs[-1].start()
+    for copy in list(stage) + stage_two + stage_three:
         copy.wait_send()
     for copy in outs:
         copy.wait()
@@ -607,7 +620,7 @@
             pltpu.VMEM((rows, width), F32),
             pltpu.VMEM((rows, hid), BF16),
             dma((4,)),
-        ] + gather_sems() + [dma((4,)), dma((4,)), dma((6,)), dma((6,))],
+        ] + gather_sems() + [dma((4,)), dma((4,)), dma((10,)), dma((10,))],
         compiler_params=pltpu.CompilerParams(collective_id=5 + layer, has_side_effects=True, vmem_limit_bytes=VMEM_MAX),
         cost_estimate=pl.CostEstimate(flops=6 * 8 * rows * width * hid, bytes_accessed=6 * width * hid, transcendentals=8 * rows * hid),
         name="mlp" + str(layer),

time: 517 us -> 507 us (0.981); the launches traced: 508 us -> 506 us
    pallas_call x2, Pallas kernels: 292 us -> 281 us  [mlp(): pl.pallas_call(functools.partial(mlp_kernel, layer), out_shape=jax.ShapeD...]
    pallas_call x2, Pallas kernels: 213 us -> 222 us  [attention(): pl.pallas_call(functools.partial(attn_kernel, layer, n_tp, n_kv, heads, h...]
where the time goes in v7:
time: 507 us; the launch traced here: 506 us
  Pallas kernels  503 us (99%)
    pallas_call x2, Pallas kernels, mlp(): pl.pallas_call(functools.partial(mlp_kernel, layer), out_shape=jax.ShapeD...  281 us
    pallas_call x2, Pallas kernels, attention(): pl.pallas_call(functools.partial(attn_kernel, layer, n_tp, n_kv, heads, h...  222 us

profile of v7, /device:TPU:0, one launch (start us, length us, event | category | flops | bytes accessed | tf_op | source)
XLA Modules:
  0.0 506.2 jit_solution(13191297762309440936)
XLA Ops:
  0.0 110.8 %attention0.1.r_hbm = f32[512,2048]{1,0:T(8,128)} custom-call(bf16[512,2048]{1,0:T(8,128)(2,1)} %bitcast.14, f32[2,2048]{1,0:T(2,128)} %gain_ref.6, f32[2,16,128]{2,1,0:T(8,128)} %constant.4.clone.far_ref, f32[2,256,128]{2,1,0:T(8,128)} %constant.5.clone.near_ref, bf16[2,4096,128]{2,1,0:T(8,128)(2,1)} %bitcast.15, bf16[2,8192,128]{2,1,0:T(8,128)(2,1)} %bitcast.12, ...), custom_call_target="tpu_custom_call" | custom-call | flops 8589934592 | bytes 4194304 | tf_op jit(solution)/shard_map/attention0/pallas_call | solution.py:434
  110.8 140.7 %mlp0.1.r_hbm = f32[512,2048]{1,0:T(8,128)} custom-call(f32[512,2048]{1,0:T(8,128)} %attention0.1.r_hbm, f32[2,2048]{1,0:T(2,128)} %gain_ref.7, bf16[2,1376,2048]{2,1,0:T(8,128)(2,1)} %bitcast.8, bf16[2,1376,2048]{2,1,0:T(8,128)(2,1)} %bitcast.10, bf16[2,1376,2048]{2,1,0:T(8,128)(2,1)} %wd_hbm.3), custom_call_target="tpu_custom_call" | custom-call | flops 69256347648 | bytes 16908288 | tf_op jit(solution)/shard_map/mlp0/pallas_call | solution.py:607
  251.6 111.6 %attention1.1.r_hbm = f32[512,2048]{1,0:T(8,128)} custom-call(f32[512,2048]{1,0:T(8,128)} %mlp0.1.r_hbm, f32[2,2048]{1,0:T(2,128)} %gain_ref.6, f32[2,16,128]{2,1,0:T(8,128)} %constant.4.clone.far_ref, f32[2,256,128]{2,1,0:T(8,128)} %constant.5.clone.near_ref, bf16[2,4096,128]{2,1,0:T(8,128)(2,1)} %bitcast.16, bf16[2,8192,128]{2,1,0:T(8,128)(2,1)} %bitcast.13, ...), custom_call_target="tpu_custom_call" | custom-call | flops 8589934592 | bytes 4194304 | tf_op jit(solution)/shard_map/attention1/pallas_call | solution.py:434
  363.2 139.8 %mlp1.1 = bf16[512,2048]{1,0:T(8,128)(2,1)} custom-call(f32[512,2048]{1,0:T(8,128)} %attention1.1.r_hbm, f32[2,2048]{1,0:T(2,128)} %gain_ref.7, bf16[2,1376,2048]{2,1,0:T(8,128)(2,1)} %bitcast.9, bf16[2,1376,2048]{2,1,0:T(8,128)(2,1)} %bitcast.11, bf16[2,1376,2048]{2,1,0:T(8,128)(2,1)} %wd_hbm.3), custom_call_target="tpu_custom_call" | custom-call | flops 69256347648 | bytes 16908288 | tf_op jit(solution)/shard_map/mlp1/pallas_call | solution.py:607
  503.1 3.2 copy.13

commit v8 on v7

--- a/solution.py
+++ b/solution.py
@@ -179,7 +179,7 @@
 
 def attend(qkv_ref, block, bq, bk, heads, head_dim):
     scale = math.log2(math.e) / math.sqrt(head_dim)
-    mask = lax.broadcasted_iota(jnp.int32, (bq, bq), 0) >= lax.broadcasted_iota(jnp.int32, (bq, bq), 1)
+    mask = lax.broadcasted_iota(jnp.int32, (bq, bq), 0) <= lax.broadcasted_iota(jnp.int32, (bq, bq), 1)
     q_at = pl.ds(pl.multiple_of(block * bq, bq), bq)
     qs = [qkv_ref[q_at, h * head_dim:(h + 1) * head_dim] for h in range(heads)]
 
@@ -190,23 +190,23 @@
         out = []
         for h in range(heads):
             m, l, acc = carry[h]
-            s = lax.dot_general(qs[h], k_blk, (((1,), (1,)), ((), ())), preferred_element_type=F32)
+            s = lax.dot_general(k_blk, qs[h], (((1,), (1,)), ((), ())), preferred_element_type=F32)
             if masked:
                 s = jnp.where(mask, s, -jnp.inf)
-            m_new = jnp.maximum(m, jnp.max(s, axis=-1, keepdims=True))
+            m_new = jnp.maximum(m, jnp.max(s, axis=0, keepdims=True))
             p = jnp.exp2((s - m_new) * scale)
             alpha = jnp.exp2((m - m_new) * scale)
-            l = l * alpha + jnp.sum(p, axis=-1, keepdims=True)
-            acc = acc * alpha + jnp.dot(p.astype(BF16), v_blk, preferred_element_type=F32)
+            l = l * alpha + jnp.sum(p, axis=0, keepdims=True)
+            acc = acc * alpha + lax.dot_general(v_blk, p.astype(BF16), (((0,), (0,)), ((), ())), preferred_element_type=F32)
             out.append((m_new, l, acc))
         return tuple(out)
 
-    carry = tuple((jnp.full((bq, 1), -jnp.inf, F32), jnp.zeros((bq, 1), F32), jnp.zeros((bq, head_dim), F32)) for _ in range(heads))
+    carry = tuple((jnp.full((1, bq), -jnp.inf, F32), jnp.zeros((1, bq), F32), jnp.zeros((head_dim, bq), F32)) for _ in range(heads))
     carry = step(block * bq, bq, carry, True)
     full = lax.div(block * bq, bk)
     carry = lax.fori_loop(0, full, lambda j, cur: step(j * bk, bk, cur, False), carry)
     carry = lax.fori_loop(full * (bk // bq), block, lambda j, cur: step(j * bq, bq, cur, False), carry)
-    return [(acc / l).astype(BF16) for _, l, acc in carry]
+    return [(acc / l).T.astype(BF16) for _, l, acc in carry]
 
 
 def attn_kernel(layer, n_tp, n_kv, heads, head_dim, bk, r_hbm, gain_ref, far_ref, near_ref, wq_hbm, wkv_hbm, wo_hbm, out_hbm,
@@ -361,8 +361,8 @@
         def _():
             qkv_ref[own, q_cols] = q_out[0]
             get_q.received(range(4))
+            get_o.start()
             take_kv()
-            get_o.start()
 
         @pl.when(n == 2)
         def _():

time: 507 us -> 505 us (level)
  no operation moved by 1% of the time
where the time goes in v8:
time: 505 us
  Pallas kernels  502 us (99%)
    pallas_call x2, Pallas kernels, mlp(): pl.pallas_call(functools.partial(mlp_kernel, layer), out_shape=jax.ShapeD...  281 us
    pallas_call x2, Pallas kernels, attention(): pl.pallas_call(functools.partial(attn_kernel, layer, n_tp, n_kv, heads, h...  221 us

profile of v8, /device:TPU:0, one launch (start us, length us, event | category | flops | bytes accessed | tf_op | source)
XLA Modules:
  0.0 504.7 jit_solution(9535671926135946147)
XLA Ops:
  0.0 110.1 %attention0.1.r_hbm = f32[512,2048]{1,0:T(8,128)} custom-call(bf16[512,2048]{1,0:T(8,128)(2,1)} %bitcast.14, f32[2,2048]{1,0:T(2,128)} %gain_ref.6, f32[2,16,128]{2,1,0:T(8,128)} %constant.4.clone.far_ref, f32[2,256,128]{2,1,0:T(8,128)} %constant.5.clone.near_ref, bf16[2,4096,128]{2,1,0:T(8,128)(2,1)} %bitcast.15, bf16[2,8192,128]{2,1,0:T(8,128)(2,1)} %bitcast.12, ...), custom_call_target="tpu_custom_call" | custom-call | flops 8589934592 | bytes 4194304 | tf_op jit(solution)/shard_map/attention0/pallas_call | solution.py:434
  110.1 140.7 %mlp0.1.r_hbm = f32[512,2048]{1,0:T(8,128)} custom-call(f32[512,2048]{1,0:T(8,128)} %attention0.1.r_hbm, f32[2,2048]{1,0:T(2,128)} %gain_ref.7, bf16[2,1376,2048]{2,1,0:T(8,128)(2,1)} %bitcast.8, bf16[2,1376,2048]{2,1,0:T(8,128)(2,1)} %bitcast.10, bf16[2,1376,2048]{2,1,0:T(8,128)(2,1)} %wd_hbm.3), custom_call_target="tpu_custom_call" | custom-call | flops 69256347648 | bytes 16908288 | tf_op jit(solution)/shard_map/mlp0/pallas_call | solution.py:607
  250.8 110.9 %attention1.1.r_hbm = f32[512,2048]{1,0:T(8,128)} custom-call(f32[512,2048]{1,0:T(8,128)} %mlp0.1.r_hbm, f32[2,2048]{1,0:T(2,128)} %gain_ref.6, f32[2,16,128]{2,1,0:T(8,128)} %constant.4.clone.far_ref, f32[2,256,128]{2,1,0:T(8,128)} %constant.5.clone.near_ref, bf16[2,4096,128]{2,1,0:T(8,128)(2,1)} %bitcast.16, bf16[2,8192,128]{2,1,0:T(8,128)(2,1)} %bitcast.13, ...), custom_call_target="tpu_custom_call" | custom-call | flops 8589934592 | bytes 4194304 | tf_op jit(solution)/shard_map/attention1/pallas_call | solution.py:434
  361.7 139.8 %mlp1.1 = bf16[512,2048]{1,0:T(8,128)(2,1)} custom-call(f32[512,2048]{1,0:T(8,128)} %attention1.1.r_hbm, f32[2,2048]{1,0:T(2,128)} %gain_ref.7, bf16[2,1376,2048]{2,1,0:T(8,128)(2,1)} %bitcast.9, bf16[2,1376,2048]{2,1,0:T(8,128)(2,1)} %bitcast.11, bf16[2,1376,2048]{2,1,0:T(8,128)(2,1)} %wd_hbm.3), custom_call_target="tpu_custom_call" | custom-call | flops 69256347648 | bytes 16908288 | tf_op jit(solution)/shard_map/mlp1/pallas_call | solution.py:607
  501.6 3.2 copy.13
